TPU v7x, 256 devices: a whole 4x4x8 slice. The times are simulated.
256 devices in a mesh: rep: 64 (over z, x, core), rows: 4 (over y).
Axes of the slice: x: 4, y: 4, z: 8, core: 2. Of those that a mesh axis runs over, the one named last changes fastest.
Arguments:
- pooled_grad: bfloat16 [262144, 2, 128], P(('rep', 'rows')), may hold values from -6 to 6
- slot_source: int32 [256, 4, 1024], P(('rep', 'rows')), may hold values from 0 to 2047, as said below
- slot_target: int32 [256, 4, 1024], P(('rep', 'rows')), may hold values from 0 to 8191, as said below
- slot_count: int32 [256, 4], P(('rep', 'rows')), may hold values from 128 to 1024, as said below
- table_rows: float32 [2, 16384, 128], P(None, 'rows'), may hold values from -1.5 to 1.5
- accum: float32 [2, 16384], P(None, 'rows'), may hold values from 0.01 to 1
Outputs:
- new_rows: float32 [2, 16384, 128], P(None, 'rows')
- new_accum: float32 [2, 16384], P(None, 'rows')
Inputs may be any that keep to these rules, and one draw needn't show every extreme that they name: `slot_source`: entry q encodes a local sample q // 2 and a table q % 2; the table agrees with that of slot_target at the same slot. `slot_target`: entry t encodes a table t // 4096 and a row t % 4096 of the owner's shard; rows repeat across slots and senders. `slot_count`: slots at or past the count carry no lookup; every sender fills all slots to some owner.
All inputs are finite; a program needn't handle non-finite values.
Results may differ from a plain program's by a relative error of at most 0.0003.
Values may be sent and summed in bfloat16 or wider, within the bound.
No kernel may reach another device: no remote copies, remote signals or barrier semaphores. Data moves between devices by JAX's collectives and lax.ppermute only.
A program may use at most 64 MiB of HBM per device.

v0:
```python
import functools

import jax
import jax.numpy as jnp
from jax import lax
from jax.experimental import pallas as pl
from jax.experimental.pallas import tpu as pltpu
from jax.sharding import Mesh
from jax.sharding import PartitionSpec as P


AXES = ("far", "pair", "ring", "core", "rows")
SQUARE = ("pair", "ring")

LEARN_RATE = 0.1
EPSILON = 1e-06
LANES = 128
SPARE = 8
CODED = LANES + SPARE
STEPS = 64.0
TOP = 32700.0
TINY = 1e-30
ROUNDER = 12582912.0

VM = pl.BlockSpec(memory_space=pltpu.VMEM)
SM = pl.BlockSpec(memory_space=pltpu.SMEM)
HB = pl.BlockSpec(memory_space=pltpu.HBM)


def room(mib):
    return pltpu.CompilerParams(vmem_limit_bytes=mib * 2**20)


def cost(flops):
    return pl.CostEstimate(flops=flops, bytes_accessed=10**6, transcendentals=0)


def loop(count, body):
    def step(i, carry):
        body(i)
        return carry

    lax.fori_loop(0, count, step, 0)


def pieces(count, size, body):
    loop(count // size, lambda i: body(pl.ds(pl.multiple_of(i * size, size), size)))


def pick(owner, keys, held, wide, out, stage):
    chunks = keys.shape[0]
    cap = chunks * LANES

    def body(chunk):
        first = chunk * LANES
        for u in range(LANES):
            key = keys[chunk, owner, u]
            stage[pl.ds(first + u, 1), :] = wide[pl.ds(key, 1), :]

    loop(chunks, body)

    def narrow(rows):
        out[rows, :] = stage[rows, :].astype(jnp.bfloat16)

    pieces(cap, LANES, narrow)
    target = held[owner]
    upper = target >> 7
    out[cap : cap + SPARE, :] = upper.astype(jnp.float32).astype(jnp.bfloat16)
    lower = target - upper * LANES
    out[cap + SPARE : cap + 2 * SPARE, :] = lower.astype(jnp.float32).astype(jnp.bfloat16)


def first_pick_kernel(
    hop, unused, place, count, keys, keys_in, targets, flat, out, wide, held, kept, stage
):
    chunks, owners, _ = targets.shape
    slots = lax.broadcasted_iota(jnp.int32, (chunks, LANES), 0) * LANES
    slots = slots + lax.broadcasted_iota(jnp.int32, (chunks, LANES), 1)
    kept[...] = keys_in[...]
    for owner in range(owners):
        held[owner] = jnp.where(slots < count[0, owner], targets[:, owner, :], unused)

    def widen(rows):
        wide[rows, :] = flat[rows, :].astype(jnp.float32)

    pieces(flat.shape[0], LANES, widen)
    pick(lax.rem(place[0] + hop, owners), keys, held, wide, out, stage)


def first_pick(hop, unused, place, count, keys, targets, flat):
    chunks, owners, _ = keys.shape
    cap = chunks * LANES
    width = flat.shape[1]
    return pl.pallas_call(
        functools.partial(first_pick_kernel, hop, unused),
        out_shape=(
            jax.ShapeDtypeStruct((cap + 2 * SPARE, width), jnp.bfloat16),
            jax.ShapeDtypeStruct(flat.shape, jnp.float32),
            jax.ShapeDtypeStruct((owners, chunks, LANES), jnp.int32),
            jax.ShapeDtypeStruct(keys.shape, jnp.int32),
        ),
        in_specs=[SM, SM, SM, VM, VM, VM],
        out_specs=(VM, VM, VM, VM),
        scratch_shapes=[pltpu.VMEM((cap, width), jnp.float32)],
        compiler_params=room(6),
        cost_estimate=cost(10**7),
        name="first_pick",
    )(place, count, keys, keys, targets, flat)


def pick_kernel(hops, place, keys, held, wide, *refs):
    outs, stages = refs[: len(hops)], refs[len(hops) :]
    owners = held.shape[0]
    for hop, out, stage in zip(hops, outs, stages):
        pick(lax.rem(place[0] + hop, owners), keys, held, wide, out, stage)


def pick_rows(hops, place, keys, held, wide):
    cap = keys.shape[0] * LANES
    width = wide.shape[1]
    shape = jax.ShapeDtypeStruct((cap + 2 * SPARE, width), jnp.bfloat16)
    return pl.pallas_call(
        functools.partial(pick_kernel, hops),
        out_shape=(shape,) * len(hops),
        in_specs=[SM, SM, VM, VM],
        out_specs=(VM,) * len(hops),
        scratch_shapes=[pltpu.VMEM((cap, width), jnp.float32)] * len(hops),
        compiler_params=room(6),
        cost_estimate=cost(10**7 * len(hops)),
        name="pick",
    )(place, keys, held, wide)


def add_rows(pairs, sums, wides, keys, rows, chunk):
    first = chunk * LANES
    for u in range(0, LANES, 2 * pairs):
        for k, row in enumerate(rows):
            for p in range(pairs):
                at, total = u + 2 * p, sums[k * pairs + p]
                one, two = keys[row + chunk, at], keys[row + chunk, at + 1]
                here, next_ = pl.ds(one, 1), pl.ds(two, 1)
                again = jnp.where(one == two, 1.0, 0.0)
                lead = wides[k][pl.ds(first + at, 1), :]
                tail = wides[k][pl.ds(first + at + 1, 1), :] + lead * again
                before, after = total[here, :], total[next_, :]
                total[here, :] = before + lead
                total[next_, :] = after + tail


def prepare(grads, cap, sums, wides, found, keys, sem):
    chunks = cap // LANES
    for k, grad in enumerate(grads):
        upper = grad[cap : cap + SPARE, :].astype(jnp.float32)
        lower = grad[cap + SPARE : cap + 2 * SPARE, :].astype(jnp.float32)
        found[k * chunks : (k + 1) * chunks, :] = (upper * LANES + lower).astype(jnp.int32)
    copy = pltpu.make_async_copy(found, keys, sem)
    copy.start()

    def widen(rows):
        for wide, grad in zip(wides, grads):
            wide[rows, :] = grad[rows, :].astype(jnp.float32)

    def clear(rows):
        for total in sums:
            total[rows, :] = jnp.zeros((64, LANES), jnp.float32)

    pieces(cap, 64, widen)
    pieces(sums[0].shape[0] // 64 * 64, 64, clear)
    copy.wait()


def own_kernel(parts, place, keys, held, wide, out, *refs):
    sums, (found, sem) = refs[:parts], refs[parts:]
    owner = place[0]
    copy = pltpu.make_async_copy(held.at[owner], found, sem)
    copy.start()

    def clear(rows):
        for total in sums:
            total[rows, :] = jnp.zeros((64, LANES), jnp.float32)

    pieces(sums[0].shape[0] // 64 * 64, 64, clear)
    copy.wait()

    def body(chunk):
        for u in range(0, LANES, 2 * parts):
            for p, total in enumerate(sums):
                at = u + 2 * p
                one, two = found[chunk, at], found[chunk, at + 1]
                lead = wide[pl.ds(keys[chunk, owner, at], 1), :]
                tail = wide[pl.ds(keys[chunk, owner, at + 1], 1), :]
                tail = tail + lead * jnp.where(one == two, 1.0, 0.0)
                here, next_ = pl.ds(one, 1), pl.ds(two, 1)
                before, after = total[here, :], total[next_, :]
                total[here, :] = before + lead
                total[next_, :] = after + tail

    loop(keys.shape[0], body)

    def add_up(rows):
        total = sums[0][rows, :]
        for part in sums[1:]:
            total = total + part[rows, :]
        out[rows, :] = total

    pieces(out.shape[0], 64, add_up)


def scatter_kernel(cap, senders, place, begun, *refs):
    grads, outs, refs = refs[:senders], refs[senders : senders + 2], refs[senders + 2 :]
    sums, wides = refs[:senders], refs[senders : 2 * senders]
    found, keys, sem = refs[2 * senders :]
    chunks = cap // LANES
    prepare(grads, cap, sums, wides, found, keys, sem)
    rows = [k * chunks for k in range(senders)]
    loop(chunks, lambda chunk: add_rows(1, sums, wides, keys, rows, chunk))
    half = outs[0].shape[0]
    for out, index in ((outs[1], 1 - place[1]), (outs[0], place[1])):

        def add_up(i):
            there = pl.ds(pl.multiple_of(index * half + i * 64, 64), 64)
            total = begun[there, :]
            for part in sums:
                total = total + part[there, :]
            out[pl.ds(pl.multiple_of(i * 64, 64), 64), :] = total

        loop(half // 64, add_up)


def tables_of(rows, width, cap, senders, pairs):
    chunks = cap // LANES
    return (
        [pltpu.VMEM((rows + SPARE, width), jnp.float32)] * (senders * pairs)
        + [pltpu.VMEM((cap, width), jnp.float32)] * senders
        + [
            pltpu.VMEM((senders * chunks, LANES), jnp.int32),
            pltpu.SMEM((senders * chunks, LANES), jnp.int32),
            pltpu.SemaphoreType.DMA,
        ]
    )


def own_rows(place, keys, held, wide, rows):
    width = wide.shape[1]
    parts = 2
    return pl.pallas_call(
        functools.partial(own_kernel, parts),
        out_shape=jax.ShapeDtypeStruct((rows, width), jnp.float32),
        in_specs=[SM, SM, VM, VM],
        out_specs=VM,
        scratch_shapes=[pltpu.VMEM((rows + SPARE, width), jnp.float32)] * parts
        + [pltpu.SMEM(held.shape[1:], jnp.int32), pltpu.SemaphoreType.DMA],
        compiler_params=room(16),
        cost_estimate=cost(10**7),
        name="own_rows",
    )(place, keys, held, wide)


def scatter_add(place, begun, grads):
    senders = len(grads)
    cap, width = grads[0].shape[0] - 2 * SPARE, grads[0].shape[1]
    rows = begun.shape[0]
    shape = jax.ShapeDtypeStruct((rows // 2, width), jnp.float32)
    return pl.pallas_call(
        functools.partial(scatter_kernel, cap, senders),
        out_shape=(shape, shape),
        in_specs=[SM, VM] + [VM] * senders,
        out_specs=(VM, VM),
        scratch_shapes=tables_of(rows, width, cap, senders, 1),
        compiler_params=room(24),
        cost_estimate=cost(10**8),
        name="scatter",
    )(place, begun, *grads)


def diagonal():
    lane = lax.broadcasted_iota(jnp.int32, (LANES, LANES), 1)
    return lax.broadcasted_iota(jnp.int32, (LANES, LANES), 0) == lane


def to_row(column, diag):
    return jnp.sum(jnp.where(diag, column, 0.0), axis=0, keepdims=True)


def to_column(row, diag):
    return jnp.sum(jnp.where(diag, row, 0.0), axis=1, keepdims=True)


def powers_of(peaks):
    return jnp.ceil(STEPS * jnp.log2(jnp.maximum(peaks, TINY) / TOP))


def short(x):
    return x.astype(jnp.int32).astype(jnp.int16)


def wide_of(x):
    return x.astype(jnp.int32).astype(jnp.float32)


def rounded(x):
    return short((x + ROUNDER) - ROUNDER)


def encode_blocks(block, put, count, peaks, shrinks, diag):
    for k in range(count):
        peak = jnp.max(jnp.abs(block(k)), axis=1, keepdims=True)
        peaks[k : k + 1, :] = to_row(peak, diag)
    powers = powers_of(peaks[...])
    peaks[...] = powers
    shrinks[...] = jnp.exp2(powers * (-1.0 / STEPS))
    for k in range(count):
        tail = short(jnp.broadcast_to(peaks[k : k + 1, :], (SPARE, LANES)))
        put(k, rounded(block(k) * to_column(shrinks[k : k + 1, :], diag)), tail)


def decode(part, diag):
    scale = to_column(jnp.exp2(wide_of(part[LANES:CODED]) * (1.0 / STEPS))[0:1], diag)
    return wide_of(part[0:LANES]) * scale


def encode_kernel(mine, got, out, peaks, shrinks):
    diag = diagonal()
    groups, blocks = out.shape[:2]
    size = blocks * LANES

    def body(group, carry):
        def block(k):
            rows = pl.ds(pl.multiple_of(group * size + k * LANES, LANES), LANES)
            return mine[rows, :] + got[rows, :]

        def put(k, code, tail):
            out[group, k, 0:LANES, :] = code
            out[group, k, LANES:CODED, :] = tail

        encode_blocks(block, put, blocks, peaks, shrinks, diag)
        return carry

    lax.fori_loop(0, groups, body, 0)


def encode_sum(mine, got, groups):
    blocks = mine.shape[0] // (groups * LANES)
    return pl.pallas_call(
        encode_kernel,
        out_shape=jax.ShapeDtypeStruct((groups, blocks, CODED, LANES), jnp.int16),
        in_specs=[VM, VM],
        out_specs=VM,
        scratch_shapes=[pltpu.VMEM((blocks, LANES), jnp.float32)] * 2,
        compiler_params=room(8),
        cost_estimate=cost(10**7),
        name="encode",
    )(mine, got)


def first_sum_kernel(parts, out, totals, peaks, shrinks):
    diag = diagonal()
    groups, blocks = parts.shape[:2]

    def body(k, carry):
        total = decode(parts[0, k], diag)
        for j in range(1, groups):
            total = total + decode(parts[j, k], diag)
        totals[k] = total
        return carry

    lax.fori_loop(0, blocks, body, 0)

    def put(k, code, tail):
        out[k, 0:LANES, :] = code
        out[k, LANES:CODED, :] = tail

    encode_blocks(lambda k: totals[k], put, blocks, peaks, shrinks, diag)


def first_sum(parts):
    blocks = parts.shape[1]
    return pl.pallas_call(
        first_sum_kernel,
        out_shape=jax.ShapeDtypeStruct(parts.shape[1:], jnp.int16),
        in_specs=[VM],
        out_specs=VM,
        scratch_shapes=[pltpu.VMEM((blocks, LANES, LANES), jnp.float32)]
        + [pltpu.VMEM((blocks, LANES), jnp.float32)] * 2,
        compiler_params=room(6),
        cost_estimate=cost(10**7),
        name="first_sum",
    )(parts)


def last_sum_kernel(parts, out):
    diag = diagonal()
    total = decode(parts[0], diag)
    for j in range(1, parts.shape[0]):
        total = total + decode(parts[j], diag)
    powers = powers_of(to_row(jnp.max(jnp.abs(total), axis=1, keepdims=True), diag))
    code = rounded(total * to_column(jnp.exp2(powers * (-1.0 / STEPS)), diag))
    tail = short(jnp.broadcast_to(powers, (SPARE, LANES)))
    for j in range(out.shape[0]):
        out[j, 0:LANES, :] = code
        out[j, LANES:CODED, :] = tail


def last_sum(parts):
    return pl.pallas_call(
        last_sum_kernel,
        out_shape=jax.ShapeDtypeStruct(parts.shape, jnp.int16),
        in_specs=[VM],
        out_specs=VM,
        compiler_params=room(4),
        cost_estimate=cost(10**6),
        name="last_sum",
    )(parts)


def update_kernel(count, groups, core, *refs):
    mine, got = refs[:count], refs[count : 2 * count]
    rows, state = refs[2 * count : 2 * count + 2]
    new_rows, new_state, held, sums, scales = refs[-5:]
    step = pl.program_id(0)
    tables, blocks = held.shape[:2]
    size = blocks * LANES
    for d in range(count):

        @pl.when(step == d)
        def _():
            held[core[0]] = mine[d][...]
            held[1 - core[0]] = got[d][...]

    diag = diagonal()
    start = groups[step] * size
    every = [(table, k) for table in range(tables) for k in range(blocks)]
    for at, (table, k) in enumerate(every):
        code = wide_of(held[table, k, 0:LANES, :])
        sums[at : at + 1, :] = to_row(jnp.sum(code * code, axis=1, keepdims=True), diag)
        scales[at : at + 1, :] = wide_of(held[table, k, LANES:CODED, :])[0:1]
    scale = jnp.exp2(scales[...] * (1.0 / STEPS))
    gain = sums[...] * (scale * scale) * (1.0 / LANES)
    for at, (table, k) in enumerate(every):
        lanes = slice(k * LANES, (k + 1) * LANES)
        there = pl.ds(pl.multiple_of(start + k * LANES, LANES), LANES)
        updated = state[table : table + 1, there] + gain[at : at + 1, :]
        new_state[table : table + 1, lanes] = updated
        sums[at : at + 1, :] = updated
    scales[...] = LEARN_RATE * scale / (jnp.sqrt(sums[...]) + EPSILON)
    for at, (table, k) in enumerate(every):
        there = slice(k * LANES, (k + 1) * LANES)
        move = wide_of(held[table, k, 0:LANES, :]) * to_column(scales[at : at + 1, :], diag)
        new_rows[table, there, :] = rows[step, table, there, :] - move


def update(groups, core, mine, got, rows, state, earlier):
    count, tables, size, width = rows.shape
    blocks = mine[0].shape[0]
    row_spec = pl.BlockSpec((tables, size, width), lambda i, g, c: (0, g[i], 0))
    state_spec = pl.BlockSpec((tables, size), lambda i, g, c: (0, g[i]))
    first = 2 + 2 * count + 2
    return pl.pallas_call(
        functools.partial(update_kernel, count),
        grid_spec=pltpu.PrefetchScalarGridSpec(
            num_scalar_prefetch=2,
            grid=(count,),
            in_specs=[VM] * (2 * count) + [VM, VM] + [HB] * len(earlier),
            out_specs=(row_spec, state_spec),
            scratch_shapes=[
                pltpu.VMEM((tables, *mine[0].shape), jnp.int16),
            ]
            + [pltpu.VMEM((tables * blocks, LANES), jnp.float32)] * 2,
        ),
        out_shape=(
            jax.ShapeDtypeStruct((tables, state.shape[1], width), jnp.float32),
            jax.ShapeDtypeStruct(state.shape, jnp.float32),
        ),
        input_output_aliases={first: 0, first + 1: 1} if earlier else {},
        compiler_params=room(12),
        cost_estimate=cost(10**7),
        name="update",
    )(groups, core, *mine, *got, rows, state, *earlier)


def fetch_kernel(groups, rows, after, *refs):
    outs, sems = refs[:-1], refs[-1]
    count, _, size, _ = outs[0].shape
    copies = []
    for i, out in enumerate(outs):
        for d in range(count):
            at = i * count + d
            there = pl.ds(pl.multiple_of(groups[at] * size, size), size)
            copies.append(pltpu.make_async_copy(rows.at[:, there, :], out.at[d], sems.at[at]))
    for copy in copies:
        copy.start()
    for copy in copies:
        copy.wait()


def fetch(groups, rows, after):
    tables, rows_dev, width = rows.shape
    count = groups.shape[0]
    shape = jax.ShapeDtypeStruct((count // 2, tables, rows_dev // count, width), rows.dtype)
    return pl.pallas_call(
        fetch_kernel,
        out_shape=(shape, shape),
        in_specs=[SM, HB, HB],
        out_specs=(VM, VM),
        scratch_shapes=[pltpu.SemaphoreType.DMA((count,))],
        compiler_params=room(5),
        cost_estimate=cost(3 * 10**7),
        name="fetch",
    )(groups, rows, after)


def shift(x, axis, by):
    count = lax.axis_size(axis)
    return lax.ppermute(x, axis, [(i, (i + by) % count) for i in range(count)])


def square_shift(x, pair_by, ring_by):
    pairs, rings = lax.axis_size("pair"), lax.axis_size("ring")
    links = [
        (p * rings + r, (p + pair_by) % pairs * rings + (r + ring_by) % rings)
        for p in range(pairs)
        for r in range(rings)
    ]
    return lax.ppermute(x, SQUARE, links)


def lane_view(slots):
    owners, cap = slots.shape[1:]
    return slots.reshape(owners, cap // LANES, LANES).transpose(1, 0, 2)


def shards(pooled_grad, slot_source, slot_target, slot_count, table_rows, accum):
    feature = pooled_grad.shape[2]
    tables, rows_dev, _ = table_rows.shape
    pairs, rings = lax.axis_size("pair"), lax.axis_size("ring")
    row, core, pair, ring = (lax.axis_index(a) for a in ("rows", "core", "pair", "ring"))
    hops = [(0, 0), (0, 1), (0, 3), (1, 0), (1, 1), (1, 3), (0, 2), (1, 2)]
    behind = [(pair + p) % pairs * rings + (ring + rings - r) % rings for p, r in hops]
    facts = jnp.stack([row, core, *behind]).astype(jnp.int32)
    place, core, behind = facts[0:2], facts[1:2], facts[2:]
    flat_grad = pooled_grad.reshape(-1, feature)
    keys, targets = lane_view(slot_source), lane_view(slot_target)

    rows = tables * rows_dev
    first, wide, held, keys = first_pick(2, rows, place, slot_count, keys, targets, flat_grad)
    picked = {2: first}
    picked.update(zip((1, 3), pick_rows((1, 3), place, keys, held, wide)))
    grads = []
    for hop, block in picked.items():
        grads.append(shift(block, "rows", hop))
    begun = own_rows(place, keys, held, wide, rows)
    mine, other = scatter_add(place, begun, grads)
    order = ((7, 6, 5, 0), (4, 3, 2, 1))
    behind = jnp.stack([behind[d] for part in order for d in part])
    fetched = fetch(behind, table_rows, begun)
    got = shift(other, "core", 1)
    coded = encode_sum(mine, got, pairs * rings)
    parts = lax.all_to_all(coded, SQUARE, 0, 0, tiled=True)
    parts = lax.all_to_all(first_sum(parts), "far", 0, 0, tiled=True)
    bundle = lax.all_to_all(last_sum(parts), "far", 0, 0, tiled=True)
    whole = [None] * len(hops)
    for d in reversed(range(len(hops))):
        whole[d] = square_shift(bundle, *hops[d]) if d else bundle
    swapped = [shift(w, "core", 1) for w in whole]
    result = ()
    for i in range(2):
        result = update(
            behind[4 * i : 4 * i + 4],
            core,
            [whole[d] for d in order[i]],
            [swapped[d] for d in order[i]],
            fetched[i],
            accum,
            result,
        )
    return result


def solution(mesh):
    split = Mesh(mesh.devices.reshape(4, 2, 4, 2, mesh.shape["rows"]), AXES)
    placed = (
        P(AXES, None, None),
        P(AXES, None, None),
        P(AXES, None, None),
        P(AXES, None),
        P(None, "rows", None),
        P(None, "rows"),
    )

    return jax.shard_map(
        shards,
        mesh=split,
        in_specs=placed,
        out_specs=(P(None, "rows", None), P(None, "rows")),
        check_vma=False,
    )
```

profile of v0, /device:TPU:1, one launch (start us, length us, event | category | flops | bytes accessed | tf_op | source)
XLA Modules:
  0.0 122.8 jit_solution(8033803792244979001)
XLA Ops:
  0.6 0.1 pad_add_fusion.1.place
  0.7 1.0 copy-done.3
  1.8 0.7 copy-done.5
  2.5 0.7 copy-done.6
  3.2 0.7 copy-done.7
  3.8 1.9 %first_pick.1 = (bf16[1040,128]{1,0:T(8,128)(2,1)S(1)}, f32[2048,128]{1,0:T(8,128)S(1)}, s32[4,8,128]{2,1,0:T(8,128)S(1)}, s32[8,4,128]{2,1,0:T(4,128)S(1)}) custom-call(s32[2]{0:T(128)S(1)} %pad_add_fusion.1.place, s32[1,4]{1,0:T(1,128)S(1)} %copy-done.7, s32[8,4,128]{2,1,0:T(4,128)S(1)} %bitcast.18, s32[8,4,128]{2,1,0:T(4,128)S(1)} %bitcast.19, ...), custom_call_target="tpu_custom_call" | custom-call | flops 10000000 | bytes 1000000 | tf_op jit(solution)/shard_map/first_pick/pallas_call | solution.py:94
  5.7 2.6 %pick.1 = (bf16[1040,128]{1,0:T(8,128)(2,1)S(1)}, bf16[1040,128]{1,0:T(8,128)(2,1)S(1)}) custom-call(s32[2]{0:T(128)S(1)} %pad_add_fusion.1.place, s32[8,4,128]{2,1,0:T(4,128)S(1)} %get-tuple-element.14.keys, s32[4,8,128]{2,1,0:T(8,128)S(1)} %get-tuple-element.15.held, f32[2048,128]{1,0:T(8,128)S(1)} %get-tuple-element.16.wide), custom_call_target="tpu_custom_call" | custom-call | flops 20000000 | bytes 1000000 | tf_op jit(solution)/shard_map/pick/pallas_call | solution.py:122
  8.4 2.2 %collective-permute-start.1 = (bf16[1040,128]{1,0:T(8,128)(2,1)S(1)}, bf16[1040,128]{1,0:T(8,128)(2,1)S(1)}, u32[]{:S(2)}, u32[]{:S(2)}) collective-permute-start(bf16[1040,128]{1,0:T(8,128)(2,1)S(1)} %get-tuple-element.18), channel_id=1, source_target_pairs={{0,1},{1,2},{2,3},{3,0},{4,5},{5,6},{6,7},{7,4},{8,9},{9,10},{10,1... | collective-permute-start | bytes 798728 | tf_op jit(solution)/shard_map/ppermute | solution.py:514
  10.6 1.5 %collective-permute-start.2 = (bf16[1040,128]{1,0:T(8,128)(2,1)S(1)}, bf16[1040,128]{1,0:T(8,128)(2,1)S(1)}, u32[]{:S(2)}, u32[]{:S(2)}) collective-permute-start(bf16[1040,128]{1,0:T(8,128)(2,1)S(1)} %get-tuple-element.19), channel_id=1, source_target_pairs={{0,3},{1,0},{2,1},{3,2},{4,7},{5,4},{6,5},{7,6},{8,11},{9,8},{10,9... | collective-permute-start | bytes 798728 | tf_op jit(solution)/shard_map/ppermute | solution.py:514
  12.1 1.6 %collective-permute-start = (bf16[1040,128]{1,0:T(8,128)(2,1)S(1)}, bf16[1040,128]{1,0:T(8,128)(2,1)S(1)}, u32[]{:S(2)}, u32[]{:S(2)}) collective-permute-start(bf16[1040,128]{1,0:T(8,128)(2,1)S(1)} %get-tuple-element.17), channel_id=1, source_target_pairs={{0,2},{1,3},{2,0},{3,1},{4,6},{5,7},{6,4},{7,5},{8,10},{9,11},{10,... | collective-permute-start | bytes 798728 | tf_op jit(solution)/shard_map/ppermute | solution.py:514
  13.7 4.5 %own_rows.1.begun.after = f32[8192,128]{1,0:T(8,128)S(1)} custom-call(s32[2]{0:T(128)S(1)} %pad_add_fusion.1.place, s32[8,4,128]{2,1,0:T(4,128)S(1)} %get-tuple-element.14.keys, s32[4,8,128]{2,1,0:T(8,128)S(1)} %get-tuple-element.15.held, f32[2048,128]{1,0:T(8,128)S(1)} %get-tuple-element.16.wide), custom_call_target="tpu_custom_call" | custom-call | flops 10000000 | bytes 1000000 | tf_op jit(solution)/shard_map/own_rows/pallas_call | solution.py:246
  18.1 0.0 copy-start
  18.1 0.0 collective-permute-done.2.refs_2_
  18.1 6.6 %collective-permute-done.refs_0_ = bf16[1040,128]{1,0:T(8,128)(2,1)S(1)} collective-permute-done((bf16[1040,128]{1,0:T(8,128)(2,1)S(1)}, bf16[1040,128]{1,0:T(8,128)(2,1)S(1)}, u32[]{:S(2)}, u32[]{:S(2)}) %collective-permute-start) | collective-permute-done | bytes 266272 | tf_op jit(solution)/shard_map/ppermute | solution.py:514
  24.7 7.3 %scatter.1 = (f32[4096,128]{1,0:T(8,128)S(1)}, f32[4096,128]{1,0:T(8,128)S(1)}) custom-call(s32[2]{0:T(128)S(1)} %pad_add_fusion.1.place, f32[8192,128]{1,0:T(8,128)S(1)} %own_rows.1.begun.after, bf16[1040,128]{1,0:T(8,128)(2,1)S(1)} %collective-permute-done.refs_0_, bf16[1040,128]{1,0:T(8,128)(2,1)S(1)} %collective-permute-done.1.refs_1_, ...), custom_call_target="tpu_custom_call" | custom-call | flops 100000000 | bytes 1000000 | tf_op jit(solution)/shard_map/scatter/pallas_call | solution.py:264
  32.0 1.9 %collective-permute-start.3 = (f32[4096,128]{1,0:T(8,128)S(1)}, f32[4096,128]{1,0:T(8,128)S(1)}, u32[]{:S(2)}, u32[]{:S(2)}) collective-permute-start(f32[4096,128]{1,0:T(8,128)S(1)} %get-tuple-element.21), channel_id=1, source_target_pairs={{0,4},{4,0},{1,5},{5,1},{2,6},{6,2},{3,7},{7,3},{8,12},{12,8},{9,1... | collective-permute-start | bytes 6291464 | tf_op jit(solution)/shard_map/ppermute | solution.py:514
  33.9 3.8 %collective-permute-done.3.got = f32[4096,128]{1,0:T(8,128)S(1)} collective-permute-done((f32[4096,128]{1,0:T(8,128)S(1)}, f32[4096,128]{1,0:T(8,128)S(1)}, u32[]{:S(2)}, u32[]{:S(2)}) %collective-permute-start.3) | collective-permute-done | bytes 2097184 | tf_op jit(solution)/shard_map/ppermute | solution.py:514
  37.6 2.6 %encode.1 = s16[8,4,136,128]{3,2,1,0:T(8,128)(2,1)S(1)} custom-call(f32[4096,128]{1,0:T(8,128)S(1)} %get-tuple-element.20.mine, f32[4096,128]{1,0:T(8,128)S(1)} %collective-permute-done.3.got), custom_call_target="tpu_custom_call" | custom-call | flops 10000000 | bytes 1000000 | tf_op jit(solution)/shard_map/encode/pallas_call | solution.py:344
  40.3 20.6 %all_to_all.15.parts = s16[8,4,136,128]{3,2,1,0:T(8,128)(2,1)S(1)} all-to-all(s16[8,4,136,128]{3,2,1,0:T(8,128)(2,1)S(1)} %encode.1), channel_id=1, replica_groups=mesh['far'=4,'pair'=2,'ring'=4,'core'=2,'rows'=4] {'pair','ring'}, dimensions={0} | all-to-all | bytes 2228224 | tf_op jit(solution)/shard_map/all_to_all | solution.py:558
  60.9 1.2 first_sum.1
  62.1 14.5 %all_to_all.16.parts = s16[4,136,128]{2,1,0:T(8,128)(2,1)S(1)} all-to-all(s16[4,136,128]{2,1,0:T(8,128)(2,1)S(1)} %first_sum.1), channel_id=1, replica_groups=mesh['far'=4,'pair'=2,'ring'=4,'core'=2,'rows'=4] {'far'}, dimensions={0} | all-to-all | bytes 278528 | tf_op jit(solution)/shard_map/all_to_all | solution.py:559
  76.6 0.4 last_sum.1
  77.0 9.8 %all_to_all.17.refs_3_ = s16[4,136,128]{2,1,0:T(8,128)(2,1)S(1)} all-to-all(s16[4,136,128]{2,1,0:T(8,128)(2,1)S(1)} %last_sum.1), channel_id=1, replica_groups=mesh['far'=4,'pair'=2,'ring'=4,'core'=2,'rows'=4] {'far'}, dimensions={0} | all-to-all | bytes 278528 | tf_op jit(solution)/shard_map/all_to_all | solution.py:560
  86.7 1.6 %collective-permute-start.12 = (s16[4,136,128]{2,1,0:T(8,128)(2,1)S(1)}, s16[4,136,128]{2,1,0:T(8,128)(2,1)S(1)}, u32[]{:S(2)}, u32[]{:S(2)}) collective-permute-start(s16[4,136,128]{2,1,0:T(8,128)(2,1)S(1)} %all_to_all.17.refs_3_), channel_id=1, source_target_pairs={{0,48},{8,56},{16,32},{24,40},{32,16},{40,24},{48,0},{56,8},{1,49}... | collective-permute-start | bytes 417800 | tf_op jit(solution)/shard_map/ppermute | solution.py:524
  88.4 1.9 %collective-permute-start.13 = (s16[4,136,128]{2,1,0:T(8,128)(2,1)S(1)}, s16[4,136,128]{2,1,0:T(8,128)(2,1)S(1)}, u32[]{:S(2)}, u32[]{:S(2)}) collective-permute-start(s16[4,136,128]{2,1,0:T(8,128)(2,1)S(1)} %all_to_all.17.refs_3_), channel_id=1, source_target_pairs={{0,16},{8,24},{16,0},{24,8},{32,48},{40,56},{48,32},{56,40},{1,17}... | collective-permute-start | bytes 417800 | tf_op jit(solution)/shard_map/ppermute | solution.py:524
  90.3 1.4 %collective-permute-start.14 = (s16[4,136,128]{2,1,0:T(8,128)(2,1)S(1)}, s16[4,136,128]{2,1,0:T(8,128)(2,1)S(1)}, u32[]{:S(2)}, u32[]{:S(2)}) collective-permute-start(s16[4,136,128]{2,1,0:T(8,128)(2,1)S(1)} %all_to_all.17.refs_3_), channel_id=1, source_target_pairs={{0,56},{8,32},{16,40},{24,48},{32,24},{40,0},{48,8},{56,16},{1,57}... | collective-permute-start | bytes 417800 | tf_op jit(solution)/shard_map/ppermute | solution.py:524
  91.7 5.1 %collective-permute-start.18 = (s16[4,136,128]{2,1,0:T(8,128)(2,1)S(1)}, s16[4,136,128]{2,1,0:T(8,128)(2,1)S(1)}, u32[]{:S(2)}, u32[]{:S(2)}) collective-permute-start(s16[4,136,128]{2,1,0:T(8,128)(2,1)S(1)} %all_to_all.17.refs_3_), channel_id=1, source_target_pairs={{0,4},{4,0},{1,5},{5,1},{2,6},{6,2},{3,7},{7,3},{8,12},{12,8},{9,1... | collective-permute-start | bytes 417800 | tf_op jit(solution)/shard_map/ppermute | solution.py:514
  96.9 0.5 collective-permute-start.6
  97.4 0.9 collective-permute-start.7
  98.3 0.0 collective-permute-done.13.refs_1_
  98.3 2.1 %collective-permute-start.4 = (s16[4,136,128]{2,1,0:T(8,128)(2,1)S(1)}, s16[4,136,128]{2,1,0:T(8,128)(2,1)S(1)}, u32[]{:S(2)}, u32[]{:S(2)}) collective-permute-start(s16[4,136,128]{2,1,0:T(8,128)(2,1)S(1)} %all_to_all.17.refs_3_), channel_id=1, source_target_pairs={{0,40},{8,48},{16,56},{24,32},{32,8},{40,16},{48,24},{56,0},{1,41}... | collective-permute-start | bytes 417800 | tf_op jit(solution)/shard_map/ppermute | solution.py:524
  100.4 0.1 collective-permute-start.5
  100.5 3.7 %collective-permute-start.15 = (s16[4,136,128]{2,1,0:T(8,128)(2,1)S(1)}, s16[4,136,128]{2,1,0:T(8,128)(2,1)S(1)}, u32[]{:S(2)}, u32[]{:S(2)}) collective-permute-start(s16[4,136,128]{2,1,0:T(8,128)(2,1)S(1)} %collective-permute-done.12.refs_0_), channel_id=1, source_target_pairs={{0,4},{4,0},{1,5},{5,1},{2,6},{6,2},{3,7},{7,3},{8,12},{12,8},{9,1... | collective-permute-start | bytes 417800 | tf_op jit(solution)/shard_map/ppermute | solution.py:514
  104.2 0.0 collective-permute-done.6.refs_2_
  104.2 0.3 collective-permute-start.16
  104.5 2.3 %collective-permute-start.17 = (s16[4,136,128]{2,1,0:T(8,128)(2,1)S(1)}, s16[4,136,128]{2,1,0:T(8,128)(2,1)S(1)}, u32[]{:S(2)}, u32[]{:S(2)}) collective-permute-start(s16[4,136,128]{2,1,0:T(8,128)(2,1)S(1)} %collective-permute-done.14.refs_2_), channel_id=1, source_target_pairs={{0,4},{4,0},{1,5},{5,1},{2,6},{6,2},{3,7},{7,3},{8,12},{12,8},{9,1... | collective-permute-start | bytes 417800 | tf_op jit(solution)/shard_map/ppermute | solution.py:514
  106.8 1.3 %collective-permute-start.10 = (s16[4,136,128]{2,1,0:T(8,128)(2,1)S(1)}, s16[4,136,128]{2,1,0:T(8,128)(2,1)S(1)}, u32[]{:S(2)}, u32[]{:S(2)}) collective-permute-start(s16[4,136,128]{2,1,0:T(8,128)(2,1)S(1)} %collective-permute-done.6.refs_2_), channel_id=1, source_target_pairs={{0,4},{4,0},{1,5},{5,1},{2,6},{6,2},{3,7},{7,3},{8,12},{12,8},{9,1... | collective-permute-start | bytes 417800 | tf_op jit(solution)/shard_map/ppermute | solution.py:514
  108.0 1.1 collective-permute-start.11
  109.1 0.0 collective-permute-start.8
  109.1 0.5 collective-permute-start.9
  109.6 0.1 pad_add_fusion.2.groups
  109.7 0.1 stack.52.groups
  109.8 2.2 %copy-done.1 = f32[8192,128]{1,0:T(8,128)S(1)} copy-done((f32[8192,128]{1,0:T(8,128)S(1)}, f32[8192,128]{1,0:T(8,128)}, u32[]{:S(2)}) %copy-start.1) | copy-done | bytes 4194328
  112.0 2.2 %copy-done.2 = f32[2,4096,128]{2,1,0:T(8,128)S(1)} copy-done((f32[2,4096,128]{2,1,0:T(8,128)S(1)}, f32[2,4096,128]{2,1,0:T(8,128)}, u32[]{:S(2)}) %copy-start.2) | copy-done | bytes 4194328
  114.2 0.9 fetch.1
  115.1 0.1 pad_add_fusion.groups
  115.2 3.8 %update.2 = (f32[2,4096,128]{2,1,0:T(8,128)}, f32[2,4096]{1,0:T(2,128)}) custom-call(s32[4]{0:T(128)S(1)} %pad_add_fusion.2.groups, s32[1]{0:T(128)} %bitcast.4.core, s16[4,136,128]{2,1,0:T(8,128)(2,1)S(1)} %collective-permute-done.12.refs_0_, s16[4,136,128]{2,1,0:T(8,128)(2,1)S(1)} %collective-permute-done.13.refs_1_, ...), custom_call_target="tpu_custom_call" | custom-call | flops 10000000 | bytes 1000000 | tf_op jit(solution)/shard_map/update/pallas_call | solution.py:458
  119.0 3.8 %update.3 = (f32[2,4096,128]{2,1,0:T(8,128)}, f32[2,4096]{1,0:T(2,128)}) custom-call(s32[4]{0:T(128)S(1)} %pad_add_fusion.groups, s32[1]{0:T(128)} %bitcast.4.core, s16[4,136,128]{2,1,0:T(8,128)(2,1)S(1)} %collective-permute-done.4.refs_0_, s16[4,136,128]{2,1,0:T(8,128)(2,1)S(1)} %collective-permute-done.5.refs_1_, ...), custom_call_target="tpu_custom_call", output_to_operand_aliasing={{0}: (12, {}), {1}: (13, {})} | custom-call | flops 10000000 | bytes 1000000 | tf_op jit(solution)/shard_map/update/pallas_call | solution.py:458
  (23 shorter events, 0.1 us)
Async XLA Ops:
  0.7 1.0 copy-start.3
  1.8 0.7 copy-start.5
  2.5 0.7 copy-start.6
  3.2 0.7 copy-start.7
  8.4 9.8 %collective-permute-start.1 = (bf16[1040,128]{1,0:T(8,128)(2,1)S(1)}, bf16[1040,128]{1,0:T(8,128)(2,1)S(1)}, u32[]{:S(2)}, u32[]{:S(2)}) collective-permute-start(bf16[1040,128]{1,0:T(8,128)(2,1)S(1)} %get-tuple-element.18), channel_id=1, source_target_pairs={{0,1},{1,2},{2,3},{3,0},{4,5},{5,6},{6,7},{7,4},{8,9},{9,10},{10,1... | collective-permute-start | bytes 798728 | tf_op jit(solution)/shard_map/ppermute | solution.py:514
  10.6 7.6 %collective-permute-start.2 = (bf16[1040,128]{1,0:T(8,128)(2,1)S(1)}, bf16[1040,128]{1,0:T(8,128)(2,1)S(1)}, u32[]{:S(2)}, u32[]{:S(2)}) collective-permute-start(bf16[1040,128]{1,0:T(8,128)(2,1)S(1)} %get-tuple-element.19), channel_id=1, source_target_pairs={{0,3},{1,0},{2,1},{3,2},{4,7},{5,4},{6,5},{7,6},{8,11},{9,8},{10,9... | collective-permute-start | bytes 798728 | tf_op jit(solution)/shard_map/ppermute | solution.py:514
  12.1 12.6 %collective-permute-start = (bf16[1040,128]{1,0:T(8,128)(2,1)S(1)}, bf16[1040,128]{1,0:T(8,128)(2,1)S(1)}, u32[]{:S(2)}, u32[]{:S(2)}) collective-permute-start(bf16[1040,128]{1,0:T(8,128)(2,1)S(1)} %get-tuple-element.17), channel_id=1, source_target_pairs={{0,2},{1,3},{2,0},{3,1},{4,6},{5,7},{6,4},{7,5},{8,10},{9,11},{10,... | collective-permute-start | bytes 798728 | tf_op jit(solution)/shard_map/ppermute | solution.py:514
  18.1 13.9 %copy-start = (f32[8192,128]{1,0:T(8,128)}, f32[8192,128]{1,0:T(8,128)S(1)}, u32[]{:S(2)}) copy-start(f32[8192,128]{1,0:T(8,128)S(1)} %own_rows.1.begun.after) | copy-start | bytes 12582916
  32.0 5.7 %collective-permute-start.3 = (f32[4096,128]{1,0:T(8,128)S(1)}, f32[4096,128]{1,0:T(8,128)S(1)}, u32[]{:S(2)}, u32[]{:S(2)}) collective-permute-start(f32[4096,128]{1,0:T(8,128)S(1)} %get-tuple-element.21), channel_id=1, source_target_pairs={{0,4},{4,0},{1,5},{5,1},{2,6},{6,2},{3,7},{7,3},{8,12},{12,8},{9,1... | collective-permute-start | bytes 6291464 | tf_op jit(solution)/shard_map/ppermute | solution.py:514
  86.7 10.7 %collective-permute-start.12 = (s16[4,136,128]{2,1,0:T(8,128)(2,1)S(1)}, s16[4,136,128]{2,1,0:T(8,128)(2,1)S(1)}, u32[]{:S(2)}, u32[]{:S(2)}) collective-permute-start(s16[4,136,128]{2,1,0:T(8,128)(2,1)S(1)} %all_to_all.17.refs_3_), channel_id=1, source_target_pairs={{0,48},{8,56},{16,32},{24,40},{32,16},{40,24},{48,0},{56,8},{1,49}... | collective-permute-start | bytes 417800 | tf_op jit(solution)/shard_map/ppermute | solution.py:524
  88.4 10.0 %collective-permute-start.13 = (s16[4,136,128]{2,1,0:T(8,128)(2,1)S(1)}, s16[4,136,128]{2,1,0:T(8,128)(2,1)S(1)}, u32[]{:S(2)}, u32[]{:S(2)}) collective-permute-start(s16[4,136,128]{2,1,0:T(8,128)(2,1)S(1)} %all_to_all.17.refs_3_), channel_id=1, source_target_pairs={{0,16},{8,24},{16,0},{24,8},{32,48},{40,56},{48,32},{56,40},{1,17}... | collective-permute-start | bytes 417800 | tf_op jit(solution)/shard_map/ppermute | solution.py:524
  90.3 10.1 %collective-permute-start.14 = (s16[4,136,128]{2,1,0:T(8,128)(2,1)S(1)}, s16[4,136,128]{2,1,0:T(8,128)(2,1)S(1)}, u32[]{:S(2)}, u32[]{:S(2)}) collective-permute-start(s16[4,136,128]{2,1,0:T(8,128)(2,1)S(1)} %all_to_all.17.refs_3_), channel_id=1, source_target_pairs={{0,56},{8,32},{16,40},{24,48},{32,24},{40,0},{48,8},{56,16},{1,57}... | collective-permute-start | bytes 417800 | tf_op jit(solution)/shard_map/ppermute | solution.py:524
  91.7 8.8 %collective-permute-start.18 = (s16[4,136,128]{2,1,0:T(8,128)(2,1)S(1)}, s16[4,136,128]{2,1,0:T(8,128)(2,1)S(1)}, u32[]{:S(2)}, u32[]{:S(2)}) collective-permute-start(s16[4,136,128]{2,1,0:T(8,128)(2,1)S(1)} %all_to_all.17.refs_3_), channel_id=1, source_target_pairs={{0,4},{4,0},{1,5},{5,1},{2,6},{6,2},{3,7},{7,3},{8,12},{12,8},{9,1... | collective-permute-start | bytes 417800 | tf_op jit(solution)/shard_map/ppermute | solution.py:514
  96.9 7.3 %collective-permute-start.6 = (s16[4,136,128]{2,1,0:T(8,128)(2,1)S(1)}, s16[4,136,128]{2,1,0:T(8,128)(2,1)S(1)}, u32[]{:S(2)}, u32[]{:S(2)}) collective-permute-start(s16[4,136,128]{2,1,0:T(8,128)(2,1)S(1)} %all_to_all.17.refs_3_), channel_id=1, source_target_pairs={{0,24},{8,0},{16,8},{24,16},{32,56},{40,32},{48,40},{56,48},{1,25}... | collective-permute-start | bytes 417800 | tf_op jit(solution)/shard_map/ppermute | solution.py:524
  97.4 7.0 %collective-permute-start.7 = (s16[4,136,128]{2,1,0:T(8,128)(2,1)S(1)}, s16[4,136,128]{2,1,0:T(8,128)(2,1)S(1)}, u32[]{:S(2)}, u32[]{:S(2)}) collective-permute-start(s16[4,136,128]{2,1,0:T(8,128)(2,1)S(1)} %all_to_all.17.refs_3_), channel_id=1, source_target_pairs={{0,8},{8,16},{16,24},{24,0},{32,40},{40,48},{48,56},{56,32},{1,9},... | collective-permute-start | bytes 417800 | tf_op jit(solution)/shard_map/ppermute | solution.py:524
  98.3 8.4 %collective-permute-start.4 = (s16[4,136,128]{2,1,0:T(8,128)(2,1)S(1)}, s16[4,136,128]{2,1,0:T(8,128)(2,1)S(1)}, u32[]{:S(2)}, u32[]{:S(2)}) collective-permute-start(s16[4,136,128]{2,1,0:T(8,128)(2,1)S(1)} %all_to_all.17.refs_3_), channel_id=1, source_target_pairs={{0,40},{8,48},{16,56},{24,32},{32,8},{40,16},{48,24},{56,0},{1,41}... | collective-permute-start | bytes 417800 | tf_op jit(solution)/shard_map/ppermute | solution.py:524
  100.4 7.6 %collective-permute-start.5 = (s16[4,136,128]{2,1,0:T(8,128)(2,1)S(1)}, s16[4,136,128]{2,1,0:T(8,128)(2,1)S(1)}, u32[]{:S(2)}, u32[]{:S(2)}) collective-permute-start(s16[4,136,128]{2,1,0:T(8,128)(2,1)S(1)} %all_to_all.17.refs_3_), channel_id=1, source_target_pairs={{0,32},{8,40},{16,48},{24,56},{32,0},{40,8},{48,16},{56,24},{1,33}... | collective-permute-start | bytes 417800 | tf_op jit(solution)/shard_map/ppermute | solution.py:524
  100.5 8.6 %collective-permute-start.15 = (s16[4,136,128]{2,1,0:T(8,128)(2,1)S(1)}, s16[4,136,128]{2,1,0:T(8,128)(2,1)S(1)}, u32[]{:S(2)}, u32[]{:S(2)}) collective-permute-start(s16[4,136,128]{2,1,0:T(8,128)(2,1)S(1)} %collective-permute-done.12.refs_0_), channel_id=1, source_target_pairs={{0,4},{4,0},{1,5},{5,1},{2,6},{6,2},{3,7},{7,3},{8,12},{12,8},{9,1... | collective-permute-start | bytes 417800 | tf_op jit(solution)/shard_map/ppermute | solution.py:514
  104.2 4.9 %collective-permute-start.16 = (s16[4,136,128]{2,1,0:T(8,128)(2,1)S(1)}, s16[4,136,128]{2,1,0:T(8,128)(2,1)S(1)}, u32[]{:S(2)}, u32[]{:S(2)}) collective-permute-start(s16[4,136,128]{2,1,0:T(8,128)(2,1)S(1)} %collective-permute-done.13.refs_1_), channel_id=1, source_target_pairs={{0,4},{4,0},{1,5},{5,1},{2,6},{6,2},{3,7},{7,3},{8,12},{12,8},{9,1... | collective-permute-start | bytes 417800 | tf_op jit(solution)/shard_map/ppermute | solution.py:514
  104.5 10.7 %collective-permute-start.17 = (s16[4,136,128]{2,1,0:T(8,128)(2,1)S(1)}, s16[4,136,128]{2,1,0:T(8,128)(2,1)S(1)}, u32[]{:S(2)}, u32[]{:S(2)}) collective-permute-start(s16[4,136,128]{2,1,0:T(8,128)(2,1)S(1)} %collective-permute-done.14.refs_2_), channel_id=1, source_target_pairs={{0,4},{4,0},{1,5},{5,1},{2,6},{6,2},{3,7},{7,3},{8,12},{12,8},{9,1... | collective-permute-start | bytes 417800 | tf_op jit(solution)/shard_map/ppermute | solution.py:514
  106.8 12.2 %collective-permute-start.10 = (s16[4,136,128]{2,1,0:T(8,128)(2,1)S(1)}, s16[4,136,128]{2,1,0:T(8,128)(2,1)S(1)}, u32[]{:S(2)}, u32[]{:S(2)}) collective-permute-start(s16[4,136,128]{2,1,0:T(8,128)(2,1)S(1)} %collective-permute-done.6.refs_2_), channel_id=1, source_target_pairs={{0,4},{4,0},{1,5},{5,1},{2,6},{6,2},{3,7},{7,3},{8,12},{12,8},{9,1... | collective-permute-start | bytes 417800 | tf_op jit(solution)/shard_map/ppermute | solution.py:514
  108.0 10.9 %collective-permute-start.11 = (s16[4,136,128]{2,1,0:T(8,128)(2,1)S(1)}, s16[4,136,128]{2,1,0:T(8,128)(2,1)S(1)}, u32[]{:S(2)}, u32[]{:S(2)}) collective-permute-start(s16[4,136,128]{2,1,0:T(8,128)(2,1)S(1)} %collective-permute-done.7.refs_3_), channel_id=1, source_target_pairs={{0,4},{4,0},{1,5},{5,1},{2,6},{6,2},{3,7},{7,3},{8,12},{12,8},{9,1... | collective-permute-start | bytes 417800 | tf_op jit(solution)/shard_map/ppermute | solution.py:514
  109.1 9.8 %collective-permute-start.8 = (s16[4,136,128]{2,1,0:T(8,128)(2,1)S(1)}, s16[4,136,128]{2,1,0:T(8,128)(2,1)S(1)}, u32[]{:S(2)}, u32[]{:S(2)}) collective-permute-start(s16[4,136,128]{2,1,0:T(8,128)(2,1)S(1)} %collective-permute-done.4.refs_0_), channel_id=1, source_target_pairs={{0,4},{4,0},{1,5},{5,1},{2,6},{6,2},{3,7},{7,3},{8,12},{12,8},{9,1... | collective-permute-start | bytes 417800 | tf_op jit(solution)/shard_map/ppermute | solution.py:514
  109.1 9.8 %collective-permute-start.9 = (s16[4,136,128]{2,1,0:T(8,128)(2,1)S(1)}, s16[4,136,128]{2,1,0:T(8,128)(2,1)S(1)}, u32[]{:S(2)}, u32[]{:S(2)}) collective-permute-start(s16[4,136,128]{2,1,0:T(8,128)(2,1)S(1)} %collective-permute-done.5.refs_1_), channel_id=1, source_target_pairs={{0,4},{4,0},{1,5},{5,1},{2,6},{6,2},{3,7},{7,3},{8,12},{12,8},{9,1... | collective-permute-start | bytes 417800 | tf_op jit(solution)/shard_map/ppermute | solution.py:514
  109.8 2.2 %copy-start.1 = (f32[8192,128]{1,0:T(8,128)S(1)}, f32[8192,128]{1,0:T(8,128)}, u32[]{:S(2)}) copy-start(f32[8192,128]{1,0:T(8,128)} %copy-done) | copy-start | bytes 12582916
  112.0 2.2 %copy-start.2 = (f32[2,4096,128]{2,1,0:T(8,128)S(1)}, f32[2,4096,128]{2,1,0:T(8,128)}, u32[]{:S(2)}) copy-start(f32[2,4096,128]{2,1,0:T(8,128)} %rows.1) | copy-start | bytes 12582916
  114.2 1.0 copy-start.4
where the time goes:
time: 123 us
  blocking collectives  44.9 us (37%)
  starting transfers between devices  30 us (24%)
  Pallas kernels  28.9 us (23%)
  waiting for transfers between devices  10.4 us (8%)
  local copies, waits for them, and re-layouts  7.6 us (6%)
    ppermute x12, starting transfers between devices, shift(): return lax.ppermute(x, axis, [(i, (i + by) % count) for i in range(count)])  21.4 us
    all_to_all x1, blocking collectives, shards(): parts = lax.all_to_all(coded, SQUARE, 0, 0, tiled=True)  20.6 us
    all_to_all x1, blocking collectives, shards(): parts = lax.all_to_all(first_sum(parts), 'far', 0, 0, tiled=True)  14.5 us
    ppermute x12, waiting for transfers between devices, shift(): return lax.ppermute(x, axis, [(i, (i + by) % count) for i in range(count)])  10.4 us
    all_to_all x1, blocking collectives, shards(): bundle = lax.all_to_all(last_sum(parts), 'far', 0, 0, tiled=True)  9.77 us
    ppermute x7, starting transfers between devices, square_shift(): return lax.ppermute(x, SQUARE, links)  8.62 us
    pallas_call x2, Pallas kernels, update(): pl.pallas_call(functools.partial(update_kernel, count), grid_spec=pltpu.P...  7.53 us
    unnamed x16, local copies, waits for them, and re-layouts  7.52 us
  transfers between devices with their start and end apart: 19, of which 2 were waited for; matrix products, arithmetic and copies ran while one was open for 0% of the time, Pallas kernels for 7%

commit v1 on v0

--- a/solution.py
+++ b/solution.py
@@ -509,6 +509,22 @@
     )(groups, rows, after)
 
 
+def keep_kernel(state, out):
+    out[...] = state[...]
+
+
+def keep(state):
+    return pl.pallas_call(
+        keep_kernel,
+        out_shape=jax.ShapeDtypeStruct(state.shape, state.dtype),
+        in_specs=[VM],
+        out_specs=VM,
+        compiler_params=room(1),
+        cost_estimate=cost(10**5),
+        name="keep",
+    )(state)
+
+
 def shift(x, axis, by):
     count = lax.axis_size(axis)
     return lax.ppermute(x, axis, [(i, (i + by) % count) for i in range(count)])
@@ -561,6 +577,7 @@
     whole = [None] * len(hops)
     for d in reversed(range(len(hops))):
         whole[d] = square_shift(bundle, *hops[d]) if d else bundle
+    state = keep(accum)
     swapped = [shift(w, "core", 1) for w in whole]
     result = ()
     for i in range(2):
@@ -570,7 +587,7 @@
             [whole[d] for d in order[i]],
             [swapped[d] for d in order[i]],
             fetched[i],
-            accum,
+            state,
             result,
         )
     return result

time: 123 us -> 123 us (level)
  no operation moved by 1% of the time
where the time goes in v1:
time: 123 us
  blocking collectives  44.9 us (37%)
  starting transfers between devices  30 us (24%)
  Pallas kernels  28.9 us (23%)
  waiting for transfers between devices  10.4 us (8%)
  local copies, waits for them, and re-layouts  7.61 us (6%)
    ppermute x12, starting transfers between devices, shift(): return lax.ppermute(x, axis, [(i, (i + by) % count) for i in range(count)])  21.4 us
    all_to_all x1, blocking collectives, shards(): parts = lax.all_to_all(coded, SQUARE, 0, 0, tiled=True)  20.6 us
    all_to_all x1, blocking collectives, shards(): parts = lax.all_to_all(first_sum(parts), 'far', 0, 0, tiled=True)  14.5 us
    ppermute x12, waiting for transfers between devices, shift(): return lax.ppermute(x, axis, [(i, (i + by) % count) for i in range(count)])  10.4 us
    all_to_all x1, blocking collectives, shards(): bundle = lax.all_to_all(last_sum(parts), 'far', 0, 0, tiled=True)  9.77 us
    ppermute x7, starting transfers between devices, square_shift(): return lax.ppermute(x, SQUARE, links)  8.62 us
    pallas_call x2, Pallas kernels, update(): pl.pallas_call(functools.partial(update_kernel, count), grid_spec=pltpu.P...  7.53 us
    unnamed x16, local copies, waits for them, and re-layouts  7.52 us
  transfers between devices with their start and end apart: 19, of which 2 were waited for; matrix products, arithmetic and copies ran while one was open for 0% of the time, Pallas kernels for 7%

profile of v1, /device:TPU:1, one launch (start us, length us, event | category | flops | bytes accessed | tf_op | source)
XLA Modules:
  0.0 122.8 jit_solution(383567205601800518)
XLA Ops:
  0.6 0.1 pad_add_fusion.1.place
  0.7 1.0 copy-done.3
  1.8 0.7 copy-done.4
  2.5 0.7 copy-done.6
  3.2 0.7 copy-done.7
  3.8 1.9 %first_pick.1 = (bf16[1040,128]{1,0:T(8,128)(2,1)S(1)}, f32[2048,128]{1,0:T(8,128)S(1)}, s32[4,8,128]{2,1,0:T(8,128)S(1)}, s32[8,4,128]{2,1,0:T(4,128)S(1)}) custom-call(s32[2]{0:T(128)S(1)} %pad_add_fusion.1.place, s32[1,4]{1,0:T(1,128)S(1)} %copy-done.7, s32[8,4,128]{2,1,0:T(4,128)S(1)} %bitcast.18, s32[8,4,128]{2,1,0:T(4,128)S(1)} %bitcast.19, ...), custom_call_target="tpu_custom_call" | custom-call | flops 10000000 | bytes 1000000 | tf_op jit(solution)/shard_map/first_pick/pallas_call | solution.py:94
  5.7 2.6 %pick.1 = (bf16[1040,128]{1,0:T(8,128)(2,1)S(1)}, bf16[1040,128]{1,0:T(8,128)(2,1)S(1)}) custom-call(s32[2]{0:T(128)S(1)} %pad_add_fusion.1.place, s32[8,4,128]{2,1,0:T(4,128)S(1)} %get-tuple-element.14.keys, s32[4,8,128]{2,1,0:T(8,128)S(1)} %get-tuple-element.15.held, f32[2048,128]{1,0:T(8,128)S(1)} %get-tuple-element.16.wide), custom_call_target="tpu_custom_call" | custom-call | flops 20000000 | bytes 1000000 | tf_op jit(solution)/shard_map/pick/pallas_call | solution.py:122
  8.4 2.2 %collective-permute-start.1 = (bf16[1040,128]{1,0:T(8,128)(2,1)S(1)}, bf16[1040,128]{1,0:T(8,128)(2,1)S(1)}, u32[]{:S(2)}, u32[]{:S(2)}) collective-permute-start(bf16[1040,128]{1,0:T(8,128)(2,1)S(1)} %get-tuple-element.18), channel_id=1, source_target_pairs={{0,1},{1,2},{2,3},{3,0},{4,5},{5,6},{6,7},{7,4},{8,9},{9,10},{10,1... | collective-permute-start | bytes 798728 | tf_op jit(solution)/shard_map/ppermute | solution.py:530
  10.6 1.5 %collective-permute-start.2 = (bf16[1040,128]{1,0:T(8,128)(2,1)S(1)}, bf16[1040,128]{1,0:T(8,128)(2,1)S(1)}, u32[]{:S(2)}, u32[]{:S(2)}) collective-permute-start(bf16[1040,128]{1,0:T(8,128)(2,1)S(1)} %get-tuple-element.19), channel_id=1, source_target_pairs={{0,3},{1,0},{2,1},{3,2},{4,7},{5,4},{6,5},{7,6},{8,11},{9,8},{10,9... | collective-permute-start | bytes 798728 | tf_op jit(solution)/shard_map/ppermute | solution.py:530
  12.1 1.6 %collective-permute-start = (bf16[1040,128]{1,0:T(8,128)(2,1)S(1)}, bf16[1040,128]{1,0:T(8,128)(2,1)S(1)}, u32[]{:S(2)}, u32[]{:S(2)}) collective-permute-start(bf16[1040,128]{1,0:T(8,128)(2,1)S(1)} %get-tuple-element.17), channel_id=1, source_target_pairs={{0,2},{1,3},{2,0},{3,1},{4,6},{5,7},{6,4},{7,5},{8,10},{9,11},{10,... | collective-permute-start | bytes 798728 | tf_op jit(solution)/shard_map/ppermute | solution.py:530
  13.7 4.5 %own_rows.1.begun.after = f32[8192,128]{1,0:T(8,128)S(1)} custom-call(s32[2]{0:T(128)S(1)} %pad_add_fusion.1.place, s32[8,4,128]{2,1,0:T(4,128)S(1)} %get-tuple-element.14.keys, s32[4,8,128]{2,1,0:T(8,128)S(1)} %get-tuple-element.15.held, f32[2048,128]{1,0:T(8,128)S(1)} %get-tuple-element.16.wide), custom_call_target="tpu_custom_call" | custom-call | flops 10000000 | bytes 1000000 | tf_op jit(solution)/shard_map/own_rows/pallas_call | solution.py:246
  18.1 0.0 copy-start
  18.1 0.0 collective-permute-done.2.refs_2_
  18.1 6.6 %collective-permute-done.refs_0_ = bf16[1040,128]{1,0:T(8,128)(2,1)S(1)} collective-permute-done((bf16[1040,128]{1,0:T(8,128)(2,1)S(1)}, bf16[1040,128]{1,0:T(8,128)(2,1)S(1)}, u32[]{:S(2)}, u32[]{:S(2)}) %collective-permute-start) | collective-permute-done | bytes 266272 | tf_op jit(solution)/shard_map/ppermute | solution.py:530
  24.7 7.3 %scatter.1 = (f32[4096,128]{1,0:T(8,128)S(1)}, f32[4096,128]{1,0:T(8,128)S(1)}) custom-call(s32[2]{0:T(128)S(1)} %pad_add_fusion.1.place, f32[8192,128]{1,0:T(8,128)S(1)} %own_rows.1.begun.after, bf16[1040,128]{1,0:T(8,128)(2,1)S(1)} %collective-permute-done.refs_0_, bf16[1040,128]{1,0:T(8,128)(2,1)S(1)} %collective-permute-done.1.refs_1_, ...), custom_call_target="tpu_custom_call" | custom-call | flops 100000000 | bytes 1000000 | tf_op jit(solution)/shard_map/scatter/pallas_call | solution.py:264
  32.0 1.9 %collective-permute-start.3 = (f32[4096,128]{1,0:T(8,128)S(1)}, f32[4096,128]{1,0:T(8,128)S(1)}, u32[]{:S(2)}, u32[]{:S(2)}) collective-permute-start(f32[4096,128]{1,0:T(8,128)S(1)} %get-tuple-element.21), channel_id=1, source_target_pairs={{0,4},{4,0},{1,5},{5,1},{2,6},{6,2},{3,7},{7,3},{8,12},{12,8},{9,1... | collective-permute-start | bytes 6291464 | tf_op jit(solution)/shard_map/ppermute | solution.py:530
  33.9 3.8 %collective-permute-done.3.got = f32[4096,128]{1,0:T(8,128)S(1)} collective-permute-done((f32[4096,128]{1,0:T(8,128)S(1)}, f32[4096,128]{1,0:T(8,128)S(1)}, u32[]{:S(2)}, u32[]{:S(2)}) %collective-permute-start.3) | collective-permute-done | bytes 2097184 | tf_op jit(solution)/shard_map/ppermute | solution.py:530
  37.6 2.6 %encode.1 = s16[8,4,136,128]{3,2,1,0:T(8,128)(2,1)S(1)} custom-call(f32[4096,128]{1,0:T(8,128)S(1)} %get-tuple-element.20.mine, f32[4096,128]{1,0:T(8,128)S(1)} %collective-permute-done.3.got), custom_call_target="tpu_custom_call" | custom-call | flops 10000000 | bytes 1000000 | tf_op jit(solution)/shard_map/encode/pallas_call | solution.py:344
  40.3 0.0 copy-start.5
  40.3 20.6 %all_to_all.15.parts = s16[8,4,136,128]{3,2,1,0:T(8,128)(2,1)S(1)} all-to-all(s16[8,4,136,128]{3,2,1,0:T(8,128)(2,1)S(1)} %encode.1), channel_id=1, replica_groups=mesh['far'=4,'pair'=2,'ring'=4,'core'=2,'rows'=4] {'pair','ring'}, dimensions={0} | all-to-all | bytes 2228224 | tf_op jit(solution)/shard_map/all_to_all | solution.py:574
  60.9 1.2 first_sum.1
  62.1 14.5 %all_to_all.16.parts = s16[4,136,128]{2,1,0:T(8,128)(2,1)S(1)} all-to-all(s16[4,136,128]{2,1,0:T(8,128)(2,1)S(1)} %first_sum.1), channel_id=1, replica_groups=mesh['far'=4,'pair'=2,'ring'=4,'core'=2,'rows'=4] {'far'}, dimensions={0} | all-to-all | bytes 278528 | tf_op jit(solution)/shard_map/all_to_all | solution.py:575
  76.6 0.4 last_sum.1
  77.0 9.8 %all_to_all.17.refs_3_ = s16[4,136,128]{2,1,0:T(8,128)(2,1)S(1)} all-to-all(s16[4,136,128]{2,1,0:T(8,128)(2,1)S(1)} %last_sum.1), channel_id=1, replica_groups=mesh['far'=4,'pair'=2,'ring'=4,'core'=2,'rows'=4] {'far'}, dimensions={0} | all-to-all | bytes 278528 | tf_op jit(solution)/shard_map/all_to_all | solution.py:576
  86.8 1.6 %collective-permute-start.12 = (s16[4,136,128]{2,1,0:T(8,128)(2,1)S(1)}, s16[4,136,128]{2,1,0:T(8,128)(2,1)S(1)}, u32[]{:S(2)}, u32[]{:S(2)}) collective-permute-start(s16[4,136,128]{2,1,0:T(8,128)(2,1)S(1)} %all_to_all.17.refs_3_), channel_id=1, source_target_pairs={{0,48},{8,56},{16,32},{24,40},{32,16},{40,24},{48,0},{56,8},{1,49}... | collective-permute-start | bytes 417800 | tf_op jit(solution)/shard_map/ppermute | solution.py:540
  88.4 1.9 %collective-permute-start.13 = (s16[4,136,128]{2,1,0:T(8,128)(2,1)S(1)}, s16[4,136,128]{2,1,0:T(8,128)(2,1)S(1)}, u32[]{:S(2)}, u32[]{:S(2)}) collective-permute-start(s16[4,136,128]{2,1,0:T(8,128)(2,1)S(1)} %all_to_all.17.refs_3_), channel_id=1, source_target_pairs={{0,16},{8,24},{16,0},{24,8},{32,48},{40,56},{48,32},{56,40},{1,17}... | collective-permute-start | bytes 417800 | tf_op jit(solution)/shard_map/ppermute | solution.py:540
  90.3 1.4 %collective-permute-start.14 = (s16[4,136,128]{2,1,0:T(8,128)(2,1)S(1)}, s16[4,136,128]{2,1,0:T(8,128)(2,1)S(1)}, u32[]{:S(2)}, u32[]{:S(2)}) collective-permute-start(s16[4,136,128]{2,1,0:T(8,128)(2,1)S(1)} %all_to_all.17.refs_3_), channel_id=1, source_target_pairs={{0,56},{8,32},{16,40},{24,48},{32,24},{40,0},{48,8},{56,16},{1,57}... | collective-permute-start | bytes 417800 | tf_op jit(solution)/shard_map/ppermute | solution.py:540
  91.7 5.1 %collective-permute-start.18 = (s16[4,136,128]{2,1,0:T(8,128)(2,1)S(1)}, s16[4,136,128]{2,1,0:T(8,128)(2,1)S(1)}, u32[]{:S(2)}, u32[]{:S(2)}) collective-permute-start(s16[4,136,128]{2,1,0:T(8,128)(2,1)S(1)} %all_to_all.17.refs_3_), channel_id=1, source_target_pairs={{0,4},{4,0},{1,5},{5,1},{2,6},{6,2},{3,7},{7,3},{8,12},{12,8},{9,1... | collective-permute-start | bytes 417800 | tf_op jit(solution)/shard_map/ppermute | solution.py:530
  96.9 0.5 collective-permute-start.6
  97.4 0.9 collective-permute-start.7
  98.4 0.0 collective-permute-done.13.refs_1_
  98.4 2.1 %collective-permute-start.4 = (s16[4,136,128]{2,1,0:T(8,128)(2,1)S(1)}, s16[4,136,128]{2,1,0:T(8,128)(2,1)S(1)}, u32[]{:S(2)}, u32[]{:S(2)}) collective-permute-start(s16[4,136,128]{2,1,0:T(8,128)(2,1)S(1)} %all_to_all.17.refs_3_), channel_id=1, source_target_pairs={{0,40},{8,48},{16,56},{24,32},{32,8},{40,16},{48,24},{56,0},{1,41}... | collective-permute-start | bytes 417800 | tf_op jit(solution)/shard_map/ppermute | solution.py:540
  100.4 0.1 collective-permute-start.5
  100.5 3.7 %collective-permute-start.15 = (s16[4,136,128]{2,1,0:T(8,128)(2,1)S(1)}, s16[4,136,128]{2,1,0:T(8,128)(2,1)S(1)}, u32[]{:S(2)}, u32[]{:S(2)}) collective-permute-start(s16[4,136,128]{2,1,0:T(8,128)(2,1)S(1)} %collective-permute-done.12.refs_0_), channel_id=1, source_target_pairs={{0,4},{4,0},{1,5},{5,1},{2,6},{6,2},{3,7},{7,3},{8,12},{12,8},{9,1... | collective-permute-start | bytes 417800 | tf_op jit(solution)/shard_map/ppermute | solution.py:530
  104.2 0.3 collective-permute-start.16
  104.5 2.3 %collective-permute-start.17 = (s16[4,136,128]{2,1,0:T(8,128)(2,1)S(1)}, s16[4,136,128]{2,1,0:T(8,128)(2,1)S(1)}, u32[]{:S(2)}, u32[]{:S(2)}) collective-permute-start(s16[4,136,128]{2,1,0:T(8,128)(2,1)S(1)} %collective-permute-done.14.refs_2_), channel_id=1, source_target_pairs={{0,4},{4,0},{1,5},{5,1},{2,6},{6,2},{3,7},{7,3},{8,12},{12,8},{9,1... | collective-permute-start | bytes 417800 | tf_op jit(solution)/shard_map/ppermute | solution.py:530
  106.8 1.3 %collective-permute-start.10 = (s16[4,136,128]{2,1,0:T(8,128)(2,1)S(1)}, s16[4,136,128]{2,1,0:T(8,128)(2,1)S(1)}, u32[]{:S(2)}, u32[]{:S(2)}) collective-permute-start(s16[4,136,128]{2,1,0:T(8,128)(2,1)S(1)} %collective-permute-done.6.refs_2_), channel_id=1, source_target_pairs={{0,4},{4,0},{1,5},{5,1},{2,6},{6,2},{3,7},{7,3},{8,12},{12,8},{9,1... | collective-permute-start | bytes 417800 | tf_op jit(solution)/shard_map/ppermute | solution.py:530
  108.1 1.1 collective-permute-start.11
  109.1 0.0 collective-permute-start.8
  109.1 0.5 collective-permute-start.9
  109.7 0.1 pad_add_fusion.2.groups
  109.7 0.1 stack.52.groups
  109.8 2.2 %copy-done.1 = f32[8192,128]{1,0:T(8,128)S(1)} copy-done((f32[8192,128]{1,0:T(8,128)S(1)}, f32[8192,128]{1,0:T(8,128)}, u32[]{:S(2)}) %copy-start.1) | copy-done | bytes 4194328
  112.0 2.2 %copy-done.2 = f32[2,4096,128]{2,1,0:T(8,128)S(1)} copy-done((f32[2,4096,128]{2,1,0:T(8,128)S(1)}, f32[2,4096,128]{2,1,0:T(8,128)}, u32[]{:S(2)}) %copy-start.2) | copy-done | bytes 4194328
  114.2 0.9 fetch.1
  115.1 0.1 pad_add_fusion.groups
  115.2 3.8 %update.2 = (f32[2,4096,128]{2,1,0:T(8,128)}, f32[2,4096]{1,0:T(2,128)}) custom-call(s32[4]{0:T(128)S(1)} %pad_add_fusion.2.groups, s32[1]{0:T(128)} %bitcast.4.core, s16[4,136,128]{2,1,0:T(8,128)(2,1)S(1)} %collective-permute-done.12.refs_0_, s16[4,136,128]{2,1,0:T(8,128)(2,1)S(1)} %collective-permute-done.13.refs_1_, ...), custom_call_target="tpu_custom_call" | custom-call | flops 10000000 | bytes 1000000 | tf_op jit(solution)/shard_map/update/pallas_call | solution.py:458
  119.0 3.8 %update.3 = (f32[2,4096,128]{2,1,0:T(8,128)}, f32[2,4096]{1,0:T(2,128)}) custom-call(s32[4]{0:T(128)S(1)} %pad_add_fusion.groups, s32[1]{0:T(128)} %bitcast.4.core, s16[4,136,128]{2,1,0:T(8,128)(2,1)S(1)} %collective-permute-done.4.refs_0_, s16[4,136,128]{2,1,0:T(8,128)(2,1)S(1)} %collective-permute-done.5.refs_1_, ...), custom_call_target="tpu_custom_call", output_to_operand_aliasing={{0}: (12, {}), {1}: (13, {})} | custom-call | flops 10000000 | bytes 1000000 | tf_op jit(solution)/shard_map/update/pallas_call | solution.py:458
  (24 shorter events, 0.1 us)
Async XLA Ops:
  0.7 1.0 copy-start.3
  1.8 0.7 copy-start.4
  2.5 0.7 copy-start.6
  3.2 0.7 copy-start.7
  8.4 9.8 %collective-permute-start.1 = (bf16[1040,128]{1,0:T(8,128)(2,1)S(1)}, bf16[1040,128]{1,0:T(8,128)(2,1)S(1)}, u32[]{:S(2)}, u32[]{:S(2)}) collective-permute-start(bf16[1040,128]{1,0:T(8,128)(2,1)S(1)} %get-tuple-element.18), channel_id=1, source_target_pairs={{0,1},{1,2},{2,3},{3,0},{4,5},{5,6},{6,7},{7,4},{8,9},{9,10},{10,1... | collective-permute-start | bytes 798728 | tf_op jit(solution)/shard_map/ppermute | solution.py:530
  10.6 7.6 %collective-permute-start.2 = (bf16[1040,128]{1,0:T(8,128)(2,1)S(1)}, bf16[1040,128]{1,0:T(8,128)(2,1)S(1)}, u32[]{:S(2)}, u32[]{:S(2)}) collective-permute-start(bf16[1040,128]{1,0:T(8,128)(2,1)S(1)} %get-tuple-element.19), channel_id=1, source_target_pairs={{0,3},{1,0},{2,1},{3,2},{4,7},{5,4},{6,5},{7,6},{8,11},{9,8},{10,9... | collective-permute-start | bytes 798728 | tf_op jit(solution)/shard_map/ppermute | solution.py:530
  12.1 12.6 %collective-permute-start = (bf16[1040,128]{1,0:T(8,128)(2,1)S(1)}, bf16[1040,128]{1,0:T(8,128)(2,1)S(1)}, u32[]{:S(2)}, u32[]{:S(2)}) collective-permute-start(bf16[1040,128]{1,0:T(8,128)(2,1)S(1)} %get-tuple-element.17), channel_id=1, source_target_pairs={{0,2},{1,3},{2,0},{3,1},{4,6},{5,7},{6,4},{7,5},{8,10},{9,11},{10,... | collective-permute-start | bytes 798728 | tf_op jit(solution)/shard_map/ppermute | solution.py:530
  18.1 13.9 %copy-start = (f32[8192,128]{1,0:T(8,128)}, f32[8192,128]{1,0:T(8,128)S(1)}, u32[]{:S(2)}) copy-start(f32[8192,128]{1,0:T(8,128)S(1)} %own_rows.1.begun.after) | copy-start | bytes 12582916
  32.0 5.7 %collective-permute-start.3 = (f32[4096,128]{1,0:T(8,128)S(1)}, f32[4096,128]{1,0:T(8,128)S(1)}, u32[]{:S(2)}, u32[]{:S(2)}) collective-permute-start(f32[4096,128]{1,0:T(8,128)S(1)} %get-tuple-element.21), channel_id=1, source_target_pairs={{0,4},{4,0},{1,5},{5,1},{2,6},{6,2},{3,7},{7,3},{8,12},{12,8},{9,1... | collective-permute-start | bytes 6291464 | tf_op jit(solution)/shard_map/ppermute | solution.py:530
  40.3 69.4 %copy-start.5 = (f32[2,4096]{1,0:T(2,128)S(1)}, f32[2,4096]{1,0:T(2,128)}, u32[]{:S(2)}) copy-start(f32[2,4096]{1,0:T(2,128)} %state.1) | copy-start | bytes 98308
  86.8 10.7 %collective-permute-start.12 = (s16[4,136,128]{2,1,0:T(8,128)(2,1)S(1)}, s16[4,136,128]{2,1,0:T(8,128)(2,1)S(1)}, u32[]{:S(2)}, u32[]{:S(2)}) collective-permute-start(s16[4,136,128]{2,1,0:T(8,128)(2,1)S(1)} %all_to_all.17.refs_3_), channel_id=1, source_target_pairs={{0,48},{8,56},{16,32},{24,40},{32,16},{40,24},{48,0},{56,8},{1,49}... | collective-permute-start | bytes 417800 | tf_op jit(solution)/shard_map/ppermute | solution.py:540
  88.4 10.0 %collective-permute-start.13 = (s16[4,136,128]{2,1,0:T(8,128)(2,1)S(1)}, s16[4,136,128]{2,1,0:T(8,128)(2,1)S(1)}, u32[]{:S(2)}, u32[]{:S(2)}) collective-permute-start(s16[4,136,128]{2,1,0:T(8,128)(2,1)S(1)} %all_to_all.17.refs_3_), channel_id=1, source_target_pairs={{0,16},{8,24},{16,0},{24,8},{32,48},{40,56},{48,32},{56,40},{1,17}... | collective-permute-start | bytes 417800 | tf_op jit(solution)/shard_map/ppermute | solution.py:540
  90.3 10.1 %collective-permute-start.14 = (s16[4,136,128]{2,1,0:T(8,128)(2,1)S(1)}, s16[4,136,128]{2,1,0:T(8,128)(2,1)S(1)}, u32[]{:S(2)}, u32[]{:S(2)}) collective-permute-start(s16[4,136,128]{2,1,0:T(8,128)(2,1)S(1)} %all_to_all.17.refs_3_), channel_id=1, source_target_pairs={{0,56},{8,32},{16,40},{24,48},{32,24},{40,0},{48,8},{56,16},{1,57}... | collective-permute-start | bytes 417800 | tf_op jit(solution)/shard_map/ppermute | solution.py:540
  91.7 8.8 %collective-permute-start.18 = (s16[4,136,128]{2,1,0:T(8,128)(2,1)S(1)}, s16[4,136,128]{2,1,0:T(8,128)(2,1)S(1)}, u32[]{:S(2)}, u32[]{:S(2)}) collective-permute-start(s16[4,136,128]{2,1,0:T(8,128)(2,1)S(1)} %all_to_all.17.refs_3_), channel_id=1, source_target_pairs={{0,4},{4,0},{1,5},{5,1},{2,6},{6,2},{3,7},{7,3},{8,12},{12,8},{9,1... | collective-permute-start | bytes 417800 | tf_op jit(solution)/shard_map/ppermute | solution.py:530
  96.9 7.3 %collective-permute-start.6 = (s16[4,136,128]{2,1,0:T(8,128)(2,1)S(1)}, s16[4,136,128]{2,1,0:T(8,128)(2,1)S(1)}, u32[]{:S(2)}, u32[]{:S(2)}) collective-permute-start(s16[4,136,128]{2,1,0:T(8,128)(2,1)S(1)} %all_to_all.17.refs_3_), channel_id=1, source_target_pairs={{0,24},{8,0},{16,8},{24,16},{32,56},{40,32},{48,40},{56,48},{1,25}... | collective-permute-start | bytes 417800 | tf_op jit(solution)/shard_map/ppermute | solution.py:540
  97.4 7.0 %collective-permute-start.7 = (s16[4,136,128]{2,1,0:T(8,128)(2,1)S(1)}, s16[4,136,128]{2,1,0:T(8,128)(2,1)S(1)}, u32[]{:S(2)}, u32[]{:S(2)}) collective-permute-start(s16[4,136,128]{2,1,0:T(8,128)(2,1)S(1)} %all_to_all.17.refs_3_), channel_id=1, source_target_pairs={{0,8},{8,16},{16,24},{24,0},{32,40},{40,48},{48,56},{56,32},{1,9},... | collective-permute-start | bytes 417800 | tf_op jit(solution)/shard_map/ppermute | solution.py:540
  98.4 8.4 %collective-permute-start.4 = (s16[4,136,128]{2,1,0:T(8,128)(2,1)S(1)}, s16[4,136,128]{2,1,0:T(8,128)(2,1)S(1)}, u32[]{:S(2)}, u32[]{:S(2)}) collective-permute-start(s16[4,136,128]{2,1,0:T(8,128)(2,1)S(1)} %all_to_all.17.refs_3_), channel_id=1, source_target_pairs={{0,40},{8,48},{16,56},{24,32},{32,8},{40,16},{48,24},{56,0},{1,41}... | collective-permute-start | bytes 417800 | tf_op jit(solution)/shard_map/ppermute | solution.py:540
  100.4 7.6 %collective-permute-start.5 = (s16[4,136,128]{2,1,0:T(8,128)(2,1)S(1)}, s16[4,136,128]{2,1,0:T(8,128)(2,1)S(1)}, u32[]{:S(2)}, u32[]{:S(2)}) collective-permute-start(s16[4,136,128]{2,1,0:T(8,128)(2,1)S(1)} %all_to_all.17.refs_3_), channel_id=1, source_target_pairs={{0,32},{8,40},{16,48},{24,56},{32,0},{40,8},{48,16},{56,24},{1,33}... | collective-permute-start | bytes 417800 | tf_op jit(solution)/shard_map/ppermute | solution.py:540
  100.5 8.6 %collective-permute-start.15 = (s16[4,136,128]{2,1,0:T(8,128)(2,1)S(1)}, s16[4,136,128]{2,1,0:T(8,128)(2,1)S(1)}, u32[]{:S(2)}, u32[]{:S(2)}) collective-permute-start(s16[4,136,128]{2,1,0:T(8,128)(2,1)S(1)} %collective-permute-done.12.refs_0_), channel_id=1, source_target_pairs={{0,4},{4,0},{1,5},{5,1},{2,6},{6,2},{3,7},{7,3},{8,12},{12,8},{9,1... | collective-permute-start | bytes 417800 | tf_op jit(solution)/shard_map/ppermute | solution.py:530
  104.2 4.9 %collective-permute-start.16 = (s16[4,136,128]{2,1,0:T(8,128)(2,1)S(1)}, s16[4,136,128]{2,1,0:T(8,128)(2,1)S(1)}, u32[]{:S(2)}, u32[]{:S(2)}) collective-permute-start(s16[4,136,128]{2,1,0:T(8,128)(2,1)S(1)} %collective-permute-done.13.refs_1_), channel_id=1, source_target_pairs={{0,4},{4,0},{1,5},{5,1},{2,6},{6,2},{3,7},{7,3},{8,12},{12,8},{9,1... | collective-permute-start | bytes 417800 | tf_op jit(solution)/shard_map/ppermute | solution.py:530
  104.5 10.7 %collective-permute-start.17 = (s16[4,136,128]{2,1,0:T(8,128)(2,1)S(1)}, s16[4,136,128]{2,1,0:T(8,128)(2,1)S(1)}, u32[]{:S(2)}, u32[]{:S(2)}) collective-permute-start(s16[4,136,128]{2,1,0:T(8,128)(2,1)S(1)} %collective-permute-done.14.refs_2_), channel_id=1, source_target_pairs={{0,4},{4,0},{1,5},{5,1},{2,6},{6,2},{3,7},{7,3},{8,12},{12,8},{9,1... | collective-permute-start | bytes 417800 | tf_op jit(solution)/shard_map/ppermute | solution.py:530
  106.8 12.2 %collective-permute-start.10 = (s16[4,136,128]{2,1,0:T(8,128)(2,1)S(1)}, s16[4,136,128]{2,1,0:T(8,128)(2,1)S(1)}, u32[]{:S(2)}, u32[]{:S(2)}) collective-permute-start(s16[4,136,128]{2,1,0:T(8,128)(2,1)S(1)} %collective-permute-done.6.refs_2_), channel_id=1, source_target_pairs={{0,4},{4,0},{1,5},{5,1},{2,6},{6,2},{3,7},{7,3},{8,12},{12,8},{9,1... | collective-permute-start | bytes 417800 | tf_op jit(solution)/shard_map/ppermute | solution.py:530
  108.1 10.9 %collective-permute-start.11 = (s16[4,136,128]{2,1,0:T(8,128)(2,1)S(1)}, s16[4,136,128]{2,1,0:T(8,128)(2,1)S(1)}, u32[]{:S(2)}, u32[]{:S(2)}) collective-permute-start(s16[4,136,128]{2,1,0:T(8,128)(2,1)S(1)} %collective-permute-done.7.refs_3_), channel_id=1, source_target_pairs={{0,4},{4,0},{1,5},{5,1},{2,6},{6,2},{3,7},{7,3},{8,12},{12,8},{9,1... | collective-permute-start | bytes 417800 | tf_op jit(solution)/shard_map/ppermute | solution.py:530
  109.1 9.9 %collective-permute-start.8 = (s16[4,136,128]{2,1,0:T(8,128)(2,1)S(1)}, s16[4,136,128]{2,1,0:T(8,128)(2,1)S(1)}, u32[]{:S(2)}, u32[]{:S(2)}) collective-permute-start(s16[4,136,128]{2,1,0:T(8,128)(2,1)S(1)} %collective-permute-done.4.refs_0_), channel_id=1, source_target_pairs={{0,4},{4,0},{1,5},{5,1},{2,6},{6,2},{3,7},{7,3},{8,12},{12,8},{9,1... | collective-permute-start | bytes 417800 | tf_op jit(solution)/shard_map/ppermute | solution.py:530
  109.1 9.9 %collective-permute-start.9 = (s16[4,136,128]{2,1,0:T(8,128)(2,1)S(1)}, s16[4,136,128]{2,1,0:T(8,128)(2,1)S(1)}, u32[]{:S(2)}, u32[]{:S(2)}) collective-permute-start(s16[4,136,128]{2,1,0:T(8,128)(2,1)S(1)} %collective-permute-done.5.refs_1_), channel_id=1, source_target_pairs={{0,4},{4,0},{1,5},{5,1},{2,6},{6,2},{3,7},{7,3},{8,12},{12,8},{9,1... | collective-permute-start | bytes 417800 | tf_op jit(solution)/shard_map/ppermute | solution.py:530
  109.8 2.2 %copy-start.1 = (f32[8192,128]{1,0:T(8,128)S(1)}, f32[8192,128]{1,0:T(8,128)}, u32[]{:S(2)}) copy-start(f32[8192,128]{1,0:T(8,128)} %copy-done) | copy-start | bytes 12582916
  112.0 2.2 %copy-start.2 = (f32[2,4096,128]{2,1,0:T(8,128)S(1)}, f32[2,4096,128]{2,1,0:T(8,128)}, u32[]{:S(2)}) copy-start(f32[2,4096,128]{2,1,0:T(8,128)} %rows.1) | copy-start | bytes 12582916

commit v2 on v1

--- a/solution.py
+++ b/solution.py
@@ -71,14 +71,14 @@
 
 
 def first_pick_kernel(
-    hop, unused, place, count, keys, keys_in, targets, flat, out, wide, held, kept, stage
+    hop, unused, place, keys, keys_in, targets, flat, out, wide, held, kept, stage
 ):
     chunks, owners, _ = targets.shape
     slots = lax.broadcasted_iota(jnp.int32, (chunks, LANES), 0) * LANES
     slots = slots + lax.broadcasted_iota(jnp.int32, (chunks, LANES), 1)
     kept[...] = keys_in[...]
     for owner in range(owners):
-        held[owner] = jnp.where(slots < count[0, owner], targets[:, owner, :], unused)
+        held[owner] = jnp.where(slots < place[2 + owner], targets[:, owner, :], unused)
 
     def widen(rows):
         wide[rows, :] = flat[rows, :].astype(jnp.float32)
@@ -87,7 +87,7 @@
     pick(lax.rem(place[0] + hop, owners), keys, held, wide, out, stage)
 
 
-def first_pick(hop, unused, place, count, keys, targets, flat):
+def first_pick(hop, unused, place, keys, targets, flat):
     chunks, owners, _ = keys.shape
     cap = chunks * LANES
     width = flat.shape[1]
@@ -99,13 +99,13 @@
             jax.ShapeDtypeStruct((owners, chunks, LANES), jnp.int32),
             jax.ShapeDtypeStruct(keys.shape, jnp.int32),
         ),
-        in_specs=[SM, SM, SM, VM, VM, VM],
+        in_specs=[SM, SM, VM, VM, VM],
         out_specs=(VM, VM, VM, VM),
         scratch_shapes=[pltpu.VMEM((cap, width), jnp.float32)],
         compiler_params=room(6),
         cost_estimate=cost(10**7),
         name="first_pick",
-    )(place, count, keys, keys, targets, flat)
+    )(place, keys, keys, targets, flat)
 
 
 def pick_kernel(hops, place, keys, held, wide, *refs):
@@ -319,34 +319,40 @@
     return wide_of(part[0:LANES]) * scale
 
 
-def encode_kernel(mine, got, out, peaks, shrinks):
+def encode_kernel(together, mine, got, out, peaks, shrinks):
     diag = diagonal()
     groups, blocks = out.shape[:2]
     size = blocks * LANES
 
-    def body(group, carry):
-        def block(k):
+    def body(step, carry):
+        def at(i):
+            return step * together + i // blocks, i % blocks
+
+        def block(i):
+            group, k = at(i)
             rows = pl.ds(pl.multiple_of(group * size + k * LANES, LANES), LANES)
             return mine[rows, :] + got[rows, :]
 
-        def put(k, code, tail):
+        def put(i, code, tail):
+            group, k = at(i)
             out[group, k, 0:LANES, :] = code
             out[group, k, LANES:CODED, :] = tail
 
-        encode_blocks(block, put, blocks, peaks, shrinks, diag)
+        encode_blocks(block, put, together * blocks, peaks, shrinks, diag)
         return carry
 
-    lax.fori_loop(0, groups, body, 0)
+    lax.fori_loop(0, groups // together, body, 0)
 
 
 def encode_sum(mine, got, groups):
     blocks = mine.shape[0] // (groups * LANES)
-    return pl.pallas_call(
-        encode_kernel,
+    together = 2
+    return pl.pallas_call(
+        functools.partial(encode_kernel, together),
         out_shape=jax.ShapeDtypeStruct((groups, blocks, CODED, LANES), jnp.int16),
         in_specs=[VM, VM],
         out_specs=VM,
-        scratch_shapes=[pltpu.VMEM((blocks, LANES), jnp.float32)] * 2,
+        scratch_shapes=[pltpu.VMEM((together * blocks, LANES), jnp.float32)] * 2,
         compiler_params=room(8),
         cost_estimate=cost(10**7),
         name="encode",
@@ -552,13 +558,13 @@
     row, core, pair, ring = (lax.axis_index(a) for a in ("rows", "core", "pair", "ring"))
     hops = [(0, 0), (0, 1), (0, 3), (1, 0), (1, 1), (1, 3), (0, 2), (1, 2)]
     behind = [(pair + p) % pairs * rings + (ring + rings - r) % rings for p, r in hops]
-    facts = jnp.stack([row, core, *behind]).astype(jnp.int32)
-    place, core, behind = facts[0:2], facts[1:2], facts[2:]
+    place = jnp.concatenate([jnp.stack([row, core]).astype(jnp.int32), slot_count[0]])
+    core = core.astype(jnp.int32).reshape(1)
     flat_grad = pooled_grad.reshape(-1, feature)
     keys, targets = lane_view(slot_source), lane_view(slot_target)
 
     rows = tables * rows_dev
-    first, wide, held, keys = first_pick(2, rows, place, slot_count, keys, targets, flat_grad)
+    first, wide, held, keys = first_pick(2, rows, place, keys, targets, flat_grad)
     picked = {2: first}
     picked.update(zip((1, 3), pick_rows((1, 3), place, keys, held, wide)))
     grads = []
@@ -567,7 +573,7 @@
     begun = own_rows(place, keys, held, wide, rows)
     mine, other = scatter_add(place, begun, grads)
     order = ((7, 6, 5, 0), (4, 3, 2, 1))
-    behind = jnp.stack([behind[d] for part in order for d in part])
+    behind = jnp.stack([behind[d] for part in order for d in part]).astype(jnp.int32)
     fetched = fetch(behind, table_rows, begun)
     got = shift(other, "core", 1)
     coded = encode_sum(mine, got, pairs * rings)

time: 123 us -> 122 us (level)
    unnamed x16 -> x14, local copies, waits for them, and re-layouts: 7.52 us -> 6.87 us
where the time goes in v2:
time: 122 us
  blocking collectives  44.9 us (37%)
  starting transfers between devices  30 us (25%)
  Pallas kernels  28.1 us (23%)
  waiting for transfers between devices  10.4 us (9%)
  local copies, waits for them, and re-layouts  6.95 us (6%)
    ppermute x12, starting transfers between devices, shift(): return lax.ppermute(x, axis, [(i, (i + by) % count) for i in range(count)])  21.4 us
    all_to_all x1, blocking collectives, shards(): parts = lax.all_to_all(coded, SQUARE, 0, 0, tiled=True)  20.6 us
    all_to_all x1, blocking collectives, shards(): parts = lax.all_to_all(first_sum(parts), 'far', 0, 0, tiled=True)  14.5 us
    ppermute x12, waiting for transfers between devices, shift(): return lax.ppermute(x, axis, [(i, (i + by) % count) for i in range(count)])  10.4 us
    all_to_all x1, blocking collectives, shards(): bundle = lax.all_to_all(last_sum(parts), 'far', 0, 0, tiled=True)  9.77 us
    ppermute x7, starting transfers between devices, square_shift(): return lax.ppermute(x, SQUARE, links)  8.62 us
    pallas_call x2, Pallas kernels, update(): pl.pallas_call(functools.partial(update_kernel, count), grid_spec=pltpu.P...  7.53 us
    pallas_call x1, Pallas kernels, scatter_add(): pl.pallas_call(functools.partial(scatter_kernel, cap, senders), out_shape...  7.25 us
  transfers between devices with their start and end apart: 19, of which 2 were waited for; matrix products, arithmetic and copies ran while one was open for 0% of the time, Pallas kernels for 7%

profile of v2, /device:TPU:1, one launch (start us, length us, event | category | flops | bytes accessed | tf_op | source)
XLA Modules:
  0.0 122.0 jit_solution(4852437579489090857)
XLA Ops:
  0.6 0.7 pad_add_fusion.1.place
  1.4 1.0 copy-done.3
  2.4 0.7 copy-done.4
  3.1 0.7 copy-done.6
  3.8 1.9 %first_pick.1 = (bf16[1040,128]{1,0:T(8,128)(2,1)S(1)}, f32[2048,128]{1,0:T(8,128)S(1)}, s32[4,8,128]{2,1,0:T(8,128)S(1)}, s32[8,4,128]{2,1,0:T(4,128)S(1)}) custom-call(s32[6]{0:T(128)S(1)} %pad_add_fusion.1.place, s32[8,4,128]{2,1,0:T(4,128)S(1)} %bitcast.19, s32[8,4,128]{2,1,0:T(4,128)S(1)} %bitcast.20, s32[8,4,128]{2,1,0:T(4,128)S(1)} %bitcast.21, ...), custom_call_target="tpu_custom_call" | custom-call | flops 10000000 | bytes 1000000 | tf_op jit(solution)/shard_map/first_pick/pallas_call | solution.py:94
  5.7 2.6 %pick.1 = (bf16[1040,128]{1,0:T(8,128)(2,1)S(1)}, bf16[1040,128]{1,0:T(8,128)(2,1)S(1)}) custom-call(s32[6]{0:T(128)S(1)} %pad_add_fusion.1.place, s32[8,4,128]{2,1,0:T(4,128)S(1)} %get-tuple-element.14.keys, s32[4,8,128]{2,1,0:T(8,128)S(1)} %get-tuple-element.15.held, f32[2048,128]{1,0:T(8,128)S(1)} %get-tuple-element.16.wide), custom_call_target="tpu_custom_call" | custom-call | flops 20000000 | bytes 1000000 | tf_op jit(solution)/shard_map/pick/pallas_call | solution.py:122
  8.4 2.2 %collective-permute-start.1 = (bf16[1040,128]{1,0:T(8,128)(2,1)S(1)}, bf16[1040,128]{1,0:T(8,128)(2,1)S(1)}, u32[]{:S(2)}, u32[]{:S(2)}) collective-permute-start(bf16[1040,128]{1,0:T(8,128)(2,1)S(1)} %get-tuple-element.18), channel_id=1, source_target_pairs={{0,1},{1,2},{2,3},{3,0},{4,5},{5,6},{6,7},{7,4},{8,9},{9,10},{10,1... | collective-permute-start | bytes 798728 | tf_op jit(solution)/shard_map/ppermute | solution.py:536
  10.6 1.5 %collective-permute-start.2 = (bf16[1040,128]{1,0:T(8,128)(2,1)S(1)}, bf16[1040,128]{1,0:T(8,128)(2,1)S(1)}, u32[]{:S(2)}, u32[]{:S(2)}) collective-permute-start(bf16[1040,128]{1,0:T(8,128)(2,1)S(1)} %get-tuple-element.19), channel_id=1, source_target_pairs={{0,3},{1,0},{2,1},{3,2},{4,7},{5,4},{6,5},{7,6},{8,11},{9,8},{10,9... | collective-permute-start | bytes 798728 | tf_op jit(solution)/shard_map/ppermute | solution.py:536
  12.1 1.6 %collective-permute-start = (bf16[1040,128]{1,0:T(8,128)(2,1)S(1)}, bf16[1040,128]{1,0:T(8,128)(2,1)S(1)}, u32[]{:S(2)}, u32[]{:S(2)}) collective-permute-start(bf16[1040,128]{1,0:T(8,128)(2,1)S(1)} %get-tuple-element.17), channel_id=1, source_target_pairs={{0,2},{1,3},{2,0},{3,1},{4,6},{5,7},{6,4},{7,5},{8,10},{9,11},{10,... | collective-permute-start | bytes 798728 | tf_op jit(solution)/shard_map/ppermute | solution.py:536
  13.6 4.5 %own_rows.1.begun.after = f32[8192,128]{1,0:T(8,128)S(1)} custom-call(s32[6]{0:T(128)S(1)} %pad_add_fusion.1.place, s32[8,4,128]{2,1,0:T(4,128)S(1)} %get-tuple-element.14.keys, s32[4,8,128]{2,1,0:T(8,128)S(1)} %get-tuple-element.15.held, f32[2048,128]{1,0:T(8,128)S(1)} %get-tuple-element.16.wide), custom_call_target="tpu_custom_call" | custom-call | flops 10000000 | bytes 1000000 | tf_op jit(solution)/shard_map/own_rows/pallas_call | solution.py:246
  18.1 0.0 copy-start
  18.1 0.0 collective-permute-done.1.refs_1_
  18.1 6.6 %collective-permute-done.refs_0_ = bf16[1040,128]{1,0:T(8,128)(2,1)S(1)} collective-permute-done((bf16[1040,128]{1,0:T(8,128)(2,1)S(1)}, bf16[1040,128]{1,0:T(8,128)(2,1)S(1)}, u32[]{:S(2)}, u32[]{:S(2)}) %collective-permute-start) | collective-permute-done | bytes 266272 | tf_op jit(solution)/shard_map/ppermute | solution.py:536
  24.7 7.3 %scatter.1 = (f32[4096,128]{1,0:T(8,128)S(1)}, f32[4096,128]{1,0:T(8,128)S(1)}) custom-call(s32[6]{0:T(128)S(1)} %pad_add_fusion.1.place, f32[8192,128]{1,0:T(8,128)S(1)} %own_rows.1.begun.after, bf16[1040,128]{1,0:T(8,128)(2,1)S(1)} %collective-permute-done.refs_0_, bf16[1040,128]{1,0:T(8,128)(2,1)S(1)} %collective-permute-done.1.refs_1_, ...), custom_call_target="tpu_custom_call" | custom-call | flops 100000000 | bytes 1000000 | tf_op jit(solution)/shard_map/scatter/pallas_call | solution.py:264
  32.0 1.9 %collective-permute-start.3 = (f32[4096,128]{1,0:T(8,128)S(1)}, f32[4096,128]{1,0:T(8,128)S(1)}, u32[]{:S(2)}, u32[]{:S(2)}) collective-permute-start(f32[4096,128]{1,0:T(8,128)S(1)} %get-tuple-element.21), channel_id=1, source_target_pairs={{0,4},{4,0},{1,5},{5,1},{2,6},{6,2},{3,7},{7,3},{8,12},{12,8},{9,1... | collective-permute-start | bytes 6291464 | tf_op jit(solution)/shard_map/ppermute | solution.py:536
  33.8 3.8 %collective-permute-done.3.got = f32[4096,128]{1,0:T(8,128)S(1)} collective-permute-done((f32[4096,128]{1,0:T(8,128)S(1)}, f32[4096,128]{1,0:T(8,128)S(1)}, u32[]{:S(2)}, u32[]{:S(2)}) %collective-permute-start.3) | collective-permute-done | bytes 2097184 | tf_op jit(solution)/shard_map/ppermute | solution.py:536
  37.6 1.9 %encode.1 = s16[8,4,136,128]{3,2,1,0:T(8,128)(2,1)S(1)} custom-call(f32[4096,128]{1,0:T(8,128)S(1)} %get-tuple-element.20.mine, f32[4096,128]{1,0:T(8,128)S(1)} %collective-permute-done.3.got), custom_call_target="tpu_custom_call" | custom-call | flops 10000000 | bytes 1000000 | tf_op jit(solution)/shard_map/encode/pallas_call | solution.py:350
  39.5 0.0 copy-start.5
  39.5 20.6 %all_to_all.15.parts = s16[8,4,136,128]{3,2,1,0:T(8,128)(2,1)S(1)} all-to-all(s16[8,4,136,128]{3,2,1,0:T(8,128)(2,1)S(1)} %encode.1), channel_id=1, replica_groups=mesh['far'=4,'pair'=2,'ring'=4,'core'=2,'rows'=4] {'pair','ring'}, dimensions={0} | all-to-all | bytes 2228224 | tf_op jit(solution)/shard_map/all_to_all | solution.py:580
  60.1 1.2 first_sum.1
  61.3 14.5 %all_to_all.16.parts = s16[4,136,128]{2,1,0:T(8,128)(2,1)S(1)} all-to-all(s16[4,136,128]{2,1,0:T(8,128)(2,1)S(1)} %first_sum.1), channel_id=1, replica_groups=mesh['far'=4,'pair'=2,'ring'=4,'core'=2,'rows'=4] {'far'}, dimensions={0} | all-to-all | bytes 278528 | tf_op jit(solution)/shard_map/all_to_all | solution.py:581
  75.8 0.4 last_sum.1
  76.2 9.8 %all_to_all.17.refs_3_ = s16[4,136,128]{2,1,0:T(8,128)(2,1)S(1)} all-to-all(s16[4,136,128]{2,1,0:T(8,128)(2,1)S(1)} %last_sum.1), channel_id=1, replica_groups=mesh['far'=4,'pair'=2,'ring'=4,'core'=2,'rows'=4] {'far'}, dimensions={0} | all-to-all | bytes 278528 | tf_op jit(solution)/shard_map/all_to_all | solution.py:582
  86.0 1.6 %collective-permute-start.12 = (s16[4,136,128]{2,1,0:T(8,128)(2,1)S(1)}, s16[4,136,128]{2,1,0:T(8,128)(2,1)S(1)}, u32[]{:S(2)}, u32[]{:S(2)}) collective-permute-start(s16[4,136,128]{2,1,0:T(8,128)(2,1)S(1)} %all_to_all.17.refs_3_), channel_id=1, source_target_pairs={{0,48},{8,56},{16,32},{24,40},{32,16},{40,24},{48,0},{56,8},{1,49}... | collective-permute-start | bytes 417800 | tf_op jit(solution)/shard_map/ppermute | solution.py:546
  87.6 1.9 %collective-permute-start.13 = (s16[4,136,128]{2,1,0:T(8,128)(2,1)S(1)}, s16[4,136,128]{2,1,0:T(8,128)(2,1)S(1)}, u32[]{:S(2)}, u32[]{:S(2)}) collective-permute-start(s16[4,136,128]{2,1,0:T(8,128)(2,1)S(1)} %all_to_all.17.refs_3_), channel_id=1, source_target_pairs={{0,16},{8,24},{16,0},{24,8},{32,48},{40,56},{48,32},{56,40},{1,17}... | collective-permute-start | bytes 417800 | tf_op jit(solution)/shard_map/ppermute | solution.py:546
  89.5 1.4 %collective-permute-start.14 = (s16[4,136,128]{2,1,0:T(8,128)(2,1)S(1)}, s16[4,136,128]{2,1,0:T(8,128)(2,1)S(1)}, u32[]{:S(2)}, u32[]{:S(2)}) collective-permute-start(s16[4,136,128]{2,1,0:T(8,128)(2,1)S(1)} %all_to_all.17.refs_3_), channel_id=1, source_target_pairs={{0,56},{8,32},{16,40},{24,48},{32,24},{40,0},{48,8},{56,16},{1,57}... | collective-permute-start | bytes 417800 | tf_op jit(solution)/shard_map/ppermute | solution.py:546
  91.0 5.1 %collective-permute-start.18 = (s16[4,136,128]{2,1,0:T(8,128)(2,1)S(1)}, s16[4,136,128]{2,1,0:T(8,128)(2,1)S(1)}, u32[]{:S(2)}, u32[]{:S(2)}) collective-permute-start(s16[4,136,128]{2,1,0:T(8,128)(2,1)S(1)} %all_to_all.17.refs_3_), channel_id=1, source_target_pairs={{0,4},{4,0},{1,5},{5,1},{2,6},{6,2},{3,7},{7,3},{8,12},{12,8},{9,1... | collective-permute-start | bytes 417800 | tf_op jit(solution)/shard_map/ppermute | solution.py:536
  96.1 0.5 collective-permute-start.6
  96.6 0.0 collective-permute-done.12.refs_0_
  96.6 0.9 collective-permute-start.7
  97.6 2.1 %collective-permute-start.4 = (s16[4,136,128]{2,1,0:T(8,128)(2,1)S(1)}, s16[4,136,128]{2,1,0:T(8,128)(2,1)S(1)}, u32[]{:S(2)}, u32[]{:S(2)}) collective-permute-start(s16[4,136,128]{2,1,0:T(8,128)(2,1)S(1)} %all_to_all.17.refs_3_), channel_id=1, source_target_pairs={{0,40},{8,48},{16,56},{24,32},{32,8},{40,16},{48,24},{56,0},{1,41}... | collective-permute-start | bytes 417800 | tf_op jit(solution)/shard_map/ppermute | solution.py:546
  99.6 0.0 collective-permute-done.14.refs_2_
  99.6 0.1 collective-permute-start.5
  99.8 3.7 %collective-permute-start.15 = (s16[4,136,128]{2,1,0:T(8,128)(2,1)S(1)}, s16[4,136,128]{2,1,0:T(8,128)(2,1)S(1)}, u32[]{:S(2)}, u32[]{:S(2)}) collective-permute-start(s16[4,136,128]{2,1,0:T(8,128)(2,1)S(1)} %collective-permute-done.12.refs_0_), channel_id=1, source_target_pairs={{0,4},{4,0},{1,5},{5,1},{2,6},{6,2},{3,7},{7,3},{8,12},{12,8},{9,1... | collective-permute-start | bytes 417800 | tf_op jit(solution)/shard_map/ppermute | solution.py:536
  103.4 0.3 collective-permute-start.16
  103.7 2.3 %collective-permute-start.17 = (s16[4,136,128]{2,1,0:T(8,128)(2,1)S(1)}, s16[4,136,128]{2,1,0:T(8,128)(2,1)S(1)}, u32[]{:S(2)}, u32[]{:S(2)}) collective-permute-start(s16[4,136,128]{2,1,0:T(8,128)(2,1)S(1)} %collective-permute-done.14.refs_2_), channel_id=1, source_target_pairs={{0,4},{4,0},{1,5},{5,1},{2,6},{6,2},{3,7},{7,3},{8,12},{12,8},{9,1... | collective-permute-start | bytes 417800 | tf_op jit(solution)/shard_map/ppermute | solution.py:536
  106.0 1.3 %collective-permute-start.10 = (s16[4,136,128]{2,1,0:T(8,128)(2,1)S(1)}, s16[4,136,128]{2,1,0:T(8,128)(2,1)S(1)}, u32[]{:S(2)}, u32[]{:S(2)}) collective-permute-start(s16[4,136,128]{2,1,0:T(8,128)(2,1)S(1)} %collective-permute-done.6.refs_2_), channel_id=1, source_target_pairs={{0,4},{4,0},{1,5},{5,1},{2,6},{6,2},{3,7},{7,3},{8,12},{12,8},{9,1... | collective-permute-start | bytes 417800 | tf_op jit(solution)/shard_map/ppermute | solution.py:536
  107.3 1.1 collective-permute-start.11
  108.4 0.0 collective-permute-start.8
  108.4 0.5 collective-permute-start.9
  108.9 0.1 pad_add_fusion.2.groups
  109.0 0.1 stack.45.groups
  109.0 2.2 %copy-done.1 = f32[8192,128]{1,0:T(8,128)S(1)} copy-done((f32[8192,128]{1,0:T(8,128)S(1)}, f32[8192,128]{1,0:T(8,128)}, u32[]{:S(2)}) %copy-start.1) | copy-done | bytes 4194328
  111.2 2.2 %copy-done.2 = f32[2,4096,128]{2,1,0:T(8,128)S(1)} copy-done((f32[2,4096,128]{2,1,0:T(8,128)S(1)}, f32[2,4096,128]{2,1,0:T(8,128)}, u32[]{:S(2)}) %copy-start.2) | copy-done | bytes 4194328
  113.4 0.9 fetch.1
  114.3 0.1 pad_add_fusion.groups
  114.4 3.8 %update.2 = (f32[2,4096,128]{2,1,0:T(8,128)}, f32[2,4096]{1,0:T(2,128)}) custom-call(s32[4]{0:T(128)S(1)} %pad_add_fusion.2.groups, s32[1]{0:T(128)} %bitcast.4.core, s16[4,136,128]{2,1,0:T(8,128)(2,1)S(1)} %collective-permute-done.12.refs_0_, s16[4,136,128]{2,1,0:T(8,128)(2,1)S(1)} %collective-permute-done.13.refs_1_, ...), custom_call_target="tpu_custom_call" | custom-call | flops 10000000 | bytes 1000000 | tf_op jit(solution)/shard_map/update/pallas_call | solution.py:464
  118.2 3.8 %update.3 = (f32[2,4096,128]{2,1,0:T(8,128)}, f32[2,4096]{1,0:T(2,128)}) custom-call(s32[4]{0:T(128)S(1)} %pad_add_fusion.groups, s32[1]{0:T(128)} %bitcast.4.core, s16[4,136,128]{2,1,0:T(8,128)(2,1)S(1)} %collective-permute-done.4.refs_0_, s16[4,136,128]{2,1,0:T(8,128)(2,1)S(1)} %collective-permute-done.5.refs_1_, ...), custom_call_target="tpu_custom_call", output_to_operand_aliasing={{0}: (12, {}), {1}: (13, {})} | custom-call | flops 10000000 | bytes 1000000 | tf_op jit(solution)/shard_map/update/pallas_call | solution.py:464
  (22 shorter events, 0.1 us)
Async XLA Ops:
  1.4 1.0 copy-start.3
  2.4 0.7 copy-start.4
  3.1 0.7 copy-start.6
  8.4 9.8 %collective-permute-start.1 = (bf16[1040,128]{1,0:T(8,128)(2,1)S(1)}, bf16[1040,128]{1,0:T(8,128)(2,1)S(1)}, u32[]{:S(2)}, u32[]{:S(2)}) collective-permute-start(bf16[1040,128]{1,0:T(8,128)(2,1)S(1)} %get-tuple-element.18), channel_id=1, source_target_pairs={{0,1},{1,2},{2,3},{3,0},{4,5},{5,6},{6,7},{7,4},{8,9},{9,10},{10,1... | collective-permute-start | bytes 798728 | tf_op jit(solution)/shard_map/ppermute | solution.py:536
  10.6 7.6 %collective-permute-start.2 = (bf16[1040,128]{1,0:T(8,128)(2,1)S(1)}, bf16[1040,128]{1,0:T(8,128)(2,1)S(1)}, u32[]{:S(2)}, u32[]{:S(2)}) collective-permute-start(bf16[1040,128]{1,0:T(8,128)(2,1)S(1)} %get-tuple-element.19), channel_id=1, source_target_pairs={{0,3},{1,0},{2,1},{3,2},{4,7},{5,4},{6,5},{7,6},{8,11},{9,8},{10,9... | collective-permute-start | bytes 798728 | tf_op jit(solution)/shard_map/ppermute | solution.py:536
  12.1 12.6 %collective-permute-start = (bf16[1040,128]{1,0:T(8,128)(2,1)S(1)}, bf16[1040,128]{1,0:T(8,128)(2,1)S(1)}, u32[]{:S(2)}, u32[]{:S(2)}) collective-permute-start(bf16[1040,128]{1,0:T(8,128)(2,1)S(1)} %get-tuple-element.17), channel_id=1, source_target_pairs={{0,2},{1,3},{2,0},{3,1},{4,6},{5,7},{6,4},{7,5},{8,10},{9,11},{10,... | collective-permute-start | bytes 798728 | tf_op jit(solution)/shard_map/ppermute | solution.py:536
  18.1 13.9 %copy-start = (f32[8192,128]{1,0:T(8,128)}, f32[8192,128]{1,0:T(8,128)S(1)}, u32[]{:S(2)}) copy-start(f32[8192,128]{1,0:T(8,128)S(1)} %own_rows.1.begun.after) | copy-start | bytes 12582916
  32.0 5.7 %collective-permute-start.3 = (f32[4096,128]{1,0:T(8,128)S(1)}, f32[4096,128]{1,0:T(8,128)S(1)}, u32[]{:S(2)}, u32[]{:S(2)}) collective-permute-start(f32[4096,128]{1,0:T(8,128)S(1)} %get-tuple-element.21), channel_id=1, source_target_pairs={{0,4},{4,0},{1,5},{5,1},{2,6},{6,2},{3,7},{7,3},{8,12},{12,8},{9,1... | collective-permute-start | bytes 6291464 | tf_op jit(solution)/shard_map/ppermute | solution.py:536
  39.5 69.4 %copy-start.5 = (f32[2,4096]{1,0:T(2,128)S(1)}, f32[2,4096]{1,0:T(2,128)}, u32[]{:S(2)}) copy-start(f32[2,4096]{1,0:T(2,128)} %state.1) | copy-start | bytes 98308
  86.0 10.7 %collective-permute-start.12 = (s16[4,136,128]{2,1,0:T(8,128)(2,1)S(1)}, s16[4,136,128]{2,1,0:T(8,128)(2,1)S(1)}, u32[]{:S(2)}, u32[]{:S(2)}) collective-permute-start(s16[4,136,128]{2,1,0:T(8,128)(2,1)S(1)} %all_to_all.17.refs_3_), channel_id=1, source_target_pairs={{0,48},{8,56},{16,32},{24,40},{32,16},{40,24},{48,0},{56,8},{1,49}... | collective-permute-start | bytes 417800 | tf_op jit(solution)/shard_map/ppermute | solution.py:546
  87.6 10.0 %collective-permute-start.13 = (s16[4,136,128]{2,1,0:T(8,128)(2,1)S(1)}, s16[4,136,128]{2,1,0:T(8,128)(2,1)S(1)}, u32[]{:S(2)}, u32[]{:S(2)}) collective-permute-start(s16[4,136,128]{2,1,0:T(8,128)(2,1)S(1)} %all_to_all.17.refs_3_), channel_id=1, source_target_pairs={{0,16},{8,24},{16,0},{24,8},{32,48},{40,56},{48,32},{56,40},{1,17}... | collective-permute-start | bytes 417800 | tf_op jit(solution)/shard_map/ppermute | solution.py:546
  89.5 10.1 %collective-permute-start.14 = (s16[4,136,128]{2,1,0:T(8,128)(2,1)S(1)}, s16[4,136,128]{2,1,0:T(8,128)(2,1)S(1)}, u32[]{:S(2)}, u32[]{:S(2)}) collective-permute-start(s16[4,136,128]{2,1,0:T(8,128)(2,1)S(1)} %all_to_all.17.refs_3_), channel_id=1, source_target_pairs={{0,56},{8,32},{16,40},{24,48},{32,24},{40,0},{48,8},{56,16},{1,57}... | collective-permute-start | bytes 417800 | tf_op jit(solution)/shard_map/ppermute | solution.py:546
  91.0 8.8 %collective-permute-start.18 = (s16[4,136,128]{2,1,0:T(8,128)(2,1)S(1)}, s16[4,136,128]{2,1,0:T(8,128)(2,1)S(1)}, u32[]{:S(2)}, u32[]{:S(2)}) collective-permute-start(s16[4,136,128]{2,1,0:T(8,128)(2,1)S(1)} %all_to_all.17.refs_3_), channel_id=1, source_target_pairs={{0,4},{4,0},{1,5},{5,1},{2,6},{6,2},{3,7},{7,3},{8,12},{12,8},{9,1... | collective-permute-start | bytes 417800 | tf_op jit(solution)/shard_map/ppermute | solution.py:536
  96.1 7.3 %collective-permute-start.6 = (s16[4,136,128]{2,1,0:T(8,128)(2,1)S(1)}, s16[4,136,128]{2,1,0:T(8,128)(2,1)S(1)}, u32[]{:S(2)}, u32[]{:S(2)}) collective-permute-start(s16[4,136,128]{2,1,0:T(8,128)(2,1)S(1)} %all_to_all.17.refs_3_), channel_id=1, source_target_pairs={{0,24},{8,0},{16,8},{24,16},{32,56},{40,32},{48,40},{56,48},{1,25}... | collective-permute-start | bytes 417800 | tf_op jit(solution)/shard_map/ppermute | solution.py:546
  96.6 7.0 %collective-permute-start.7 = (s16[4,136,128]{2,1,0:T(8,128)(2,1)S(1)}, s16[4,136,128]{2,1,0:T(8,128)(2,1)S(1)}, u32[]{:S(2)}, u32[]{:S(2)}) collective-permute-start(s16[4,136,128]{2,1,0:T(8,128)(2,1)S(1)} %all_to_all.17.refs_3_), channel_id=1, source_target_pairs={{0,8},{8,16},{16,24},{24,0},{32,40},{40,48},{48,56},{56,32},{1,9},... | collective-permute-start | bytes 417800 | tf_op jit(solution)/shard_map/ppermute | solution.py:546
  97.6 8.4 %collective-permute-start.4 = (s16[4,136,128]{2,1,0:T(8,128)(2,1)S(1)}, s16[4,136,128]{2,1,0:T(8,128)(2,1)S(1)}, u32[]{:S(2)}, u32[]{:S(2)}) collective-permute-start(s16[4,136,128]{2,1,0:T(8,128)(2,1)S(1)} %all_to_all.17.refs_3_), channel_id=1, source_target_pairs={{0,40},{8,48},{16,56},{24,32},{32,8},{40,16},{48,24},{56,0},{1,41}... | collective-permute-start | bytes 417800 | tf_op jit(solution)/shard_map/ppermute | solution.py:546
  99.6 7.6 %collective-permute-start.5 = (s16[4,136,128]{2,1,0:T(8,128)(2,1)S(1)}, s16[4,136,128]{2,1,0:T(8,128)(2,1)S(1)}, u32[]{:S(2)}, u32[]{:S(2)}) collective-permute-start(s16[4,136,128]{2,1,0:T(8,128)(2,1)S(1)} %all_to_all.17.refs_3_), channel_id=1, source_target_pairs={{0,32},{8,40},{16,48},{24,56},{32,0},{40,8},{48,16},{56,24},{1,33}... | collective-permute-start | bytes 417800 | tf_op jit(solution)/shard_map/ppermute | solution.py:546
  99.8 8.6 %collective-permute-start.15 = (s16[4,136,128]{2,1,0:T(8,128)(2,1)S(1)}, s16[4,136,128]{2,1,0:T(8,128)(2,1)S(1)}, u32[]{:S(2)}, u32[]{:S(2)}) collective-permute-start(s16[4,136,128]{2,1,0:T(8,128)(2,1)S(1)} %collective-permute-done.12.refs_0_), channel_id=1, source_target_pairs={{0,4},{4,0},{1,5},{5,1},{2,6},{6,2},{3,7},{7,3},{8,12},{12,8},{9,1... | collective-permute-start | bytes 417800 | tf_op jit(solution)/shard_map/ppermute | solution.py:536
  103.4 4.9 %collective-permute-start.16 = (s16[4,136,128]{2,1,0:T(8,128)(2,1)S(1)}, s16[4,136,128]{2,1,0:T(8,128)(2,1)S(1)}, u32[]{:S(2)}, u32[]{:S(2)}) collective-permute-start(s16[4,136,128]{2,1,0:T(8,128)(2,1)S(1)} %collective-permute-done.13.refs_1_), channel_id=1, source_target_pairs={{0,4},{4,0},{1,5},{5,1},{2,6},{6,2},{3,7},{7,3},{8,12},{12,8},{9,1... | collective-permute-start | bytes 417800 | tf_op jit(solution)/shard_map/ppermute | solution.py:536
  103.7 10.7 %collective-permute-start.17 = (s16[4,136,128]{2,1,0:T(8,128)(2,1)S(1)}, s16[4,136,128]{2,1,0:T(8,128)(2,1)S(1)}, u32[]{:S(2)}, u32[]{:S(2)}) collective-permute-start(s16[4,136,128]{2,1,0:T(8,128)(2,1)S(1)} %collective-permute-done.14.refs_2_), channel_id=1, source_target_pairs={{0,4},{4,0},{1,5},{5,1},{2,6},{6,2},{3,7},{7,3},{8,12},{12,8},{9,1... | collective-permute-start | bytes 417800 | tf_op jit(solution)/shard_map/ppermute | solution.py:536
  106.0 12.2 %collective-permute-start.10 = (s16[4,136,128]{2,1,0:T(8,128)(2,1)S(1)}, s16[4,136,128]{2,1,0:T(8,128)(2,1)S(1)}, u32[]{:S(2)}, u32[]{:S(2)}) collective-permute-start(s16[4,136,128]{2,1,0:T(8,128)(2,1)S(1)} %collective-permute-done.6.refs_2_), channel_id=1, source_target_pairs={{0,4},{4,0},{1,5},{5,1},{2,6},{6,2},{3,7},{7,3},{8,12},{12,8},{9,1... | collective-permute-start | bytes 417800 | tf_op jit(solution)/shard_map/ppermute | solution.py:536
  107.3 10.9 %collective-permute-start.11 = (s16[4,136,128]{2,1,0:T(8,128)(2,1)S(1)}, s16[4,136,128]{2,1,0:T(8,128)(2,1)S(1)}, u32[]{:S(2)}, u32[]{:S(2)}) collective-permute-start(s16[4,136,128]{2,1,0:T(8,128)(2,1)S(1)} %collective-permute-done.7.refs_3_), channel_id=1, source_target_pairs={{0,4},{4,0},{1,5},{5,1},{2,6},{6,2},{3,7},{7,3},{8,12},{12,8},{9,1... | collective-permute-start | bytes 417800 | tf_op jit(solution)/shard_map/ppermute | solution.py:536
  108.4 9.9 %collective-permute-start.8 = (s16[4,136,128]{2,1,0:T(8,128)(2,1)S(1)}, s16[4,136,128]{2,1,0:T(8,128)(2,1)S(1)}, u32[]{:S(2)}, u32[]{:S(2)}) collective-permute-start(s16[4,136,128]{2,1,0:T(8,128)(2,1)S(1)} %collective-permute-done.4.refs_0_), channel_id=1, source_target_pairs={{0,4},{4,0},{1,5},{5,1},{2,6},{6,2},{3,7},{7,3},{8,12},{12,8},{9,1... | collective-permute-start | bytes 417800 | tf_op jit(solution)/shard_map/ppermute | solution.py:536
  108.4 9.9 %collective-permute-start.9 = (s16[4,136,128]{2,1,0:T(8,128)(2,1)S(1)}, s16[4,136,128]{2,1,0:T(8,128)(2,1)S(1)}, u32[]{:S(2)}, u32[]{:S(2)}) collective-permute-start(s16[4,136,128]{2,1,0:T(8,128)(2,1)S(1)} %collective-permute-done.5.refs_1_), channel_id=1, source_target_pairs={{0,4},{4,0},{1,5},{5,1},{2,6},{6,2},{3,7},{7,3},{8,12},{12,8},{9,1... | collective-permute-start | bytes 417800 | tf_op jit(solution)/shard_map/ppermute | solution.py:536
  109.0 2.2 %copy-start.1 = (f32[8192,128]{1,0:T(8,128)S(1)}, f32[8192,128]{1,0:T(8,128)}, u32[]{:S(2)}) copy-start(f32[8192,128]{1,0:T(8,128)} %copy-done) | copy-start | bytes 12582916
  111.2 2.2 %copy-start.2 = (f32[2,4096,128]{2,1,0:T(8,128)S(1)}, f32[2,4096,128]{2,1,0:T(8,128)}, u32[]{:S(2)}) copy-start(f32[2,4096,128]{2,1,0:T(8,128)} %rows.1) | copy-start | bytes 12582916

commit v3 on v2

--- a/solution.py
+++ b/solution.py
@@ -319,54 +319,52 @@
     return wide_of(part[0:LANES]) * scale
 
 
-def encode_kernel(together, mine, got, out, peaks, shrinks):
+def encode_kernel(offset, targets, mine, got, *refs):
+    outs, (peaks, shrinks) = refs[:-2], refs[-2:]
     diag = diagonal()
-    groups, blocks = out.shape[:2]
+    blocks = outs[0].shape[0]
+    together = peaks.shape[0] // blocks
     size = blocks * LANES
-
-    def body(step, carry):
-        def at(i):
-            return step * together + i // blocks, i % blocks
-
-        def block(i):
-            group, k = at(i)
-            rows = pl.ds(pl.multiple_of(group * size + k * LANES, LANES), LANES)
+    for low in range(0, len(outs), together):
+        some = outs[low : low + together]
+
+        def block(i, low=low):
+            first = targets[offset + low + i // blocks] * size + i % blocks * LANES
+            rows = pl.ds(pl.multiple_of(first, LANES), LANES)
             return mine[rows, :] + got[rows, :]
 
-        def put(i, code, tail):
-            group, k = at(i)
-            out[group, k, 0:LANES, :] = code
-            out[group, k, LANES:CODED, :] = tail
-
-        encode_blocks(block, put, together * blocks, peaks, shrinks, diag)
-        return carry
-
-    lax.fori_loop(0, groups // together, body, 0)
-
-
-def encode_sum(mine, got, groups):
+        def put(i, code, tail, some=some):
+            out, k = some[i // blocks], i % blocks
+            out[k, 0:LANES, :] = code
+            out[k, LANES:CODED, :] = tail
+
+        encode_blocks(block, put, len(some) * blocks, peaks, shrinks, diag)
+
+
+def encode_sum(offset, count, targets, mine, got, groups):
     blocks = mine.shape[0] // (groups * LANES)
-    together = 2
-    return pl.pallas_call(
-        functools.partial(encode_kernel, together),
-        out_shape=jax.ShapeDtypeStruct((groups, blocks, CODED, LANES), jnp.int16),
-        in_specs=[VM, VM],
-        out_specs=VM,
-        scratch_shapes=[pltpu.VMEM((together * blocks, LANES), jnp.float32)] * 2,
+    shape = jax.ShapeDtypeStruct((blocks, CODED, LANES), jnp.int16)
+    return pl.pallas_call(
+        functools.partial(encode_kernel, offset),
+        out_shape=(shape,) * count,
+        in_specs=[SM, VM, VM],
+        out_specs=(VM,) * count,
+        scratch_shapes=[pltpu.VMEM((2 * blocks, LANES), jnp.float32)] * 2,
         compiler_params=room(8),
         cost_estimate=cost(10**7),
         name="encode",
-    )(mine, got)
-
-
-def first_sum_kernel(parts, out, totals, peaks, shrinks):
+    )(targets, mine, got)
+
+
+def first_sum_kernel(*refs):
+    parts, (out, totals, peaks, shrinks) = refs[:-4], refs[-4:]
     diag = diagonal()
-    groups, blocks = parts.shape[:2]
+    blocks = out.shape[0]
 
     def body(k, carry):
-        total = decode(parts[0, k], diag)
-        for j in range(1, groups):
-            total = total + decode(parts[j, k], diag)
+        total = decode(parts[0][k], diag)
+        for part in parts[1:]:
+            total = total + decode(part[k], diag)
         totals[k] = total
         return carry
 
@@ -380,18 +378,18 @@
 
 
 def first_sum(parts):
-    blocks = parts.shape[1]
+    blocks = parts[0].shape[0]
     return pl.pallas_call(
         first_sum_kernel,
-        out_shape=jax.ShapeDtypeStruct(parts.shape[1:], jnp.int16),
-        in_specs=[VM],
+        out_shape=jax.ShapeDtypeStruct(parts[0].shape, jnp.int16),
+        in_specs=[VM] * len(parts),
         out_specs=VM,
         scratch_shapes=[pltpu.VMEM((blocks, LANES, LANES), jnp.float32)]
         + [pltpu.VMEM((blocks, LANES), jnp.float32)] * 2,
         compiler_params=room(6),
         cost_estimate=cost(10**7),
         name="first_sum",
-    )(parts)
+    )(*parts)
 
 
 def last_sum_kernel(parts, out):
@@ -419,7 +417,7 @@
     )(parts)
 
 
-def update_kernel(count, groups, core, *refs):
+def update_kernel(count, offset, groups, core, *refs):
     mine, got = refs[:count], refs[count : 2 * count]
     rows, state = refs[2 * count : 2 * count + 2]
     new_rows, new_state, held, sums, scales = refs[-5:]
@@ -434,7 +432,7 @@
             held[1 - core[0]] = got[d][...]
 
     diag = diagonal()
-    start = groups[step] * size
+    start = groups[offset + step] * size
     every = [(table, k) for table in range(tables) for k in range(blocks)]
     for at, (table, k) in enumerate(every):
         code = wide_of(held[table, k, 0:LANES, :])
@@ -455,14 +453,14 @@
         new_rows[table, there, :] = rows[step, table, there, :] - move
 
 
-def update(groups, core, mine, got, rows, state, earlier):
+def update(offset, groups, core, mine, got, rows, state, earlier):
     count, tables, size, width = rows.shape
     blocks = mine[0].shape[0]
-    row_spec = pl.BlockSpec((tables, size, width), lambda i, g, c: (0, g[i], 0))
-    state_spec = pl.BlockSpec((tables, size), lambda i, g, c: (0, g[i]))
+    row_spec = pl.BlockSpec((tables, size, width), lambda i, g, c: (0, g[offset + i], 0))
+    state_spec = pl.BlockSpec((tables, size), lambda i, g, c: (0, g[offset + i]))
     first = 2 + 2 * count + 2
     return pl.pallas_call(
-        functools.partial(update_kernel, count),
+        functools.partial(update_kernel, count, offset),
         grid_spec=pltpu.PrefetchScalarGridSpec(
             num_scalar_prefetch=2,
             grid=(count,),
@@ -486,11 +484,11 @@
 
 def fetch_kernel(groups, rows, after, *refs):
     outs, sems = refs[:-1], refs[-1]
-    count, _, size, _ = outs[0].shape
+    size = outs[0].shape[2]
     copies = []
-    for i, out in enumerate(outs):
-        for d in range(count):
-            at = i * count + d
+    for out in outs:
+        for d in range(out.shape[0]):
+            at = len(copies)
             there = pl.ds(pl.multiple_of(groups[at] * size, size), size)
             copies.append(pltpu.make_async_copy(rows.at[:, there, :], out.at[d], sems.at[at]))
     for copy in copies:
@@ -499,13 +497,15 @@
         copy.wait()
 
 
-def fetch(groups, rows, after):
+def fetch(groups, split, count, rows, after):
     tables, rows_dev, width = rows.shape
-    count = groups.shape[0]
-    shape = jax.ShapeDtypeStruct((count // 2, tables, rows_dev // count, width), rows.dtype)
+    shapes = [
+        jax.ShapeDtypeStruct((size, tables, rows_dev // count, width), rows.dtype)
+        for size in (split, count - split)
+    ]
     return pl.pallas_call(
         fetch_kernel,
-        out_shape=(shape, shape),
+        out_shape=shapes,
         in_specs=[SM, HB, HB],
         out_specs=(VM, VM),
         scratch_shapes=[pltpu.SemaphoreType.DMA((count,))],
@@ -558,6 +558,11 @@
     row, core, pair, ring = (lax.axis_index(a) for a in ("rows", "core", "pair", "ring"))
     hops = [(0, 0), (0, 1), (0, 3), (1, 0), (1, 1), (1, 3), (0, 2), (1, 2)]
     behind = [(pair + p) % pairs * rings + (ring + rings - r) % rings for p, r in hops]
+    ahead = [(pair + p) % pairs * rings + (ring + r) % rings for p, r in hops]
+    order = ((7, 6, 5, 2, 0), (1, 4, 3))
+    sends = ((7, 6, 5), (2, 1, 4, 3, 0))
+    facts = [behind[d] for part in order for d in part]
+    facts = jnp.stack(facts + [ahead[d] for part in sends for d in part]).astype(jnp.int32)
     place = jnp.concatenate([jnp.stack([row, core]).astype(jnp.int32), slot_count[0]])
     core = core.astype(jnp.int32).reshape(1)
     flat_grad = pooled_grad.reshape(-1, feature)
@@ -572,12 +577,15 @@
         grads.append(shift(block, "rows", hop))
     begun = own_rows(place, keys, held, wide, rows)
     mine, other = scatter_add(place, begun, grads)
-    order = ((7, 6, 5, 0), (4, 3, 2, 1))
-    behind = jnp.stack([behind[d] for part in order for d in part]).astype(jnp.int32)
-    fetched = fetch(behind, table_rows, begun)
+    fetched = fetch(facts, len(order[0]), len(hops), table_rows, begun)
     got = shift(other, "core", 1)
-    coded = encode_sum(mine, got, pairs * rings)
-    parts = lax.all_to_all(coded, SQUARE, 0, 0, tiled=True)
+    parts = [None] * len(hops)
+    offset = len(hops)
+    for part in sends:
+        coded = encode_sum(offset, len(part), facts, mine, got, pairs * rings)
+        offset += len(part)
+        for d, block in zip(part, coded):
+            parts[d] = square_shift(block, *hops[d]) if d else block
     parts = lax.all_to_all(first_sum(parts), "far", 0, 0, tiled=True)
     bundle = lax.all_to_all(last_sum(parts), "far", 0, 0, tiled=True)
     whole = [None] * len(hops)
@@ -588,7 +596,8 @@
     result = ()
     for i in range(2):
         result = update(
-            behind[4 * i : 4 * i + 4],
+            i * len(order[0]),
+            facts,
             core,
             [whole[d] for d in order[i]],
             [swapped[d] for d in order[i]],

time: 122 us -> 123 us (level)
  blocking collectives: 44.9 us -> 24.7 us
  starting transfers between devices: 30 us -> 41.9 us
  waiting for transfers between devices: 10.4 us -> 16.9 us
  Pallas kernels: 28.1 us -> 33 us
  local copies, waits for them, and re-layouts: 6.95 us -> 4.58 us
    all_to_all x1 -> x0, blocking collectives: 20.6 us -> none  [shards(): parts = lax.all_to_all(coded, SQUARE, 0, 0, tiled=True)]
    ppermute x7 -> x14, starting transfers between devices: 8.62 us -> 18.4 us  [square_shift(): return lax.ppermute(x, SQUARE, links)]
    ppermute x7 -> x14, waiting for transfers between devices: 0.02 us -> 6.24 us  [square_shift(): return lax.ppermute(x, SQUARE, links)]
    pallas_call x5 -> x6, Pallas kernels: 11.5 us -> 15.1 us  [the longest x2 7.72 us: update(): pl.pallas_call(functools.partial(update_kernel, count, offset), grid_spec...]
    unnamed x14, local copies, waits for them, and re-layouts: 6.87 us -> 4.5 us
    ppermute x12, starting transfers between devices: 21.4 us -> 23.5 us  [shift(): return lax.ppermute(x, axis, [(i, (i + by) % count) for i in range(count)])]
    pallas_call x1, Pallas kernels: 7.25 us -> 8.61 us  [scatter_add(): pl.pallas_call(functools.partial(scatter_kernel, cap, senders), out_shape...]
  transfers between devices with their start and end apart: 19 -> 26, of which waited for: 2 -> 5; matrix products, arithmetic and copies ran while one was open for 0% -> 0% of each run, Pallas kernels for 7% -> 10%
where the time goes in v3:
time: 123 us
  starting transfers between devices  41.9 us (34%)
  Pallas kernels  33 us (27%)
  blocking collectives  24.7 us (20%)
  waiting for transfers between devices  16.9 us (14%)
  local copies, waits for them, and re-layouts  4.58 us (4%)
    ppermute x12, starting transfers between devices, shift(): return lax.ppermute(x, axis, [(i, (i + by) % count) for i in range(count)])  23.5 us
    ppermute x14, starting transfers between devices, square_shift(): return lax.ppermute(x, SQUARE, links)  18.4 us
    all_to_all x1, blocking collectives, shards(): parts = lax.all_to_all(first_sum(parts), 'far', 0, 0, tiled=True)  14.9 us
    ppermute x12, waiting for transfers between devices, shift(): return lax.ppermute(x, axis, [(i, (i + by) % count) for i in range(count)])  10.6 us
    all_to_all x1, blocking collectives, shards(): bundle = lax.all_to_all(last_sum(parts), 'far', 0, 0, tiled=True)  9.75 us
    pallas_call x1, Pallas kernels, scatter_add(): pl.pallas_call(functools.partial(scatter_kernel, cap, senders), out_shape...  8.61 us
    pallas_call x2, Pallas kernels, update(): pl.pallas_call(functools.partial(update_kernel, count, offset), grid_spec...  7.72 us
    ppermute x14, waiting for transfers between devices, square_shift(): return lax.ppermute(x, SQUARE, links)  6.24 us
  transfers between devices with their start and end apart: 26, of which 5 were waited for; matrix products, arithmetic and copies ran while one was open for 0% of the time, Pallas kernels for 10%

profile of v3, /device:TPU:1, one launch (start us, length us, event | category | flops | bytes accessed | tf_op | source)
XLA Modules:
  0.0 122.6 jit_solution(8222163423314306734)
XLA Ops:
  0.6 0.7 pad_add_fusion.place
  1.4 1.0 copy-done.3
  2.4 0.7 copy-done.4
  3.1 0.7 copy-done.6
  3.8 1.9 %first_pick.1 = (bf16[1040,128]{1,0:T(8,128)(2,1)S(1)}, f32[2048,128]{1,0:T(8,128)S(1)}, s32[4,8,128]{2,1,0:T(8,128)S(1)}, s32[8,4,128]{2,1,0:T(4,128)S(1)}) custom-call(s32[6]{0:T(128)S(1)} %pad_add_fusion.place, s32[8,4,128]{2,1,0:T(4,128)S(1)} %bitcast.21, s32[8,4,128]{2,1,0:T(4,128)S(1)} %bitcast.22, s32[8,4,128]{2,1,0:T(4,128)S(1)} %bitcast.23, ...), custom_call_target="tpu_custom_call" | custom-call | flops 10000000 | bytes 1000000 | tf_op jit(solution)/shard_map/first_pick/pallas_call | solution.py:94
  5.7 2.6 %pick.1 = (bf16[1040,128]{1,0:T(8,128)(2,1)S(1)}, bf16[1040,128]{1,0:T(8,128)(2,1)S(1)}) custom-call(s32[6]{0:T(128)S(1)} %pad_add_fusion.place, s32[8,4,128]{2,1,0:T(4,128)S(1)} %get-tuple-element.22.keys, s32[4,8,128]{2,1,0:T(8,128)S(1)} %get-tuple-element.23.held, f32[2048,128]{1,0:T(8,128)S(1)} %get-tuple-element.24.wide), custom_call_target="tpu_custom_call" | custom-call | flops 20000000 | bytes 1000000 | tf_op jit(solution)/shard_map/pick/pallas_call | solution.py:122
  8.4 2.2 %collective-permute-start.1 = (bf16[1040,128]{1,0:T(8,128)(2,1)S(1)}, bf16[1040,128]{1,0:T(8,128)(2,1)S(1)}, u32[]{:S(2)}, u32[]{:S(2)}) collective-permute-start(bf16[1040,128]{1,0:T(8,128)(2,1)S(1)} %get-tuple-element.26), channel_id=1, source_target_pairs={{0,1},{1,2},{2,3},{3,0},{4,5},{5,6},{6,7},{7,4},{8,9},{9,10},{10,1... | collective-permute-start | bytes 798728 | tf_op jit(solution)/shard_map/ppermute | solution.py:536
  10.6 1.5 %collective-permute-start.2 = (bf16[1040,128]{1,0:T(8,128)(2,1)S(1)}, bf16[1040,128]{1,0:T(8,128)(2,1)S(1)}, u32[]{:S(2)}, u32[]{:S(2)}) collective-permute-start(bf16[1040,128]{1,0:T(8,128)(2,1)S(1)} %get-tuple-element.27), channel_id=1, source_target_pairs={{0,3},{1,0},{2,1},{3,2},{4,7},{5,4},{6,5},{7,6},{8,11},{9,8},{10,9... | collective-permute-start | bytes 798728 | tf_op jit(solution)/shard_map/ppermute | solution.py:536
  12.1 1.6 %collective-permute-start = (bf16[1040,128]{1,0:T(8,128)(2,1)S(1)}, bf16[1040,128]{1,0:T(8,128)(2,1)S(1)}, u32[]{:S(2)}, u32[]{:S(2)}) collective-permute-start(bf16[1040,128]{1,0:T(8,128)(2,1)S(1)} %get-tuple-element.25), channel_id=1, source_target_pairs={{0,2},{1,3},{2,0},{3,1},{4,6},{5,7},{6,4},{7,5},{8,10},{9,11},{10,... | collective-permute-start | bytes 798728 | tf_op jit(solution)/shard_map/ppermute | solution.py:536
  13.6 4.5 %own_rows.1.begun.after = f32[8192,128]{1,0:T(8,128)S(1)} custom-call(s32[6]{0:T(128)S(1)} %pad_add_fusion.place, s32[8,4,128]{2,1,0:T(4,128)S(1)} %get-tuple-element.22.keys, s32[4,8,128]{2,1,0:T(8,128)S(1)} %get-tuple-element.23.held, f32[2048,128]{1,0:T(8,128)S(1)} %get-tuple-element.24.wide), custom_call_target="tpu_custom_call" | custom-call | flops 10000000 | bytes 1000000 | tf_op jit(solution)/shard_map/own_rows/pallas_call | solution.py:246
  18.1 6.6 %collective-permute-done.refs_0_ = bf16[1040,128]{1,0:T(8,128)(2,1)S(1)} collective-permute-done((bf16[1040,128]{1,0:T(8,128)(2,1)S(1)}, bf16[1040,128]{1,0:T(8,128)(2,1)S(1)}, u32[]{:S(2)}, u32[]{:S(2)}) %collective-permute-start) | collective-permute-done | bytes 266272 | tf_op jit(solution)/shard_map/ppermute | solution.py:536
  24.7 8.6 %scatter.1 = (f32[4096,128]{1,0:T(8,128)S(1)}, f32[4096,128]{1,0:T(8,128)}) custom-call(s32[6]{0:T(128)S(1)} %pad_add_fusion.place, f32[8192,128]{1,0:T(8,128)S(1)} %own_rows.1.begun.after, bf16[1040,128]{1,0:T(8,128)(2,1)S(1)} %collective-permute-done.refs_0_, bf16[1040,128]{1,0:T(8,128)(2,1)S(1)} %collective-permute-done.1.refs_1_, ...), custom_call_target="tpu_custom_call" | custom-call | flops 100000000 | bytes 1000000 | tf_op jit(solution)/shard_map/scatter/pallas_call | solution.py:264
  33.3 2.0 %copy-done = f32[8192,128]{1,0:T(8,128)} copy-done((f32[8192,128]{1,0:T(8,128)}, f32[8192,128]{1,0:T(8,128)S(1)}, u32[]{:S(2)}) %copy-start) | copy-done | bytes 4194328
  35.3 1.8 %collective-permute-start.3 = (f32[4096,128]{1,0:T(8,128)}, f32[4096,128]{1,0:T(8,128)}, u32[]{:S(2)}, u32[]{:S(2)}) collective-permute-start(f32[4096,128]{1,0:T(8,128)} %get-tuple-element.29), channel_id=1, source_target_pairs={{0,4},{4,0},{1,5},{5,1},{2,6},{6,2},{3,7},{7,3},{8,12},{12,8},{9,1... | collective-permute-start | bytes 6291464 | tf_op jit(solution)/shard_map/ppermute | solution.py:536
  37.1 0.1 stack.53.targets.groups
  37.2 4.0 %collective-permute-done.3.got = f32[4096,128]{1,0:T(8,128)} collective-permute-done((f32[4096,128]{1,0:T(8,128)}, f32[4096,128]{1,0:T(8,128)}, u32[]{:S(2)}, u32[]{:S(2)}) %collective-permute-start.3) | collective-permute-done | bytes 2097184 | tf_op jit(solution)/shard_map/ppermute | solution.py:536
  41.3 2.5 %encode.3 = (s16[4,136,128]{2,1,0:T(8,128)(2,1)S(1)}, s16[4,136,128]{2,1,0:T(8,128)(2,1)S(1)}, s16[4,136,128]{2,1,0:T(8,128)(2,1)S(1)}) custom-call(s32[16]{0:T(128)S(1)} %stack.53.targets.groups, f32[4096,128]{1,0:T(8,128)S(1)} %get-tuple-element.28.mine, f32[4096,128]{1,0:T(8,128)} %collective-permute-done.3.got), custom_call_target="tpu_custom_call" | custom-call | flops 10000000 | bytes 1000000 | tf_op jit(solution)/shard_map/encode/pallas_call | solution.py:347
  43.8 3.8 %collective-permute-start.10 = (s16[4,136,128]{2,1,0:T(8,128)(2,1)S(1)}, s16[4,136,128]{2,1,0:T(8,128)(2,1)S(1)}, u32[]{:S(2)}, u32[]{:S(2)}) collective-permute-start(s16[4,136,128]{2,1,0:T(8,128)(2,1)S(1)} %get-tuple-element.37), channel_id=1, source_target_pairs={{0,48},{8,56},{16,32},{24,40},{32,16},{40,24},{48,0},{56,8},{1,49}... | collective-permute-start | bytes 417800 | tf_op jit(solution)/shard_map/ppermute | solution.py:546
  47.6 0.4 collective-permute-start.8
  48.0 1.7 %collective-permute-start.9 = (s16[4,136,128]{2,1,0:T(8,128)(2,1)S(1)}, s16[4,136,128]{2,1,0:T(8,128)(2,1)S(1)}, u32[]{:S(2)}, u32[]{:S(2)}) collective-permute-start(s16[4,136,128]{2,1,0:T(8,128)(2,1)S(1)} %get-tuple-element.36), channel_id=1, source_target_pairs={{0,16},{8,24},{16,0},{24,8},{32,48},{40,56},{48,32},{56,40},{1,17}... | collective-permute-start | bytes 417800 | tf_op jit(solution)/shard_map/ppermute | solution.py:546
  49.6 2.8 %encode.2 = (s16[4,136,128]{2,1,0:T(8,128)(2,1)S(1)}, s16[4,136,128]{2,1,0:T(8,128)(2,1)S(1)}, s16[4,136,128]{2,1,0:T(8,128)(2,1)S(1)}, s16[4,136,128]{2,1,0:T(8,128)(2,1)S(1)}, s16[4,136,128]{2,1,0:T(8,128)(2,1)S(1)}) custom-call(s32[16]{0:T(128)S(1)} %stack.53.targets.groups, f32[4096,128]{1,0:T(8,128)S(1)} %get-tuple-element.28.mine, ...), custom_call_target="tpu_custom_call" | custom-call | flops 10000000 | bytes 1000000 | tf_op jit(solution)/shard_map/encode/pallas_call | solution.py:347
  52.4 0.1 collective-permute-start.4
  52.5 2.7 %collective-permute-start.5 = (s16[4,136,128]{2,1,0:T(8,128)(2,1)S(1)}, s16[4,136,128]{2,1,0:T(8,128)(2,1)S(1)}, u32[]{:S(2)}, u32[]{:S(2)}) collective-permute-start(s16[4,136,128]{2,1,0:T(8,128)(2,1)S(1)} %get-tuple-element.32), channel_id=1, source_target_pairs={{0,24},{8,0},{16,8},{24,16},{32,56},{40,32},{48,40},{56,48},{1,25}... | collective-permute-start | bytes 417800 | tf_op jit(solution)/shard_map/ppermute | solution.py:546
  55.1 1.7 %collective-permute-start.6 = (s16[4,136,128]{2,1,0:T(8,128)(2,1)S(1)}, s16[4,136,128]{2,1,0:T(8,128)(2,1)S(1)}, u32[]{:S(2)}, u32[]{:S(2)}) collective-permute-start(s16[4,136,128]{2,1,0:T(8,128)(2,1)S(1)} %get-tuple-element.33), channel_id=1, source_target_pairs={{0,32},{8,40},{16,48},{24,56},{32,0},{40,8},{48,16},{56,24},{1,33}... | collective-permute-start | bytes 417800 | tf_op jit(solution)/shard_map/ppermute | solution.py:546
  56.8 0.8 collective-permute-done.4.refs_1_
  57.6 3.3 %collective-permute-done.5.refs_2_ = s16[4,136,128]{2,1,0:T(8,128)(2,1)S(1)} collective-permute-done((s16[4,136,128]{2,1,0:T(8,128)(2,1)S(1)}, s16[4,136,128]{2,1,0:T(8,128)(2,1)S(1)}, u32[]{:S(2)}, u32[]{:S(2)}) %collective-permute-start.5) | collective-permute-done | bytes 139296 | tf_op jit(solution)/shard_map/ppermute | solution.py:546
  60.9 2.1 %collective-permute-done.7.refs_4_ = s16[4,136,128]{2,1,0:T(8,128)(2,1)S(1)} collective-permute-done((s16[4,136,128]{2,1,0:T(8,128)(2,1)S(1)}, s16[4,136,128]{2,1,0:T(8,128)(2,1)S(1)}, u32[]{:S(2)}, u32[]{:S(2)}) %collective-permute-start.7) | collective-permute-done | bytes 139296 | tf_op jit(solution)/shard_map/ppermute | solution.py:546
  63.0 1.2 first_sum.1
  64.3 14.9 %all_to_all.10.parts = s16[4,136,128]{2,1,0:T(8,128)(2,1)S(1)} all-to-all(s16[4,136,128]{2,1,0:T(8,128)(2,1)S(1)} %first_sum.1), channel_id=1, replica_groups=mesh['far'=4,'pair'=2,'ring'=4,'core'=2,'rows'=4] {'far'}, dimensions={0} | all-to-all | bytes 278528 | tf_op jit(solution)/shard_map/all_to_all | solution.py:589
  79.2 0.4 last_sum.1
  79.5 9.7 %all_to_all.11.refs_4_ = s16[4,136,128]{2,1,0:T(8,128)(2,1)S(1)} all-to-all(s16[4,136,128]{2,1,0:T(8,128)(2,1)S(1)} %last_sum.1), channel_id=1, replica_groups=mesh['far'=4,'pair'=2,'ring'=4,'core'=2,'rows'=4] {'far'}, dimensions={0} | all-to-all | bytes 278528 | tf_op jit(solution)/shard_map/all_to_all | solution.py:590
  89.3 0.2 collective-permute-start.17
  89.5 3.3 %collective-permute-start.18 = (s16[4,136,128]{2,1,0:T(8,128)(2,1)S(1)}, s16[4,136,128]{2,1,0:T(8,128)(2,1)S(1)}, u32[]{:S(2)}, u32[]{:S(2)}) collective-permute-start(s16[4,136,128]{2,1,0:T(8,128)(2,1)S(1)} %all_to_all.11.refs_4_), channel_id=1, source_target_pairs={{0,16},{8,24},{16,0},{24,8},{32,48},{40,56},{48,32},{56,40},{1,17}... | collective-permute-start | bytes 417800 | tf_op jit(solution)/shard_map/ppermute | solution.py:546
  92.8 0.7 collective-permute-start.19
  93.5 6.6 %collective-permute-start.25 = (s16[4,136,128]{2,1,0:T(8,128)(2,1)S(1)}, s16[4,136,128]{2,1,0:T(8,128)(2,1)S(1)}, u32[]{:S(2)}, u32[]{:S(2)}) collective-permute-start(s16[4,136,128]{2,1,0:T(8,128)(2,1)S(1)} %all_to_all.11.refs_4_), channel_id=1, source_target_pairs={{0,4},{4,0},{1,5},{5,1},{2,6},{6,2},{3,7},{7,3},{8,12},{12,8},{9,1... | collective-permute-start | bytes 417800 | tf_op jit(solution)/shard_map/ppermute | solution.py:536
  100.1 1.7 %collective-permute-start.11 = (s16[4,136,128]{2,1,0:T(8,128)(2,1)S(1)}, s16[4,136,128]{2,1,0:T(8,128)(2,1)S(1)}, u32[]{:S(2)}, u32[]{:S(2)}) collective-permute-start(s16[4,136,128]{2,1,0:T(8,128)(2,1)S(1)} %all_to_all.11.refs_4_), channel_id=1, source_target_pairs={{0,8},{8,16},{16,24},{24,0},{32,40},{40,48},{48,56},{56,32},{1,9},... | collective-permute-start | bytes 417800 | tf_op jit(solution)/shard_map/ppermute | solution.py:546
  101.9 1.0 collective-permute-start.12
  102.9 1.1 collective-permute-start.13
  104.0 4.8 %collective-permute-start.21 = (s16[4,136,128]{2,1,0:T(8,128)(2,1)S(1)}, s16[4,136,128]{2,1,0:T(8,128)(2,1)S(1)}, u32[]{:S(2)}, u32[]{:S(2)}) collective-permute-start(s16[4,136,128]{2,1,0:T(8,128)(2,1)S(1)} %collective-permute-done.17.refs_0_), channel_id=1, source_target_pairs={{0,4},{4,0},{1,5},{5,1},{2,6},{6,2},{3,7},{7,3},{8,12},{12,8},{9,1... | collective-permute-start | bytes 417800 | tf_op jit(solution)/shard_map/ppermute | solution.py:536
  108.9 0.1 collective-permute-start.22
  109.0 1.7 %collective-permute-start.23 = (s16[4,136,128]{2,1,0:T(8,128)(2,1)S(1)}, s16[4,136,128]{2,1,0:T(8,128)(2,1)S(1)}, u32[]{:S(2)}, u32[]{:S(2)}) collective-permute-start(s16[4,136,128]{2,1,0:T(8,128)(2,1)S(1)} %collective-permute-done.19.refs_2_), channel_id=1, source_target_pairs={{0,4},{4,0},{1,5},{5,1},{2,6},{6,2},{3,7},{7,3},{8,12},{12,8},{9,1... | collective-permute-start | bytes 417800 | tf_op jit(solution)/shard_map/ppermute | solution.py:536
  110.7 0.9 collective-permute-start.24
  111.5 1.8 %collective-permute-start.14 = (s16[4,136,128]{2,1,0:T(8,128)(2,1)S(1)}, s16[4,136,128]{2,1,0:T(8,128)(2,1)S(1)}, u32[]{:S(2)}, u32[]{:S(2)}) collective-permute-start(s16[4,136,128]{2,1,0:T(8,128)(2,1)S(1)} %collective-permute-done.11.refs_0_), channel_id=1, source_target_pairs={{0,4},{4,0},{1,5},{5,1},{2,6},{6,2},{3,7},{7,3},{8,12},{12,8},{9,1... | collective-permute-start | bytes 417800 | tf_op jit(solution)/shard_map/ppermute | solution.py:536
  113.4 0.0 collective-permute-start.15
  113.4 0.5 collective-permute-start.16
  113.9 0.9 fetch.1
  114.9 4.5 %update.2 = (f32[2,4096,128]{2,1,0:T(8,128)}, f32[2,4096]{1,0:T(2,128)}) custom-call(s32[16]{0:T(128)S(1)} %stack.53.targets.groups, s32[1]{0:T(128)} %bitcast.10.core, s16[4,136,128]{2,1,0:T(8,128)(2,1)S(1)} %collective-permute-done.17.refs_0_, s16[4,136,128]{2,1,0:T(8,128)(2,1)S(1)} %collective-permute-done.18.refs_1_, ...), custom_call_target="tpu_custom_call" | custom-call | flops 10000000 | bytes 1000000 | tf_op jit(solution)/shard_map/update/pallas_call | solution.py:462
  119.4 3.2 %update.3 = (f32[2,4096,128]{2,1,0:T(8,128)}, f32[2,4096]{1,0:T(2,128)}) custom-call(s32[16]{0:T(128)S(1)} %stack.53.targets.groups, s32[1]{0:T(128)} %bitcast.10.core, s16[4,136,128]{2,1,0:T(8,128)(2,1)S(1)} %collective-permute-done.11.refs_0_, ...), custom_call_target="tpu_custom_call", output_to_operand_aliasing={{0}: (10, {}), {1}: (11, {})} | custom-call | flops 10000000 | bytes 1000000 | tf_op jit(solution)/shard_map/update/pallas_call | solution.py:462
  (34 shorter events, 0.1 us)
Async XLA Ops:
  1.4 1.0 copy-start.3
  2.4 0.7 copy-start.4
  3.1 0.7 copy-start.6
  8.4 9.7 %collective-permute-start.1 = (bf16[1040,128]{1,0:T(8,128)(2,1)S(1)}, bf16[1040,128]{1,0:T(8,128)(2,1)S(1)}, u32[]{:S(2)}, u32[]{:S(2)}) collective-permute-start(bf16[1040,128]{1,0:T(8,128)(2,1)S(1)} %get-tuple-element.26), channel_id=1, source_target_pairs={{0,1},{1,2},{2,3},{3,0},{4,5},{5,6},{6,7},{7,4},{8,9},{9,10},{10,1... | collective-permute-start | bytes 798728 | tf_op jit(solution)/shard_map/ppermute | solution.py:536
  10.6 7.6 %collective-permute-start.2 = (bf16[1040,128]{1,0:T(8,128)(2,1)S(1)}, bf16[1040,128]{1,0:T(8,128)(2,1)S(1)}, u32[]{:S(2)}, u32[]{:S(2)}) collective-permute-start(bf16[1040,128]{1,0:T(8,128)(2,1)S(1)} %get-tuple-element.27), channel_id=1, source_target_pairs={{0,3},{1,0},{2,1},{3,2},{4,7},{5,4},{6,5},{7,6},{8,11},{9,8},{10,9... | collective-permute-start | bytes 798728 | tf_op jit(solution)/shard_map/ppermute | solution.py:536
  12.1 12.6 %collective-permute-start = (bf16[1040,128]{1,0:T(8,128)(2,1)S(1)}, bf16[1040,128]{1,0:T(8,128)(2,1)S(1)}, u32[]{:S(2)}, u32[]{:S(2)}) collective-permute-start(bf16[1040,128]{1,0:T(8,128)(2,1)S(1)} %get-tuple-element.25), channel_id=1, source_target_pairs={{0,2},{1,3},{2,0},{3,1},{4,6},{5,7},{6,4},{7,5},{8,10},{9,11},{10,... | collective-permute-start | bytes 798728 | tf_op jit(solution)/shard_map/ppermute | solution.py:536
  33.3 2.0 %copy-start = (f32[8192,128]{1,0:T(8,128)}, f32[8192,128]{1,0:T(8,128)S(1)}, u32[]{:S(2)}) copy-start(f32[8192,128]{1,0:T(8,128)S(1)} %own_rows.1.begun.after) | copy-start | bytes 12582916
  35.3 5.9 %collective-permute-start.3 = (f32[4096,128]{1,0:T(8,128)}, f32[4096,128]{1,0:T(8,128)}, u32[]{:S(2)}, u32[]{:S(2)}) collective-permute-start(f32[4096,128]{1,0:T(8,128)} %get-tuple-element.29), channel_id=1, source_target_pairs={{0,4},{4,0},{1,5},{5,1},{2,6},{6,2},{3,7},{7,3},{8,12},{12,8},{9,1... | collective-permute-start | bytes 6291464 | tf_op jit(solution)/shard_map/ppermute | solution.py:536
  41.3 72.6 %copy-start.2 = (f32[2,4096,128]{2,1,0:T(8,128)S(1)}, f32[2,4096,128]{2,1,0:T(8,128)}, u32[]{:S(2)}) copy-start(f32[2,4096,128]{2,1,0:T(8,128)} %rows.1) | copy-start | bytes 12582916
  43.8 11.4 %collective-permute-start.10 = (s16[4,136,128]{2,1,0:T(8,128)(2,1)S(1)}, s16[4,136,128]{2,1,0:T(8,128)(2,1)S(1)}, u32[]{:S(2)}, u32[]{:S(2)}) collective-permute-start(s16[4,136,128]{2,1,0:T(8,128)(2,1)S(1)} %get-tuple-element.37), channel_id=1, source_target_pairs={{0,48},{8,56},{16,32},{24,40},{32,16},{40,24},{48,0},{56,8},{1,49}... | collective-permute-start | bytes 417800 | tf_op jit(solution)/shard_map/ppermute | solution.py:546
  47.6 9.2 %collective-permute-start.8 = (s16[4,136,128]{2,1,0:T(8,128)(2,1)S(1)}, s16[4,136,128]{2,1,0:T(8,128)(2,1)S(1)}, u32[]{:S(2)}, u32[]{:S(2)}) collective-permute-start(s16[4,136,128]{2,1,0:T(8,128)(2,1)S(1)} %get-tuple-element.35), channel_id=1, source_target_pairs={{0,56},{8,32},{16,40},{24,48},{32,24},{40,0},{48,8},{56,16},{1,57}... | collective-permute-start | bytes 417800 | tf_op jit(solution)/shard_map/ppermute | solution.py:546
  48.0 65.9 %copy-start.5 = (f32[2,4096]{1,0:T(2,128)S(1)}, f32[2,4096]{1,0:T(2,128)}, u32[]{:S(2)}) copy-start(f32[2,4096]{1,0:T(2,128)} %state.1) | copy-start | bytes 98308
  48.0 65.9 %copy-start.1 = (f32[8192,128]{1,0:T(8,128)S(1)}, f32[8192,128]{1,0:T(8,128)}, u32[]{:S(2)}) copy-start(f32[8192,128]{1,0:T(8,128)} %copy-done) | copy-start | bytes 12582916
  48.0 8.8 %collective-permute-start.9 = (s16[4,136,128]{2,1,0:T(8,128)(2,1)S(1)}, s16[4,136,128]{2,1,0:T(8,128)(2,1)S(1)}, u32[]{:S(2)}, u32[]{:S(2)}) collective-permute-start(s16[4,136,128]{2,1,0:T(8,128)(2,1)S(1)} %get-tuple-element.36), channel_id=1, source_target_pairs={{0,16},{8,24},{16,0},{24,8},{32,48},{40,56},{48,32},{56,40},{1,17}... | collective-permute-start | bytes 417800 | tf_op jit(solution)/shard_map/ppermute | solution.py:546
  52.4 5.2 %collective-permute-start.4 = (s16[4,136,128]{2,1,0:T(8,128)(2,1)S(1)}, s16[4,136,128]{2,1,0:T(8,128)(2,1)S(1)}, u32[]{:S(2)}, u32[]{:S(2)}) collective-permute-start(s16[4,136,128]{2,1,0:T(8,128)(2,1)S(1)} %get-tuple-element.31), channel_id=1, source_target_pairs={{0,8},{8,16},{16,24},{24,0},{32,40},{40,48},{48,56},{56,32},{1,9},... | collective-permute-start | bytes 417800 | tf_op jit(solution)/shard_map/ppermute | solution.py:546
  52.5 8.4 %collective-permute-start.5 = (s16[4,136,128]{2,1,0:T(8,128)(2,1)S(1)}, s16[4,136,128]{2,1,0:T(8,128)(2,1)S(1)}, u32[]{:S(2)}, u32[]{:S(2)}) collective-permute-start(s16[4,136,128]{2,1,0:T(8,128)(2,1)S(1)} %get-tuple-element.32), channel_id=1, source_target_pairs={{0,24},{8,0},{16,8},{24,16},{32,56},{40,32},{48,40},{56,48},{1,25}... | collective-permute-start | bytes 417800 | tf_op jit(solution)/shard_map/ppermute | solution.py:546
  55.1 5.8 %collective-permute-start.6 = (s16[4,136,128]{2,1,0:T(8,128)(2,1)S(1)}, s16[4,136,128]{2,1,0:T(8,128)(2,1)S(1)}, u32[]{:S(2)}, u32[]{:S(2)}) collective-permute-start(s16[4,136,128]{2,1,0:T(8,128)(2,1)S(1)} %get-tuple-element.33), channel_id=1, source_target_pairs={{0,32},{8,40},{16,48},{24,56},{32,0},{40,8},{48,16},{56,24},{1,33}... | collective-permute-start | bytes 417800 | tf_op jit(solution)/shard_map/ppermute | solution.py:546
  56.8 6.2 %collective-permute-start.7 = (s16[4,136,128]{2,1,0:T(8,128)(2,1)S(1)}, s16[4,136,128]{2,1,0:T(8,128)(2,1)S(1)}, u32[]{:S(2)}, u32[]{:S(2)}) collective-permute-start(s16[4,136,128]{2,1,0:T(8,128)(2,1)S(1)} %get-tuple-element.34), channel_id=1, source_target_pairs={{0,40},{8,48},{16,56},{24,32},{32,8},{40,16},{48,24},{56,0},{1,41}... | collective-permute-start | bytes 417800 | tf_op jit(solution)/shard_map/ppermute | solution.py:546
  89.3 10.8 %collective-permute-start.17 = (s16[4,136,128]{2,1,0:T(8,128)(2,1)S(1)}, s16[4,136,128]{2,1,0:T(8,128)(2,1)S(1)}, u32[]{:S(2)}, u32[]{:S(2)}) collective-permute-start(s16[4,136,128]{2,1,0:T(8,128)(2,1)S(1)} %all_to_all.11.refs_4_), channel_id=1, source_target_pairs={{0,48},{8,56},{16,32},{24,40},{32,16},{40,24},{48,0},{56,8},{1,49}... | collective-permute-start | bytes 417800 | tf_op jit(solution)/shard_map/ppermute | solution.py:546
  89.5 12.4 %collective-permute-start.18 = (s16[4,136,128]{2,1,0:T(8,128)(2,1)S(1)}, s16[4,136,128]{2,1,0:T(8,128)(2,1)S(1)}, u32[]{:S(2)}, u32[]{:S(2)}) collective-permute-start(s16[4,136,128]{2,1,0:T(8,128)(2,1)S(1)} %all_to_all.11.refs_4_), channel_id=1, source_target_pairs={{0,16},{8,24},{16,0},{24,8},{32,48},{40,56},{48,32},{56,40},{1,17}... | collective-permute-start | bytes 417800 | tf_op jit(solution)/shard_map/ppermute | solution.py:546
  92.8 10.1 %collective-permute-start.19 = (s16[4,136,128]{2,1,0:T(8,128)(2,1)S(1)}, s16[4,136,128]{2,1,0:T(8,128)(2,1)S(1)}, u32[]{:S(2)}, u32[]{:S(2)}) collective-permute-start(s16[4,136,128]{2,1,0:T(8,128)(2,1)S(1)} %all_to_all.11.refs_4_), channel_id=1, source_target_pairs={{0,56},{8,32},{16,40},{24,48},{32,24},{40,0},{48,8},{56,16},{1,57}... | collective-permute-start | bytes 417800 | tf_op jit(solution)/shard_map/ppermute | solution.py:546
  93.5 10.5 %collective-permute-start.20 = (s16[4,136,128]{2,1,0:T(8,128)(2,1)S(1)}, s16[4,136,128]{2,1,0:T(8,128)(2,1)S(1)}, u32[]{:S(2)}, u32[]{:S(2)}) collective-permute-start(s16[4,136,128]{2,1,0:T(8,128)(2,1)S(1)} %all_to_all.11.refs_4_), channel_id=1, source_target_pairs={{0,24},{8,0},{16,8},{24,16},{32,56},{40,32},{48,40},{56,48},{1,25}... | collective-permute-start | bytes 417800 | tf_op jit(solution)/shard_map/ppermute | solution.py:546
  93.5 15.3 %collective-permute-start.25 = (s16[4,136,128]{2,1,0:T(8,128)(2,1)S(1)}, s16[4,136,128]{2,1,0:T(8,128)(2,1)S(1)}, u32[]{:S(2)}, u32[]{:S(2)}) collective-permute-start(s16[4,136,128]{2,1,0:T(8,128)(2,1)S(1)} %all_to_all.11.refs_4_), channel_id=1, source_target_pairs={{0,4},{4,0},{1,5},{5,1},{2,6},{6,2},{3,7},{7,3},{8,12},{12,8},{9,1... | collective-permute-start | bytes 417800 | tf_op jit(solution)/shard_map/ppermute | solution.py:536
  100.1 8.9 %collective-permute-start.11 = (s16[4,136,128]{2,1,0:T(8,128)(2,1)S(1)}, s16[4,136,128]{2,1,0:T(8,128)(2,1)S(1)}, u32[]{:S(2)}, u32[]{:S(2)}) collective-permute-start(s16[4,136,128]{2,1,0:T(8,128)(2,1)S(1)} %all_to_all.11.refs_4_), channel_id=1, source_target_pairs={{0,8},{8,16},{16,24},{24,0},{32,40},{40,48},{48,56},{56,32},{1,9},... | collective-permute-start | bytes 417800 | tf_op jit(solution)/shard_map/ppermute | solution.py:546
  101.9 8.8 %collective-permute-start.12 = (s16[4,136,128]{2,1,0:T(8,128)(2,1)S(1)}, s16[4,136,128]{2,1,0:T(8,128)(2,1)S(1)}, u32[]{:S(2)}, u32[]{:S(2)}) collective-permute-start(s16[4,136,128]{2,1,0:T(8,128)(2,1)S(1)} %all_to_all.11.refs_4_), channel_id=1, source_target_pairs={{0,40},{8,48},{16,56},{24,32},{32,8},{40,16},{48,24},{56,0},{1,41}... | collective-permute-start | bytes 417800 | tf_op jit(solution)/shard_map/ppermute | solution.py:546
  102.9 8.7 %collective-permute-start.13 = (s16[4,136,128]{2,1,0:T(8,128)(2,1)S(1)}, s16[4,136,128]{2,1,0:T(8,128)(2,1)S(1)}, u32[]{:S(2)}, u32[]{:S(2)}) collective-permute-start(s16[4,136,128]{2,1,0:T(8,128)(2,1)S(1)} %all_to_all.11.refs_4_), channel_id=1, source_target_pairs={{0,32},{8,40},{16,48},{24,56},{32,0},{40,8},{48,16},{56,24},{1,33}... | collective-permute-start | bytes 417800 | tf_op jit(solution)/shard_map/ppermute | solution.py:546
  104.0 9.3 %collective-permute-start.21 = (s16[4,136,128]{2,1,0:T(8,128)(2,1)S(1)}, s16[4,136,128]{2,1,0:T(8,128)(2,1)S(1)}, u32[]{:S(2)}, u32[]{:S(2)}) collective-permute-start(s16[4,136,128]{2,1,0:T(8,128)(2,1)S(1)} %collective-permute-done.17.refs_0_), channel_id=1, source_target_pairs={{0,4},{4,0},{1,5},{5,1},{2,6},{6,2},{3,7},{7,3},{8,12},{12,8},{9,1... | collective-permute-start | bytes 417800 | tf_op jit(solution)/shard_map/ppermute | solution.py:536
  108.9 4.5 %collective-permute-start.22 = (s16[4,136,128]{2,1,0:T(8,128)(2,1)S(1)}, s16[4,136,128]{2,1,0:T(8,128)(2,1)S(1)}, u32[]{:S(2)}, u32[]{:S(2)}) collective-permute-start(s16[4,136,128]{2,1,0:T(8,128)(2,1)S(1)} %collective-permute-done.18.refs_1_), channel_id=1, source_target_pairs={{0,4},{4,0},{1,5},{5,1},{2,6},{6,2},{3,7},{7,3},{8,12},{12,8},{9,1... | collective-permute-start | bytes 417800 | tf_op jit(solution)/shard_map/ppermute | solution.py:536
  109.0 5.9 %collective-permute-start.23 = (s16[4,136,128]{2,1,0:T(8,128)(2,1)S(1)}, s16[4,136,128]{2,1,0:T(8,128)(2,1)S(1)}, u32[]{:S(2)}, u32[]{:S(2)}) collective-permute-start(s16[4,136,128]{2,1,0:T(8,128)(2,1)S(1)} %collective-permute-done.19.refs_2_), channel_id=1, source_target_pairs={{0,4},{4,0},{1,5},{5,1},{2,6},{6,2},{3,7},{7,3},{8,12},{12,8},{9,1... | collective-permute-start | bytes 417800 | tf_op jit(solution)/shard_map/ppermute | solution.py:536
  110.7 4.2 %collective-permute-start.24 = (s16[4,136,128]{2,1,0:T(8,128)(2,1)S(1)}, s16[4,136,128]{2,1,0:T(8,128)(2,1)S(1)}, u32[]{:S(2)}, u32[]{:S(2)}) collective-permute-start(s16[4,136,128]{2,1,0:T(8,128)(2,1)S(1)} %collective-permute-done.20.refs_3_), channel_id=1, source_target_pairs={{0,4},{4,0},{1,5},{5,1},{2,6},{6,2},{3,7},{7,3},{8,12},{12,8},{9,1... | collective-permute-start | bytes 417800 | tf_op jit(solution)/shard_map/ppermute | solution.py:536
  111.5 7.8 %collective-permute-start.14 = (s16[4,136,128]{2,1,0:T(8,128)(2,1)S(1)}, s16[4,136,128]{2,1,0:T(8,128)(2,1)S(1)}, u32[]{:S(2)}, u32[]{:S(2)}) collective-permute-start(s16[4,136,128]{2,1,0:T(8,128)(2,1)S(1)} %collective-permute-done.11.refs_0_), channel_id=1, source_target_pairs={{0,4},{4,0},{1,5},{5,1},{2,6},{6,2},{3,7},{7,3},{8,12},{12,8},{9,1... | collective-permute-start | bytes 417800 | tf_op jit(solution)/shard_map/ppermute | solution.py:536
  113.4 6.0 %collective-permute-start.15 = (s16[4,136,128]{2,1,0:T(8,128)(2,1)S(1)}, s16[4,136,128]{2,1,0:T(8,128)(2,1)S(1)}, u32[]{:S(2)}, u32[]{:S(2)}) collective-permute-start(s16[4,136,128]{2,1,0:T(8,128)(2,1)S(1)} %collective-permute-done.12.refs_1_), channel_id=1, source_target_pairs={{0,4},{4,0},{1,5},{5,1},{2,6},{6,2},{3,7},{7,3},{8,12},{12,8},{9,1... | collective-permute-start | bytes 417800 | tf_op jit(solution)/shard_map/ppermute | solution.py:536
  113.4 6.0 %collective-permute-start.16 = (s16[4,136,128]{2,1,0:T(8,128)(2,1)S(1)}, s16[4,136,128]{2,1,0:T(8,128)(2,1)S(1)}, u32[]{:S(2)}, u32[]{:S(2)}) collective-permute-start(s16[4,136,128]{2,1,0:T(8,128)(2,1)S(1)} %collective-permute-done.13.refs_2_), channel_id=1, source_target_pairs={{0,4},{4,0},{1,5},{5,1},{2,6},{6,2},{3,7},{7,3},{8,12},{12,8},{9,1... | collective-permute-start | bytes 417800 | tf_op jit(solution)/shard_map/ppermute | solution.py:536

commit v4 on v3

--- a/solution.py
+++ b/solution.py
@@ -206,25 +206,32 @@
     pieces(out.shape[0], 64, add_up)
 
 
+def add_half(index, begun, sums, out):
+    half = out.shape[0]
+
+    def add_up(i):
+        there = pl.ds(pl.multiple_of(index * half + i * 64, 64), 64)
+        total = begun[there, :]
+        for part in sums:
+            total = total + part[there, :]
+        out[pl.ds(pl.multiple_of(i * 64, 64), 64), :] = total
+
+    loop(half // 64, add_up)
+
+
 def scatter_kernel(cap, senders, place, begun, *refs):
-    grads, outs, refs = refs[:senders], refs[senders : senders + 2], refs[senders + 2 :]
+    grads, other, refs = refs[:senders], refs[senders], refs[senders + 1 :]
     sums, wides = refs[:senders], refs[senders : 2 * senders]
     found, keys, sem = refs[2 * senders :]
     chunks = cap // LANES
     prepare(grads, cap, sums, wides, found, keys, sem)
     rows = [k * chunks for k in range(senders)]
     loop(chunks, lambda chunk: add_rows(1, sums, wides, keys, rows, chunk))
-    half = outs[0].shape[0]
-    for out, index in ((outs[1], 1 - place[1]), (outs[0], place[1])):
-
-        def add_up(i):
-            there = pl.ds(pl.multiple_of(index * half + i * 64, 64), 64)
-            total = begun[there, :]
-            for part in sums:
-                total = total + part[there, :]
-            out[pl.ds(pl.multiple_of(i * 64, 64), 64), :] = total
-
-        loop(half // 64, add_up)
+    add_half(1 - place[1], begun, sums, other)
+
+
+def half_kernel(place, begun, *refs):
+    add_half(place[1], begun, refs[:-1], refs[-1])
 
 
 def tables_of(rows, width, cap, senders, pairs):
@@ -260,17 +267,32 @@
     senders = len(grads)
     cap, width = grads[0].shape[0] - 2 * SPARE, grads[0].shape[1]
     rows = begun.shape[0]
-    shape = jax.ShapeDtypeStruct((rows // 2, width), jnp.float32)
-    return pl.pallas_call(
+    other = jax.ShapeDtypeStruct((rows // 2, width), jnp.float32)
+    table = jax.ShapeDtypeStruct((rows + SPARE, width), jnp.float32)
+    other, *sums = pl.pallas_call(
         functools.partial(scatter_kernel, cap, senders),
-        out_shape=(shape, shape),
+        out_shape=(other,) + (table,) * senders,
         in_specs=[SM, VM] + [VM] * senders,
-        out_specs=(VM, VM),
-        scratch_shapes=tables_of(rows, width, cap, senders, 1),
-        compiler_params=room(24),
+        out_specs=(VM,) * (senders + 1),
+        scratch_shapes=tables_of(rows, width, cap, senders, 1)[senders:],
+        compiler_params=room(8),
         cost_estimate=cost(10**8),
         name="scatter",
     )(place, begun, *grads)
+    return other, sums
+
+
+def sum_half(place, begun, sums):
+    rows, width = begun.shape
+    return pl.pallas_call(
+        half_kernel,
+        out_shape=jax.ShapeDtypeStruct((rows // 2, width), jnp.float32),
+        in_specs=[SM, VM] + [VM] * len(sums),
+        out_specs=VM,
+        compiler_params=room(8),
+        cost_estimate=cost(10**6),
+        name="half",
+    )(place, begun, *sums)
 
 
 def diagonal():
@@ -559,7 +581,7 @@
     hops = [(0, 0), (0, 1), (0, 3), (1, 0), (1, 1), (1, 3), (0, 2), (1, 2)]
     behind = [(pair + p) % pairs * rings + (ring + rings - r) % rings for p, r in hops]
     ahead = [(pair + p) % pairs * rings + (ring + r) % rings for p, r in hops]
-    order = ((7, 6, 5, 2, 0), (1, 4, 3))
+    order = ((7, 6, 5, 2, 1, 0), (4, 3))
     sends = ((7, 6, 5), (2, 1, 4, 3, 0))
     facts = [behind[d] for part in order for d in part]
     facts = jnp.stack(facts + [ahead[d] for part in sends for d in part]).astype(jnp.int32)
@@ -576,7 +598,8 @@
     for hop, block in picked.items():
         grads.append(shift(block, "rows", hop))
     begun = own_rows(place, keys, held, wide, rows)
-    mine, other = scatter_add(place, begun, grads)
+    other, sums = scatter_add(place, begun, grads)
+    mine = sum_half(place, begun, sums)
     fetched = fetch(facts, len(order[0]), len(hops), table_rows, begun)
     got = shift(other, "core", 1)
     parts = [None] * len(hops)

time: 123 us -> 131 us (1.065)
  local copies, waits for them, and re-layouts: 4.58 us -> 19.4 us
  waiting for transfers between devices: 16.9 us -> 11.6 us
  Pallas kernels: 33 us -> 31.2 us
    unnamed x14 -> x28, local copies, waits for them, and re-layouts: 4.5 us -> 19.3 us
    ppermute x12, waiting for transfers between devices: 10.6 us -> 6.6 us  [shift(): return lax.ppermute(x, axis, [(i, (i + by) % count) for i in range(count)])]
    ppermute x14, starting transfers between devices: 18.4 us -> 21 us  [square_shift(): return lax.ppermute(x, SQUARE, links)]
    pallas_call x2, Pallas kernels: 5.25 us -> 2.9 us  [encode_sum(): pl.pallas_call(functools.partial(encode_kernel, offset), out_shape=(shape...]
    ppermute x12, starting transfers between devices: 23.5 us -> 21.2 us  [shift(): return lax.ppermute(x, axis, [(i, (i + by) % count) for i in range(count)])]
    pallas_call x0 -> x1, Pallas kernels: none -> 1.42 us  [sum_half(): pl.pallas_call(half_kernel, out_shape=jax.ShapeDtypeStruct((rows // 2, wi...]
  transfers between devices with their start and end apart: 26 -> 26, of which waited for: 5 -> 4; matrix products, arithmetic and copies ran while one was open for 0% -> 0% of each run, Pallas kernels for 10% -> 10%
where the time goes in v4:
time: 131 us
  starting transfers between devices  42.1 us (32%)
  Pallas kernels  31.2 us (24%)
  blocking collectives  25 us (19%)
  local copies, waits for them, and re-layouts  19.4 us (15%)
  waiting for transfers between devices  11.6 us (9%)
    ppermute x12, starting transfers between devices, shift(): return lax.ppermute(x, axis, [(i, (i + by) % count) for i in range(count)])  21.2 us
    ppermute x14, starting transfers between devices, square_shift(): return lax.ppermute(x, SQUARE, links)  21 us
    unnamed x28, local copies, waits for them, and re-layouts  19.3 us
    all_to_all x1, blocking collectives, shards(): parts = lax.all_to_all(first_sum(parts), 'far', 0, 0, tiled=True)  15.2 us
    all_to_all x1, blocking collectives, shards(): bundle = lax.all_to_all(last_sum(parts), 'far', 0, 0, tiled=True)  9.77 us
    pallas_call x1, Pallas kernels, scatter_add(): pl.pallas_call(functools.partial(scatter_kernel, cap, senders), out_shape...  7.93 us
    pallas_call x2, Pallas kernels, update(): pl.pallas_call(functools.partial(update_kernel, count, offset), grid_spec...  7.54 us
    ppermute x12, waiting for transfers between devices, shift(): return lax.ppermute(x, axis, [(i, (i + by) % count) for i in range(count)])  6.6 us
  transfers between devices with their start and end apart: 26, of which 4 were waited for; matrix products, arithmetic and copies ran while one was open for 0% of the time, Pallas kernels for 10%

profile of v4, /device:TPU:1, one launch (start us, length us, event | category | flops | bytes accessed | tf_op | source)
XLA Modules:
  0.0 130.9 jit_solution(15529818662086982650)
XLA Ops:
  0.6 0.7 pad_add_fusion.place
  1.4 1.0 copy-done.10
  2.4 0.7 copy-done.11
  3.1 0.7 copy-done.13
  3.8 1.9 %first_pick.1 = (bf16[1040,128]{1,0:T(8,128)(2,1)S(1)}, f32[2048,128]{1,0:T(8,128)S(1)}, s32[4,8,128]{2,1,0:T(8,128)S(1)}, s32[8,4,128]{2,1,0:T(4,128)S(1)}) custom-call(s32[6]{0:T(128)S(1)} %pad_add_fusion.place, s32[8,4,128]{2,1,0:T(4,128)S(1)} %bitcast.21, s32[8,4,128]{2,1,0:T(4,128)S(1)} %bitcast.22, s32[8,4,128]{2,1,0:T(4,128)S(1)} %bitcast.23, ...), custom_call_target="tpu_custom_call" | custom-call | flops 10000000 | bytes 1000000 | tf_op jit(solution)/shard_map/first_pick/pallas_call | solution.py:94
  5.7 2.6 %pick.1 = (bf16[1040,128]{1,0:T(8,128)(2,1)S(1)}, bf16[1040,128]{1,0:T(8,128)(2,1)S(1)}) custom-call(s32[6]{0:T(128)S(1)} %pad_add_fusion.place, s32[8,4,128]{2,1,0:T(4,128)S(1)} %get-tuple-element.24.keys, s32[4,8,128]{2,1,0:T(8,128)S(1)} %get-tuple-element.25.held, f32[2048,128]{1,0:T(8,128)S(1)} %get-tuple-element.26.wide), custom_call_target="tpu_custom_call" | custom-call | flops 20000000 | bytes 1000000 | tf_op jit(solution)/shard_map/pick/pallas_call | solution.py:122
  8.4 2.2 %collective-permute-start.1 = (bf16[1040,128]{1,0:T(8,128)(2,1)S(1)}, bf16[1040,128]{1,0:T(8,128)(2,1)S(1)}, u32[]{:S(2)}, u32[]{:S(2)}) collective-permute-start(bf16[1040,128]{1,0:T(8,128)(2,1)S(1)} %get-tuple-element.28), channel_id=1, source_target_pairs={{0,1},{1,2},{2,3},{3,0},{4,5},{5,6},{6,7},{7,4},{8,9},{9,10},{10,1... | collective-permute-start | bytes 798728 | tf_op jit(solution)/shard_map/ppermute | solution.py:558
  10.6 1.5 %collective-permute-start.2 = (bf16[1040,128]{1,0:T(8,128)(2,1)S(1)}, bf16[1040,128]{1,0:T(8,128)(2,1)S(1)}, u32[]{:S(2)}, u32[]{:S(2)}) collective-permute-start(bf16[1040,128]{1,0:T(8,128)(2,1)S(1)} %get-tuple-element.29), channel_id=1, source_target_pairs={{0,3},{1,0},{2,1},{3,2},{4,7},{5,4},{6,5},{7,6},{8,11},{9,8},{10,9... | collective-permute-start | bytes 798728 | tf_op jit(solution)/shard_map/ppermute | solution.py:558
  12.1 1.6 %collective-permute-start = (bf16[1040,128]{1,0:T(8,128)(2,1)S(1)}, bf16[1040,128]{1,0:T(8,128)(2,1)S(1)}, u32[]{:S(2)}, u32[]{:S(2)}) collective-permute-start(bf16[1040,128]{1,0:T(8,128)(2,1)S(1)} %get-tuple-element.27), channel_id=1, source_target_pairs={{0,2},{1,3},{2,0},{3,1},{4,6},{5,7},{6,4},{7,5},{8,10},{9,11},{10,... | collective-permute-start | bytes 798728 | tf_op jit(solution)/shard_map/ppermute | solution.py:558
  13.6 4.5 %own_rows.1.begun.after = f32[8192,128]{1,0:T(8,128)S(1)} custom-call(s32[6]{0:T(128)S(1)} %pad_add_fusion.place, s32[8,4,128]{2,1,0:T(4,128)S(1)} %get-tuple-element.24.keys, s32[4,8,128]{2,1,0:T(8,128)S(1)} %get-tuple-element.25.held, f32[2048,128]{1,0:T(8,128)S(1)} %get-tuple-element.26.wide), custom_call_target="tpu_custom_call" | custom-call | flops 10000000 | bytes 1000000 | tf_op jit(solution)/shard_map/own_rows/pallas_call | solution.py:253
  18.1 6.6 %collective-permute-done.refs_0_ = bf16[1040,128]{1,0:T(8,128)(2,1)S(1)} collective-permute-done((bf16[1040,128]{1,0:T(8,128)(2,1)S(1)}, bf16[1040,128]{1,0:T(8,128)(2,1)S(1)}, u32[]{:S(2)}, u32[]{:S(2)}) %collective-permute-start) | collective-permute-done | bytes 266272 | tf_op jit(solution)/shard_map/ppermute | solution.py:558
  24.7 7.9 %scatter.1 = (f32[4096,128]{1,0:T(8,128)}, f32[8200,128]{1,0:T(8,128)S(1)}, f32[8200,128]{1,0:T(8,128)S(1)}, f32[8200,128]{1,0:T(8,128)S(1)}) custom-call(s32[6]{0:T(128)S(1)} %pad_add_fusion.place, f32[8192,128]{1,0:T(8,128)S(1)} %own_rows.1.begun.after, bf16[1040,128]{1,0:T(8,128)(2,1)S(1)} %collective-permute-done.refs_0_, ...), custom_call_target="tpu_custom_call" | custom-call | flops 100000000 | bytes 1000000 | tf_op jit(solution)/shard_map/scatter/pallas_call | solution.py:272
  32.7 2.0 %copy-done = f32[8192,128]{1,0:T(8,128)} copy-done((f32[8192,128]{1,0:T(8,128)}, f32[8192,128]{1,0:T(8,128)S(1)}, u32[]{:S(2)}) %copy-start) | copy-done | bytes 4194328
  34.7 2.0 %copy-done.3 = f32[8200,128]{1,0:T(8,128)} copy-done((f32[8200,128]{1,0:T(8,128)}, f32[8200,128]{1,0:T(8,128)S(1)}, u32[]{:S(2)}) %copy-start.3) | copy-done | bytes 4198424
  36.6 2.0 %copy-done.5 = f32[8200,128]{1,0:T(8,128)} copy-done((f32[8200,128]{1,0:T(8,128)}, f32[8200,128]{1,0:T(8,128)S(1)}, u32[]{:S(2)}) %copy-start.5) | copy-done | bytes 4198424
  38.7 2.1 %copy-done.7 = f32[8200,128]{1,0:T(8,128)} copy-done((f32[8200,128]{1,0:T(8,128)}, f32[8200,128]{1,0:T(8,128)S(1)}, u32[]{:S(2)}) %copy-start.7) | copy-done | bytes 4198424
  40.7 1.8 %collective-permute-start.3 = (f32[4096,128]{1,0:T(8,128)}, f32[4096,128]{1,0:T(8,128)S(1)}, u32[]{:S(2)}, u32[]{:S(2)}) collective-permute-start(f32[4096,128]{1,0:T(8,128)} %get-tuple-element.33), channel_id=1, source_target_pairs={{0,4},{4,0},{1,5},{5,1},{2,6},{6,2},{3,7},{7,3},{8,12},{12,8},{9,1... | collective-permute-start | bytes 6291464 | tf_op jit(solution)/shard_map/ppermute | solution.py:558
  42.6 2.2 %copy-done.1 = f32[8192,128]{1,0:T(8,128)S(1)} copy-done((f32[8192,128]{1,0:T(8,128)S(1)}, f32[8192,128]{1,0:T(8,128)}, u32[]{:S(2)}) %copy-start.1) | copy-done | bytes 4194328
  44.8 2.2 %copy-done.4 = f32[8200,128]{1,0:T(8,128)S(1)} copy-done((f32[8200,128]{1,0:T(8,128)S(1)}, f32[8200,128]{1,0:T(8,128)}, u32[]{:S(2)}) %copy-start.4) | copy-done | bytes 4198424
  47.0 2.2 %copy-done.6 = f32[8200,128]{1,0:T(8,128)S(1)} copy-done((f32[8200,128]{1,0:T(8,128)S(1)}, f32[8200,128]{1,0:T(8,128)}, u32[]{:S(2)}) %copy-start.6) | copy-done | bytes 4198424
  49.2 2.2 %copy-done.8 = f32[8200,128]{1,0:T(8,128)S(1)} copy-done((f32[8200,128]{1,0:T(8,128)S(1)}, f32[8200,128]{1,0:T(8,128)}, u32[]{:S(2)}) %copy-start.8) | copy-done | bytes 4198424
  51.4 1.4 %half.1.mine = f32[4096,128]{1,0:T(8,128)S(1)} custom-call(s32[6]{0:T(128)S(1)} %pad_add_fusion.place, f32[8192,128]{1,0:T(8,128)S(1)} %copy-done.1, f32[8200,128]{1,0:T(8,128)S(1)} %copy-done.4, f32[8200,128]{1,0:T(8,128)S(1)} %copy-done.6, f32[8200,128]{1,0:T(8,128)S(1)} %copy-done.8), custom_call_target="tpu_custom_call" | custom-call | flops 1000000 | bytes 1000000 | tf_op jit(solution)/shard_map/half/pallas_call | solution.py:287
  52.8 1.3 encode.3
  54.1 3.8 %collective-permute-start.10 = (s16[4,136,128]{2,1,0:T(8,128)(2,1)S(1)}, s16[4,136,128]{2,1,0:T(8,128)(2,1)S(1)}, u32[]{:S(2)}, u32[]{:S(2)}) collective-permute-start(s16[4,136,128]{2,1,0:T(8,128)(2,1)S(1)} %get-tuple-element.41), channel_id=1, source_target_pairs={{0,48},{8,56},{16,32},{24,40},{32,16},{40,24},{48,0},{56,8},{1,49}... | collective-permute-start | bytes 417800 | tf_op jit(solution)/shard_map/ppermute | solution.py:568
  58.3 1.7 %collective-permute-start.9 = (s16[4,136,128]{2,1,0:T(8,128)(2,1)S(1)}, s16[4,136,128]{2,1,0:T(8,128)(2,1)S(1)}, u32[]{:S(2)}, u32[]{:S(2)}) collective-permute-start(s16[4,136,128]{2,1,0:T(8,128)(2,1)S(1)} %get-tuple-element.40), channel_id=1, source_target_pairs={{0,16},{8,24},{16,0},{24,8},{32,48},{40,56},{48,32},{56,40},{1,17}... | collective-permute-start | bytes 417800 | tf_op jit(solution)/shard_map/ppermute | solution.py:568
  59.9 1.6 %encode.2 = (s16[4,136,128]{2,1,0:T(8,128)(2,1)S(1)}, s16[4,136,128]{2,1,0:T(8,128)(2,1)S(1)}, s16[4,136,128]{2,1,0:T(8,128)(2,1)S(1)}, s16[4,136,128]{2,1,0:T(8,128)(2,1)S(1)}, s16[4,136,128]{2,1,0:T(8,128)(2,1)S(1)}) custom-call(s32[16]{0:T(128)S(1)} %stack.53.targets.groups, f32[4096,128]{1,0:T(8,128)S(1)} %half.1.mine, ...), custom_call_target="tpu_custom_call" | custom-call | flops 10000000 | bytes 1000000 | tf_op jit(solution)/shard_map/encode/pallas_call | solution.py:369
  61.7 2.7 %collective-permute-start.5 = (s16[4,136,128]{2,1,0:T(8,128)(2,1)S(1)}, s16[4,136,128]{2,1,0:T(8,128)(2,1)S(1)}, u32[]{:S(2)}, u32[]{:S(2)}) collective-permute-start(s16[4,136,128]{2,1,0:T(8,128)(2,1)S(1)} %get-tuple-element.36), channel_id=1, source_target_pairs={{0,24},{8,0},{16,8},{24,16},{32,56},{40,32},{48,40},{56,48},{1,25}... | collective-permute-start | bytes 417800 | tf_op jit(solution)/shard_map/ppermute | solution.py:568
  64.3 1.4 %collective-permute-start.6 = (s16[4,136,128]{2,1,0:T(8,128)(2,1)S(1)}, s16[4,136,128]{2,1,0:T(8,128)(2,1)S(1)}, u32[]{:S(2)}, u32[]{:S(2)}) collective-permute-start(s16[4,136,128]{2,1,0:T(8,128)(2,1)S(1)} %get-tuple-element.37), channel_id=1, source_target_pairs={{0,32},{8,40},{16,48},{24,56},{32,0},{40,8},{48,16},{56,24},{1,33}... | collective-permute-start | bytes 417800 | tf_op jit(solution)/shard_map/ppermute | solution.py:568
  65.7 1.5 %collective-permute-start.7 = (s16[4,136,128]{2,1,0:T(8,128)(2,1)S(1)}, s16[4,136,128]{2,1,0:T(8,128)(2,1)S(1)}, u32[]{:S(2)}, u32[]{:S(2)}) collective-permute-start(s16[4,136,128]{2,1,0:T(8,128)(2,1)S(1)} %get-tuple-element.38), channel_id=1, source_target_pairs={{0,40},{8,48},{16,56},{24,32},{32,8},{40,16},{48,24},{56,0},{1,41}... | collective-permute-start | bytes 417800 | tf_op jit(solution)/shard_map/ppermute | solution.py:568
  67.3 4.0 %collective-permute-done.5.refs_2_ = s16[4,136,128]{2,1,0:T(8,128)(2,1)S(1)} collective-permute-done((s16[4,136,128]{2,1,0:T(8,128)(2,1)S(1)}, s16[4,136,128]{2,1,0:T(8,128)(2,1)S(1)}, u32[]{:S(2)}, u32[]{:S(2)}) %collective-permute-start.5) | collective-permute-done | bytes 139296 | tf_op jit(solution)/shard_map/ppermute | solution.py:568
  71.3 0.6 collective-permute-done.7.refs_4_
  71.9 1.2 first_sum.1
  73.1 15.2 %all_to_all.10.parts = s16[4,136,128]{2,1,0:T(8,128)(2,1)S(1)} all-to-all(s16[4,136,128]{2,1,0:T(8,128)(2,1)S(1)} %first_sum.1), channel_id=1, replica_groups=mesh['far'=4,'pair'=2,'ring'=4,'core'=2,'rows'=4] {'far'}, dimensions={0} | all-to-all | bytes 278528 | tf_op jit(solution)/shard_map/all_to_all | solution.py:612
  88.6 9.8 %all_to_all.11.refs_5_ = s16[4,136,128]{2,1,0:T(8,128)(2,1)S(1)} all-to-all(s16[4,136,128]{2,1,0:T(8,128)(2,1)S(1)} %last_sum.1), channel_id=1, replica_groups=mesh['far'=4,'pair'=2,'ring'=4,'core'=2,'rows'=4] {'far'}, dimensions={0} | all-to-all | bytes 278528 | tf_op jit(solution)/shard_map/all_to_all | solution.py:613
  98.4 2.1 %collective-permute-start.15 = (s16[4,136,128]{2,1,0:T(8,128)(2,1)S(1)}, s16[4,136,128]{2,1,0:T(8,128)(2,1)S(1)}, u32[]{:S(2)}, u32[]{:S(2)}) collective-permute-start(s16[4,136,128]{2,1,0:T(8,128)(2,1)S(1)} %all_to_all.11.refs_5_), channel_id=1, source_target_pairs={{0,48},{8,56},{16,32},{24,40},{32,16},{40,24},{48,0},{56,8},{1,49}... | collective-permute-start | bytes 417800 | tf_op jit(solution)/shard_map/ppermute | solution.py:568
  100.5 1.7 %collective-permute-start.16 = (s16[4,136,128]{2,1,0:T(8,128)(2,1)S(1)}, s16[4,136,128]{2,1,0:T(8,128)(2,1)S(1)}, u32[]{:S(2)}, u32[]{:S(2)}) collective-permute-start(s16[4,136,128]{2,1,0:T(8,128)(2,1)S(1)} %all_to_all.11.refs_5_), channel_id=1, source_target_pairs={{0,16},{8,24},{16,0},{24,8},{32,48},{40,56},{48,32},{56,40},{1,17}... | collective-permute-start | bytes 417800 | tf_op jit(solution)/shard_map/ppermute | solution.py:568
  102.2 2.4 %collective-permute-start.17 = (s16[4,136,128]{2,1,0:T(8,128)(2,1)S(1)}, s16[4,136,128]{2,1,0:T(8,128)(2,1)S(1)}, u32[]{:S(2)}, u32[]{:S(2)}) collective-permute-start(s16[4,136,128]{2,1,0:T(8,128)(2,1)S(1)} %all_to_all.11.refs_5_), channel_id=1, source_target_pairs={{0,56},{8,32},{16,40},{24,48},{32,24},{40,0},{48,8},{56,16},{1,57}... | collective-permute-start | bytes 417800 | tf_op jit(solution)/shard_map/ppermute | solution.py:568
  104.6 1.5 %collective-permute-start.19 = (s16[4,136,128]{2,1,0:T(8,128)(2,1)S(1)}, s16[4,136,128]{2,1,0:T(8,128)(2,1)S(1)}, u32[]{:S(2)}, u32[]{:S(2)}) collective-permute-start(s16[4,136,128]{2,1,0:T(8,128)(2,1)S(1)} %all_to_all.11.refs_5_), channel_id=1, source_target_pairs={{0,8},{8,16},{16,24},{24,0},{32,40},{40,48},{48,56},{56,32},{1,9},... | collective-permute-start | bytes 417800 | tf_op jit(solution)/shard_map/ppermute | solution.py:568
  106.0 6.0 %collective-permute-start.25 = (s16[4,136,128]{2,1,0:T(8,128)(2,1)S(1)}, s16[4,136,128]{2,1,0:T(8,128)(2,1)S(1)}, u32[]{:S(2)}, u32[]{:S(2)}) collective-permute-start(s16[4,136,128]{2,1,0:T(8,128)(2,1)S(1)} %all_to_all.11.refs_5_), channel_id=1, source_target_pairs={{0,4},{4,0},{1,5},{5,1},{2,6},{6,2},{3,7},{7,3},{8,12},{12,8},{9,1... | collective-permute-start | bytes 417800 | tf_op jit(solution)/shard_map/ppermute | solution.py:558
  112.0 0.8 collective-permute-start.11
  112.8 1.1 collective-permute-start.12
  113.9 3.3 %collective-permute-start.20 = (s16[4,136,128]{2,1,0:T(8,128)(2,1)S(1)}, s16[4,136,128]{2,1,0:T(8,128)(2,1)S(1)}, u32[]{:S(2)}, u32[]{:S(2)}) collective-permute-start(s16[4,136,128]{2,1,0:T(8,128)(2,1)S(1)} %collective-permute-done.15.refs_0_), channel_id=1, source_target_pairs={{0,4},{4,0},{1,5},{5,1},{2,6},{6,2},{3,7},{7,3},{8,12},{12,8},{9,1... | collective-permute-start | bytes 417800 | tf_op jit(solution)/shard_map/ppermute | solution.py:558
  117.3 0.4 collective-permute-start.22
  118.1 3.7 %collective-permute-start.23 = (s16[4,136,128]{2,1,0:T(8,128)(2,1)S(1)}, s16[4,136,128]{2,1,0:T(8,128)(2,1)S(1)}, u32[]{:S(2)}, u32[]{:S(2)}) collective-permute-start(s16[4,136,128]{2,1,0:T(8,128)(2,1)S(1)} %collective-permute-done.18.refs_3_), channel_id=1, source_target_pairs={{0,4},{4,0},{1,5},{5,1},{2,6},{6,2},{3,7},{7,3},{8,12},{12,8},{9,1... | collective-permute-start | bytes 417800 | tf_op jit(solution)/shard_map/ppermute | solution.py:558
  121.7 0.5 collective-permute-start.13
  122.4 0.9 fetch.1
  123.3 5.1 %update.2 = (f32[2,4096,128]{2,1,0:T(8,128)}, f32[2,4096]{1,0:T(2,128)}) custom-call(s32[16]{0:T(128)S(1)} %stack.53.targets.groups, s32[1]{0:T(128)} %bitcast.10.core, s16[4,136,128]{2,1,0:T(8,128)(2,1)S(1)} %collective-permute-done.15.refs_0_, s16[4,136,128]{2,1,0:T(8,128)(2,1)S(1)} %collective-permute-done.16.refs_1_, ...), custom_call_target="tpu_custom_call" | custom-call | flops 10000000 | bytes 1000000 | tf_op jit(solution)/shard_map/update/pallas_call | solution.py:484
  128.4 2.4 %update.3 = (f32[2,4096,128]{2,1,0:T(8,128)}, f32[2,4096]{1,0:T(2,128)}) custom-call(s32[16]{0:T(128)S(1)} %stack.53.targets.groups, s32[1]{0:T(128)} %bitcast.10.core, s16[4,136,128]{2,1,0:T(8,128)(2,1)S(1)} %collective-permute-done.11.refs_0_, ...), custom_call_target="tpu_custom_call", output_to_operand_aliasing={{0}: (8, {}), {1}: (9, {})} | custom-call | flops 10000000 | bytes 1000000 | tf_op jit(solution)/shard_map/update/pallas_call | solution.py:484
  (49 shorter events, 1.6 us)
Async XLA Ops:
  1.4 1.0 copy-start.10
  2.4 0.7 copy-start.11
  3.1 0.7 copy-start.13
  8.4 9.7 %collective-permute-start.1 = (bf16[1040,128]{1,0:T(8,128)(2,1)S(1)}, bf16[1040,128]{1,0:T(8,128)(2,1)S(1)}, u32[]{:S(2)}, u32[]{:S(2)}) collective-permute-start(bf16[1040,128]{1,0:T(8,128)(2,1)S(1)} %get-tuple-element.28), channel_id=1, source_target_pairs={{0,1},{1,2},{2,3},{3,0},{4,5},{5,6},{6,7},{7,4},{8,9},{9,10},{10,1... | collective-permute-start | bytes 798728 | tf_op jit(solution)/shard_map/ppermute | solution.py:558
  10.6 7.6 %collective-permute-start.2 = (bf16[1040,128]{1,0:T(8,128)(2,1)S(1)}, bf16[1040,128]{1,0:T(8,128)(2,1)S(1)}, u32[]{:S(2)}, u32[]{:S(2)}) collective-permute-start(bf16[1040,128]{1,0:T(8,128)(2,1)S(1)} %get-tuple-element.29), channel_id=1, source_target_pairs={{0,3},{1,0},{2,1},{3,2},{4,7},{5,4},{6,5},{7,6},{8,11},{9,8},{10,9... | collective-permute-start | bytes 798728 | tf_op jit(solution)/shard_map/ppermute | solution.py:558
  12.1 12.6 %collective-permute-start = (bf16[1040,128]{1,0:T(8,128)(2,1)S(1)}, bf16[1040,128]{1,0:T(8,128)(2,1)S(1)}, u32[]{:S(2)}, u32[]{:S(2)}) collective-permute-start(bf16[1040,128]{1,0:T(8,128)(2,1)S(1)} %get-tuple-element.27), channel_id=1, source_target_pairs={{0,2},{1,3},{2,0},{3,1},{4,6},{5,7},{6,4},{7,5},{8,10},{9,11},{10,... | collective-permute-start | bytes 798728 | tf_op jit(solution)/shard_map/ppermute | solution.py:558
  32.6 2.0 %copy-start = (f32[8192,128]{1,0:T(8,128)}, f32[8192,128]{1,0:T(8,128)S(1)}, u32[]{:S(2)}) copy-start(f32[8192,128]{1,0:T(8,128)S(1)} %own_rows.1.begun.after) | copy-start | bytes 12582916
  34.7 2.0 %copy-start.3 = (f32[8200,128]{1,0:T(8,128)}, f32[8200,128]{1,0:T(8,128)S(1)}, u32[]{:S(2)}) copy-start(f32[8200,128]{1,0:T(8,128)S(1)} %get-tuple-element.30.refs_0_) | copy-start | bytes 12595204
  36.6 2.0 %copy-start.5 = (f32[8200,128]{1,0:T(8,128)}, f32[8200,128]{1,0:T(8,128)S(1)}, u32[]{:S(2)}) copy-start(f32[8200,128]{1,0:T(8,128)S(1)} %get-tuple-element.31.refs_1_) | copy-start | bytes 12595204
  38.7 2.1 %copy-start.7 = (f32[8200,128]{1,0:T(8,128)}, f32[8200,128]{1,0:T(8,128)S(1)}, u32[]{:S(2)}) copy-start(f32[8200,128]{1,0:T(8,128)S(1)} %get-tuple-element.32.refs_2_) | copy-start | bytes 12595204
  40.7 12.1 %collective-permute-start.3 = (f32[4096,128]{1,0:T(8,128)}, f32[4096,128]{1,0:T(8,128)S(1)}, u32[]{:S(2)}, u32[]{:S(2)}) collective-permute-start(f32[4096,128]{1,0:T(8,128)} %get-tuple-element.33), channel_id=1, source_target_pairs={{0,4},{4,0},{1,5},{5,1},{2,6},{6,2},{3,7},{7,3},{8,12},{12,8},{9,1... | collective-permute-start | bytes 6291464 | tf_op jit(solution)/shard_map/ppermute | solution.py:558
  42.6 2.2 %copy-start.1 = (f32[8192,128]{1,0:T(8,128)S(1)}, f32[8192,128]{1,0:T(8,128)}, u32[]{:S(2)}) copy-start(f32[8192,128]{1,0:T(8,128)} %copy-done) | copy-start | bytes 12582916
  44.8 2.2 %copy-start.4 = (f32[8200,128]{1,0:T(8,128)S(1)}, f32[8200,128]{1,0:T(8,128)}, u32[]{:S(2)}) copy-start(f32[8200,128]{1,0:T(8,128)} %copy-done.3) | copy-start | bytes 12595204
  47.0 2.2 %copy-start.6 = (f32[8200,128]{1,0:T(8,128)S(1)}, f32[8200,128]{1,0:T(8,128)}, u32[]{:S(2)}) copy-start(f32[8200,128]{1,0:T(8,128)} %copy-done.5) | copy-start | bytes 12595204
  49.2 2.2 %copy-start.8 = (f32[8200,128]{1,0:T(8,128)S(1)}, f32[8200,128]{1,0:T(8,128)}, u32[]{:S(2)}) copy-start(f32[8200,128]{1,0:T(8,128)} %copy-done.7) | copy-start | bytes 12595204
  52.8 69.6 %copy-start.9 = (f32[2,4096,128]{2,1,0:T(8,128)S(1)}, f32[2,4096,128]{2,1,0:T(8,128)}, u32[]{:S(2)}) copy-start(f32[2,4096,128]{2,1,0:T(8,128)} %rows.1) | copy-start | bytes 12582916
  54.1 68.3 %copy-start.12 = (f32[2,4096]{1,0:T(2,128)S(1)}, f32[2,4096]{1,0:T(2,128)}, u32[]{:S(2)}) copy-start(f32[2,4096]{1,0:T(2,128)} %state.1) | copy-start | bytes 98308
  54.1 68.3 %copy-start.2 = (f32[8192,128]{1,0:T(8,128)S(1)}, f32[8192,128]{1,0:T(8,128)}, u32[]{:S(2)}) copy-start(f32[8192,128]{1,0:T(8,128)} %copy-done) | copy-start | bytes 12582916
  54.1 10.2 %collective-permute-start.10 = (s16[4,136,128]{2,1,0:T(8,128)(2,1)S(1)}, s16[4,136,128]{2,1,0:T(8,128)(2,1)S(1)}, u32[]{:S(2)}, u32[]{:S(2)}) collective-permute-start(s16[4,136,128]{2,1,0:T(8,128)(2,1)S(1)} %get-tuple-element.41), channel_id=1, source_target_pairs={{0,48},{8,56},{16,32},{24,40},{32,16},{40,24},{48,0},{56,8},{1,49}... | collective-permute-start | bytes 417800 | tf_op jit(solution)/shard_map/ppermute | solution.py:568
  57.9 7.8 %collective-permute-start.8 = (s16[4,136,128]{2,1,0:T(8,128)(2,1)S(1)}, s16[4,136,128]{2,1,0:T(8,128)(2,1)S(1)}, u32[]{:S(2)}, u32[]{:S(2)}) collective-permute-start(s16[4,136,128]{2,1,0:T(8,128)(2,1)S(1)} %get-tuple-element.39), channel_id=1, source_target_pairs={{0,56},{8,32},{16,40},{24,48},{32,24},{40,0},{48,8},{56,16},{1,57}... | collective-permute-start | bytes 417800 | tf_op jit(solution)/shard_map/ppermute | solution.py:568
  58.3 9.0 %collective-permute-start.9 = (s16[4,136,128]{2,1,0:T(8,128)(2,1)S(1)}, s16[4,136,128]{2,1,0:T(8,128)(2,1)S(1)}, u32[]{:S(2)}, u32[]{:S(2)}) collective-permute-start(s16[4,136,128]{2,1,0:T(8,128)(2,1)S(1)} %get-tuple-element.40), channel_id=1, source_target_pairs={{0,16},{8,24},{16,0},{24,8},{32,48},{40,56},{48,32},{56,40},{1,17}... | collective-permute-start | bytes 417800 | tf_op jit(solution)/shard_map/ppermute | solution.py:568
  61.6 5.7 %collective-permute-start.4 = (s16[4,136,128]{2,1,0:T(8,128)(2,1)S(1)}, s16[4,136,128]{2,1,0:T(8,128)(2,1)S(1)}, u32[]{:S(2)}, u32[]{:S(2)}) collective-permute-start(s16[4,136,128]{2,1,0:T(8,128)(2,1)S(1)} %get-tuple-element.35), channel_id=1, source_target_pairs={{0,8},{8,16},{16,24},{24,0},{32,40},{40,48},{48,56},{56,32},{1,9},... | collective-permute-start | bytes 417800 | tf_op jit(solution)/shard_map/ppermute | solution.py:568
  61.7 9.6 %collective-permute-start.5 = (s16[4,136,128]{2,1,0:T(8,128)(2,1)S(1)}, s16[4,136,128]{2,1,0:T(8,128)(2,1)S(1)}, u32[]{:S(2)}, u32[]{:S(2)}) collective-permute-start(s16[4,136,128]{2,1,0:T(8,128)(2,1)S(1)} %get-tuple-element.36), channel_id=1, source_target_pairs={{0,24},{8,0},{16,8},{24,16},{32,56},{40,32},{48,40},{56,48},{1,25}... | collective-permute-start | bytes 417800 | tf_op jit(solution)/shard_map/ppermute | solution.py:568
  64.3 7.0 %collective-permute-start.6 = (s16[4,136,128]{2,1,0:T(8,128)(2,1)S(1)}, s16[4,136,128]{2,1,0:T(8,128)(2,1)S(1)}, u32[]{:S(2)}, u32[]{:S(2)}) collective-permute-start(s16[4,136,128]{2,1,0:T(8,128)(2,1)S(1)} %get-tuple-element.37), channel_id=1, source_target_pairs={{0,32},{8,40},{16,48},{24,56},{32,0},{40,8},{48,16},{56,24},{1,33}... | collective-permute-start | bytes 417800 | tf_op jit(solution)/shard_map/ppermute | solution.py:568
  65.7 6.1 %collective-permute-start.7 = (s16[4,136,128]{2,1,0:T(8,128)(2,1)S(1)}, s16[4,136,128]{2,1,0:T(8,128)(2,1)S(1)}, u32[]{:S(2)}, u32[]{:S(2)}) collective-permute-start(s16[4,136,128]{2,1,0:T(8,128)(2,1)S(1)} %get-tuple-element.38), channel_id=1, source_target_pairs={{0,40},{8,48},{16,56},{24,32},{32,8},{40,16},{48,24},{56,0},{1,41}... | collective-permute-start | bytes 417800 | tf_op jit(solution)/shard_map/ppermute | solution.py:568
  98.4 7.6 %collective-permute-start.15 = (s16[4,136,128]{2,1,0:T(8,128)(2,1)S(1)}, s16[4,136,128]{2,1,0:T(8,128)(2,1)S(1)}, u32[]{:S(2)}, u32[]{:S(2)}) collective-permute-start(s16[4,136,128]{2,1,0:T(8,128)(2,1)S(1)} %all_to_all.11.refs_5_), channel_id=1, source_target_pairs={{0,48},{8,56},{16,32},{24,40},{32,16},{40,24},{48,0},{56,8},{1,49}... | collective-permute-start | bytes 417800 | tf_op jit(solution)/shard_map/ppermute | solution.py:568
  100.5 11.6 %collective-permute-start.16 = (s16[4,136,128]{2,1,0:T(8,128)(2,1)S(1)}, s16[4,136,128]{2,1,0:T(8,128)(2,1)S(1)}, u32[]{:S(2)}, u32[]{:S(2)}) collective-permute-start(s16[4,136,128]{2,1,0:T(8,128)(2,1)S(1)} %all_to_all.11.refs_5_), channel_id=1, source_target_pairs={{0,16},{8,24},{16,0},{24,8},{32,48},{40,56},{48,32},{56,40},{1,17}... | collective-permute-start | bytes 417800 | tf_op jit(solution)/shard_map/ppermute | solution.py:568
  102.2 10.6 %collective-permute-start.17 = (s16[4,136,128]{2,1,0:T(8,128)(2,1)S(1)}, s16[4,136,128]{2,1,0:T(8,128)(2,1)S(1)}, u32[]{:S(2)}, u32[]{:S(2)}) collective-permute-start(s16[4,136,128]{2,1,0:T(8,128)(2,1)S(1)} %all_to_all.11.refs_5_), channel_id=1, source_target_pairs={{0,56},{8,32},{16,40},{24,48},{32,24},{40,0},{48,8},{56,16},{1,57}... | collective-permute-start | bytes 417800 | tf_op jit(solution)/shard_map/ppermute | solution.py:568
  104.6 9.3 %collective-permute-start.18 = (s16[4,136,128]{2,1,0:T(8,128)(2,1)S(1)}, s16[4,136,128]{2,1,0:T(8,128)(2,1)S(1)}, u32[]{:S(2)}, u32[]{:S(2)}) collective-permute-start(s16[4,136,128]{2,1,0:T(8,128)(2,1)S(1)} %all_to_all.11.refs_5_), channel_id=1, source_target_pairs={{0,24},{8,0},{16,8},{24,16},{32,56},{40,32},{48,40},{56,48},{1,25}... | collective-permute-start | bytes 417800 | tf_op jit(solution)/shard_map/ppermute | solution.py:568
  104.6 12.6 %collective-permute-start.19 = (s16[4,136,128]{2,1,0:T(8,128)(2,1)S(1)}, s16[4,136,128]{2,1,0:T(8,128)(2,1)S(1)}, u32[]{:S(2)}, u32[]{:S(2)}) collective-permute-start(s16[4,136,128]{2,1,0:T(8,128)(2,1)S(1)} %all_to_all.11.refs_5_), channel_id=1, source_target_pairs={{0,8},{8,16},{16,24},{24,0},{32,40},{40,48},{48,56},{56,32},{1,9},... | collective-permute-start | bytes 417800 | tf_op jit(solution)/shard_map/ppermute | solution.py:568
  106.0 11.2 %collective-permute-start.25 = (s16[4,136,128]{2,1,0:T(8,128)(2,1)S(1)}, s16[4,136,128]{2,1,0:T(8,128)(2,1)S(1)}, u32[]{:S(2)}, u32[]{:S(2)}) collective-permute-start(s16[4,136,128]{2,1,0:T(8,128)(2,1)S(1)} %all_to_all.11.refs_5_), channel_id=1, source_target_pairs={{0,4},{4,0},{1,5},{5,1},{2,6},{6,2},{3,7},{7,3},{8,12},{12,8},{9,1... | collective-permute-start | bytes 417800 | tf_op jit(solution)/shard_map/ppermute | solution.py:558
  112.0 6.0 %collective-permute-start.11 = (s16[4,136,128]{2,1,0:T(8,128)(2,1)S(1)}, s16[4,136,128]{2,1,0:T(8,128)(2,1)S(1)}, u32[]{:S(2)}, u32[]{:S(2)}) collective-permute-start(s16[4,136,128]{2,1,0:T(8,128)(2,1)S(1)} %all_to_all.11.refs_5_), channel_id=1, source_target_pairs={{0,40},{8,48},{16,56},{24,32},{32,8},{40,16},{48,24},{56,0},{1,41}... | collective-permute-start | bytes 417800 | tf_op jit(solution)/shard_map/ppermute | solution.py:568
  112.8 8.9 %collective-permute-start.12 = (s16[4,136,128]{2,1,0:T(8,128)(2,1)S(1)}, s16[4,136,128]{2,1,0:T(8,128)(2,1)S(1)}, u32[]{:S(2)}, u32[]{:S(2)}) collective-permute-start(s16[4,136,128]{2,1,0:T(8,128)(2,1)S(1)} %all_to_all.11.refs_5_), channel_id=1, source_target_pairs={{0,32},{8,40},{16,48},{24,56},{32,0},{40,8},{48,16},{56,24},{1,33}... | collective-permute-start | bytes 417800 | tf_op jit(solution)/shard_map/ppermute | solution.py:568
  113.9 7.9 %collective-permute-start.20 = (s16[4,136,128]{2,1,0:T(8,128)(2,1)S(1)}, s16[4,136,128]{2,1,0:T(8,128)(2,1)S(1)}, u32[]{:S(2)}, u32[]{:S(2)}) collective-permute-start(s16[4,136,128]{2,1,0:T(8,128)(2,1)S(1)} %collective-permute-done.15.refs_0_), channel_id=1, source_target_pairs={{0,4},{4,0},{1,5},{5,1},{2,6},{6,2},{3,7},{7,3},{8,12},{12,8},{9,1... | collective-permute-start | bytes 417800 | tf_op jit(solution)/shard_map/ppermute | solution.py:558
  117.2 5.1 %collective-permute-start.21 = (s16[4,136,128]{2,1,0:T(8,128)(2,1)S(1)}, s16[4,136,128]{2,1,0:T(8,128)(2,1)S(1)}, u32[]{:S(2)}, u32[]{:S(2)}) collective-permute-start(s16[4,136,128]{2,1,0:T(8,128)(2,1)S(1)} %collective-permute-done.16.refs_1_), channel_id=1, source_target_pairs={{0,4},{4,0},{1,5},{5,1},{2,6},{6,2},{3,7},{7,3},{8,12},{12,8},{9,1... | collective-permute-start | bytes 417800 | tf_op jit(solution)/shard_map/ppermute | solution.py:558
  117.3 6.0 %collective-permute-start.22 = (s16[4,136,128]{2,1,0:T(8,128)(2,1)S(1)}, s16[4,136,128]{2,1,0:T(8,128)(2,1)S(1)}, u32[]{:S(2)}, u32[]{:S(2)}) collective-permute-start(s16[4,136,128]{2,1,0:T(8,128)(2,1)S(1)} %collective-permute-done.17.refs_2_), channel_id=1, source_target_pairs={{0,4},{4,0},{1,5},{5,1},{2,6},{6,2},{3,7},{7,3},{8,12},{12,8},{9,1... | collective-permute-start | bytes 417800 | tf_op jit(solution)/shard_map/ppermute | solution.py:558
  118.1 5.3 %collective-permute-start.23 = (s16[4,136,128]{2,1,0:T(8,128)(2,1)S(1)}, s16[4,136,128]{2,1,0:T(8,128)(2,1)S(1)}, u32[]{:S(2)}, u32[]{:S(2)}) collective-permute-start(s16[4,136,128]{2,1,0:T(8,128)(2,1)S(1)} %collective-permute-done.18.refs_3_), channel_id=1, source_target_pairs={{0,4},{4,0},{1,5},{5,1},{2,6},{6,2},{3,7},{7,3},{8,12},{12,8},{9,1... | collective-permute-start | bytes 417800 | tf_op jit(solution)/shard_map/ppermute | solution.py:558
  121.7 1.6 %collective-permute-start.24 = (s16[4,136,128]{2,1,0:T(8,128)(2,1)S(1)}, s16[4,136,128]{2,1,0:T(8,128)(2,1)S(1)}, u32[]{:S(2)}, u32[]{:S(2)}) collective-permute-start(s16[4,136,128]{2,1,0:T(8,128)(2,1)S(1)} %collective-permute-done.19.refs_4_), channel_id=1, source_target_pairs={{0,4},{4,0},{1,5},{5,1},{2,6},{6,2},{3,7},{7,3},{8,12},{12,8},{9,1... | collective-permute-start | bytes 417800 | tf_op jit(solution)/shard_map/ppermute | solution.py:558
  121.7 6.7 %collective-permute-start.13 = (s16[4,136,128]{2,1,0:T(8,128)(2,1)S(1)}, s16[4,136,128]{2,1,0:T(8,128)(2,1)S(1)}, u32[]{:S(2)}, u32[]{:S(2)}) collective-permute-start(s16[4,136,128]{2,1,0:T(8,128)(2,1)S(1)} %collective-permute-done.11.refs_0_), channel_id=1, source_target_pairs={{0,4},{4,0},{1,5},{5,1},{2,6},{6,2},{3,7},{7,3},{8,12},{12,8},{9,1... | collective-permute-start | bytes 417800 | tf_op jit(solution)/shard_map/ppermute | solution.py:558
  122.3 6.2 %collective-permute-start.14 = (s16[4,136,128]{2,1,0:T(8,128)(2,1)S(1)}, s16[4,136,128]{2,1,0:T(8,128)(2,1)S(1)}, u32[]{:S(2)}, u32[]{:S(2)}) collective-permute-start(s16[4,136,128]{2,1,0:T(8,128)(2,1)S(1)} %collective-permute-done.12.refs_1_), channel_id=1, source_target_pairs={{0,4},{4,0},{1,5},{5,1},{2,6},{6,2},{3,7},{7,3},{8,12},{12,8},{9,1... | collective-permute-start | bytes 417800 | tf_op jit(solution)/shard_map/ppermute | solution.py:558
